TPU v7x, 32 devices: a whole 2x2x4 slice. The times are simulated.
32 devices in a mesh: seq: 16 (over z, y, core), head: 2 (over x).
Axes of the slice: x: 2, y: 2, z: 4, core: 2. Of those that a mesh axis runs over, the one named last changes fastest.
Arguments:
- queries: bfloat16 [256, 64, 128], P('seq', 'head'), may hold values from -5 to 5
- cache: bfloat16 [2, 1024, 8, 128, 128], P(None, 'seq', 'head'), may hold values from -5 to 5
- page_table: int32 [256, 64], replicated, may hold values from 0 to 1023, as said below
- page_count: int32 [256], replicated, may hold values from 32 to 64, as said below
- out_weight: bfloat16 [8192, 8192], P('head', 'seq'), may hold values from -0.0625 to 0.0625
Outputs:
- output: bfloat16 [256, 8192], P('head', 'seq')
Inputs may be any that keep to these rules, and one draw needn't show every extreme that they name: `page_table`: within a row all 64 entries are distinct page ids; only the first page_count entries of a row are selected, the rest are arbitrary. In every row at most 4 entries lie in one aligned block of 64 page ids, and the first 4 entries of every row lie in one such block. `page_count`: some sequence has exactly 64 selected pages.
All inputs are finite; a program needn't handle non-finite values.
Results may differ from a plain program's by a relative error of at most 0.0095.
Values may be sent and summed in bfloat16 or wider, within the bound.
No kernel may reach another device: no remote copies, remote signals or barrier semaphores. Data moves between devices by JAX's collectives and lax.ppermute only.
A program may use at most 192 MiB of HBM per device.

v0:
```python
import math

import jax
import jax.numpy as jnp
from jax import lax
from jax.sharding import PartitionSpec as P

CAP = 4


def shards(queries, cache, page_table, page_count, out_weight):
    own_index = lax.axis_index("seq")
    key_pages = cache[0]
    value_pages = cache[1]
    pages_here = key_pages.shape[0]
    kv_local = key_pages.shape[1]
    query_heads = queries.shape[1]
    head_dim = queries.shape[2]
    group_size = query_heads // kv_local
    score_scale = 1.0 / math.sqrt(head_dim)

    def local_pages(selected, counts):
        slots = selected.shape[1]
        position = jnp.arange(slots, dtype=jnp.int32)
        usable = position[None, :] < counts[:, None]
        present = usable & (selected // pages_here == own_index)
        upper = (position[:, None] <= position[None, :]).astype(jnp.float32)
        ranks = jnp.dot(present.astype(jnp.float32), upper).astype(jnp.int32) - 1
        target = jnp.arange(CAP, dtype=jnp.int32)[None, :, None]
        onehot = present[:, None, :] & (ranks[:, None, :] == target)
        picked = jnp.sum(jnp.where(onehot, selected[:, None, :], 0), axis=2)
        valid = jnp.any(onehot, axis=2)
        index = jnp.where(valid, picked - own_index * pages_here, 0)
        return (index, valid)

    def block_scores(query_block, index, valid):
        block_rows = query_block.shape[0]
        grouped = query_block.reshape(block_rows, kv_local, group_size, head_dim)
        keys = key_pages[index]
        scores = (
            jnp.einsum("skgd,scktd->skgct", grouped, keys, preferred_element_type=jnp.float32)
            * score_scale
        )
        allowed = valid[:, None, None, :, None]
        return jnp.where(allowed, scores, jnp.float32(-1e30))

    def weigh_block(scores, index, valid, maxima):
        allowed = valid[:, None, None, :, None]
        weights = jnp.where(allowed, jnp.exp(scores - maxima[..., None, None]), jnp.float32(0.0))
        totals = jnp.sum(weights, axis=(3, 4))
        values = value_pages[index]
        update = jnp.einsum(
            "skgct,scktd->skgd",
            weights.astype(jnp.bfloat16),
            values,
            preferred_element_type=jnp.float32,
        )
        return (totals, update)

    all_queries = lax.all_gather(queries, "seq", axis=0, tiled=True)
    batch_rows = all_queries.shape[0]
    block_size = math.gcd(batch_rows, 64)
    blocks = batch_rows // block_size
    query_blocks = all_queries.reshape(blocks, block_size, query_heads, head_dim)
    table_blocks = page_table.reshape(blocks, block_size, page_table.shape[1])
    count_blocks = page_count.reshape(blocks, block_size)

    def score_many(inputs):
        query_block, selected, counts = inputs
        index, valid = local_pages(selected, counts)
        scores = block_scores(query_block, index, valid)
        return (scores, index, valid, jnp.max(scores, axis=(3, 4)))

    scores, index, valid, maxima = lax.map(score_many, (query_blocks, table_blocks, count_blocks))
    largest = lax.pmax(maxima, "seq")

    def weigh_many(inputs):
        block_scores_now, block_index, block_valid, block_largest = inputs
        return weigh_block(block_scores_now, block_index, block_valid, block_largest)

    totals, outputs = lax.map(weigh_many, (scores, index, valid, largest))
    totals = totals.reshape(batch_rows, kv_local, group_size)
    outputs = outputs.reshape(batch_rows, kv_local, group_size, head_dim)
    summed_outputs, summed_totals = lax.psum((outputs, totals), "seq")
    attention = (
        (summed_outputs / summed_totals[..., None])
        .reshape(batch_rows, query_heads * head_dim)
        .astype(jnp.bfloat16)
    )
    picked = attention
    summed = lax.psum_scatter(
        jnp.dot(picked, out_weight, preferred_element_type=jnp.float32),
        "head",
        scatter_dimension=0,
        tiled=True,
    )
    return summed.astype(jnp.bfloat16)


def solution(mesh):
    return jax.shard_map(
        shards,
        mesh=mesh,
        in_specs=(
            P("seq", "head", None),
            P(None, "seq", "head", None, None),
            P(),
            P(),
            P("head", "seq"),
        ),
        out_specs=P("head", "seq"),
        check_vma=False,
    )
```

profile of v0, /device:TPU:0, one launch (start us, length us, event | category | flops | bytes accessed | tf_op | source)
XLA Modules:
  0.0 540.8 jit_solution(4979630972835469058)
XLA Ops:
  9.1 11.9 %slice_bitcast_fusion = (bf16[64,4,128,128]{3,2,1,0:T(8,128)(2,1)}, bf16[64,4,128,128]{3,2,1,0:T(8,128)(2,1)}) fusion(bf16[2,64,4,128,128]{4,3,2,1,0:T(8,128)(2,1)} %param.10), kind=kLoop, calls=%fused_computation.56 | loop fusion | bytes 33554432 | tf_op jit(solution)/shard_map/squeeze | solution.py:14
  21.0 32.8 %all-gather.2.cloned.1.call-done = bf16[256,32,128]{2,1,0:T(8,128)(2,1)} async-done(((bf16[16,32,128]{2,1,0:T(8,128)(2,1)}), bf16[256,32,128]{2,1,0:T(8,128)(2,1)}) %all-gather.2.cloned.1.call-update) | async-done | bytes 2097168 | tf_op jit(solution)/shard_map/all_gather | solution.py:60
  53.8 142.4 %while.31 = (s32[]{:T(128)}, f32[4,64,4,8,4,128]{5,3,4,2,1,0:T(8,128)}, s32[4,64,4]{1,2,0:T(4,128)S(1)}, pred[4,64,4]{1,2,0:T(4,128)(4,1)S(1)}, f32[4,64,4,8]{3,...) while((s32[]{:T(128)}, ...), condition=%wide.region_4.5_spmd, body=%wide.region_0.4_spmd.sunk | while | flops 274403584 | bytes 114177944 | solution.py:74
  54.6 17.1 %gather_fusion.1 = bf16[256,4,128,128]{3,2,1,0:T(8,128)(2,1)} fusion(bf16[64,4,128,128]{3,2,1,0:T(8,128)(2,1)} %get-tuple-element.437, s32[1024]{0:T(1024)S(1)} %pad_clamp_fusion.4), kind=kCustom, calls=%fused_computation.clone.1 | custom fusion | bytes 67109888 | tf_op jit(solution)/shard_map/while/body/eval_jaxpr/gather | solution.py:39
  71.8 16.0 %bitcast_dynamic-update-slice_fusion.8 = (f32[4,64,4,8,4,128]{5,3,4,2,1,0:T(8,128)}, f32[64,4,8,4,128]{4,2,3,1,0:T(8,128)S(1)}) fusion(f32[4,64,4,8,4,128]{5,3,4,2,1,0:T(8,128)} %get-tuple-element.416, s32[]{:T(128)} %get-tuple-element.415, pred[64,4]{1,0:T(8,128)(4,1)S(1)} %copy.58, bf16[64,4,4,128,128]{4,3,2,1,0:T(8,128)(2,1)} %bitcast.114, ...), kind=kOutput, calls=%fused_computation.4.clone.1 | convolution fusion | flops 270532608 | bytes 42468608 | tf_op jit(solution)/shard_map/while/body/eval_jaxpr/skgd,scktd->skgct/dot_general | solution.py:41
  90.2 17.1 %gather_fusion.1 = bf16[256,4,128,128]{3,2,1,0:T(8,128)(2,1)} fusion(bf16[64,4,128,128]{3,2,1,0:T(8,128)(2,1)} %get-tuple-element.437, s32[1024]{0:T(1024)S(1)} %pad_clamp_fusion.4), kind=kCustom, calls=%fused_computation.clone.1 | custom fusion | bytes 67109888 | tf_op jit(solution)/shard_map/while/body/eval_jaxpr/gather | solution.py:39
  107.5 16.0 %bitcast_dynamic-update-slice_fusion.8 = (f32[4,64,4,8,4,128]{5,3,4,2,1,0:T(8,128)}, f32[64,4,8,4,128]{4,2,3,1,0:T(8,128)S(1)}) fusion(f32[4,64,4,8,4,128]{5,3,4,2,1,0:T(8,128)} %get-tuple-element.416, s32[]{:T(128)} %get-tuple-element.415, pred[64,4]{1,0:T(8,128)(4,1)S(1)} %copy.58, bf16[64,4,4,128,128]{4,3,2,1,0:T(8,128)(2,1)} %bitcast.114, ...), kind=kOutput, calls=%fused_computation.4.clone.1 | convolution fusion | flops 270532608 | bytes 42468608 | tf_op jit(solution)/shard_map/while/body/eval_jaxpr/skgd,scktd->skgct/dot_general | solution.py:41
  125.9 17.1 %gather_fusion.1 = bf16[256,4,128,128]{3,2,1,0:T(8,128)(2,1)} fusion(bf16[64,4,128,128]{3,2,1,0:T(8,128)(2,1)} %get-tuple-element.437, s32[1024]{0:T(1024)S(1)} %pad_clamp_fusion.4), kind=kCustom, calls=%fused_computation.clone.1 | custom fusion | bytes 67109888 | tf_op jit(solution)/shard_map/while/body/eval_jaxpr/gather | solution.py:39
  143.1 15.9 %bitcast_dynamic-update-slice_fusion.8 = (f32[4,64,4,8,4,128]{5,3,4,2,1,0:T(8,128)}, f32[64,4,8,4,128]{4,2,3,1,0:T(8,128)S(1)}) fusion(f32[4,64,4,8,4,128]{5,3,4,2,1,0:T(8,128)} %get-tuple-element.416, s32[]{:T(128)} %get-tuple-element.415, pred[64,4]{1,0:T(8,128)(4,1)S(1)} %copy.58, bf16[64,4,4,128,128]{4,3,2,1,0:T(8,128)(2,1)} %bitcast.114, ...), kind=kOutput, calls=%fused_computation.4.clone.1 | convolution fusion | flops 270532608 | bytes 42468608 | tf_op jit(solution)/shard_map/while/body/eval_jaxpr/skgd,scktd->skgct/dot_general | solution.py:41
  161.5 17.0 %gather_fusion.1 = bf16[256,4,128,128]{3,2,1,0:T(8,128)(2,1)} fusion(bf16[64,4,128,128]{3,2,1,0:T(8,128)(2,1)} %get-tuple-element.437, s32[1024]{0:T(1024)S(1)} %pad_clamp_fusion.4), kind=kCustom, calls=%fused_computation.clone.1 | custom fusion | bytes 67109888 | tf_op jit(solution)/shard_map/while/body/eval_jaxpr/gather | solution.py:39
  178.6 16.0 %bitcast_dynamic-update-slice_fusion.8 = (f32[4,64,4,8,4,128]{5,3,4,2,1,0:T(8,128)}, f32[64,4,8,4,128]{4,2,3,1,0:T(8,128)S(1)}) fusion(f32[4,64,4,8,4,128]{5,3,4,2,1,0:T(8,128)} %get-tuple-element.416, s32[]{:T(128)} %get-tuple-element.415, pred[64,4]{1,0:T(8,128)(4,1)S(1)} %copy.58, bf16[64,4,4,128,128]{4,3,2,1,0:T(8,128)(2,1)} %bitcast.114, ...), kind=kOutput, calls=%fused_computation.4.clone.1 | convolution fusion | flops 270532608 | bytes 42468608 | tf_op jit(solution)/shard_map/while/body/eval_jaxpr/skgd,scktd->skgct/dot_general | solution.py:41
  196.2 64.8 %pmax.7 = f32[4,64,4,8]{3,2,1,0:T(4,128)S(1)} all-reduce(f32[4,64,4,8]{3,2,1,0:T(4,128)S(1)} %get-tuple-element.215), channel_id=1, replica_groups=mesh['seq'=16,'head'=2] {'seq'}, use_global_device_ids=true, to_apply=%region_5.6 | all-reduce | flops 8192 | bytes 65536 | tf_op jit(solution)/shard_map/pmax | solution.py:75
  261.1 143.1 %while.32 = (s32[]{:T(128)}, f32[4,64,4,8]{3,2,1,0:T(4,128)S(1)}, f32[4,64,4,8,128]{4,3,2,1,0:T(8,128)}, pred[4,64,4]{1,2,0:T(4,128)(4,1)S(1)}, f32[4,64,4,8,4,1...) while((s32[]{:T(128)}, f32[4,64,4,8]{3,2,1,0:T(4,128)S(1)}, ...), condition=%wide.region_8.9_spmd, body=%wide.region_6.8_spmd.sunk | while | flops 274726656 | bytes 110420592 | solution.py:81
  261.3 17.1 %gather_fusion = bf16[256,4,128,128]{3,2,1,0:T(8,128)(2,1)} fusion(bf16[64,4,128,128]{3,2,1,0:T(8,128)(2,1)} %get-tuple-element.464, s32[1024]{0:T(1024)S(1)} %pad_clamp_fusion.5), kind=kCustom, calls=%fused_computation.1.clone.1 | custom fusion | bytes 67109888 | tf_op jit(solution)/shard_map/while/body/eval_jaxpr/gather | solution.py:51
  278.6 15.2 %fusion.63 = f32[4,64,4,8,128]{4,3,2,1,0:T(8,128)} fusion(f32[4,64,4,8,128]{4,3,2,1,0:T(8,128)} %get-tuple-element.450, s32[]{:T(128)} %get-tuple-element.448, bf16[64,4,4,128,128]{4,3,2,1,0:T(8,128)(2,1)} %bitcast.115, f32[4,64,4,8,4,128]{5,3,4,2,1,0:T(8,128)} %get-tuple-element.461, f32[64,4,8]{2,1,0:T(4,128)S(1)} %dynamic-slice_bitcast_fusion.4, ...), kind=kOutput, calls=%fused_computation.47.clone.1 | convolution fusion | flops 271581184 | bytes 38806784 | tf_op jit(solution)/shard_map/while/body/eval_jaxpr/skgct,scktd->skgd/dot_general | solution.py:52
  297.1 17.1 %gather_fusion = bf16[256,4,128,128]{3,2,1,0:T(8,128)(2,1)} fusion(bf16[64,4,128,128]{3,2,1,0:T(8,128)(2,1)} %get-tuple-element.464, s32[1024]{0:T(1024)S(1)} %pad_clamp_fusion.5), kind=kCustom, calls=%fused_computation.1.clone.1 | custom fusion | bytes 67109888 | tf_op jit(solution)/shard_map/while/body/eval_jaxpr/gather | solution.py:51
  314.4 15.2 %fusion.63 = f32[4,64,4,8,128]{4,3,2,1,0:T(8,128)} fusion(f32[4,64,4,8,128]{4,3,2,1,0:T(8,128)} %get-tuple-element.450, s32[]{:T(128)} %get-tuple-element.448, bf16[64,4,4,128,128]{4,3,2,1,0:T(8,128)(2,1)} %bitcast.115, f32[4,64,4,8,4,128]{5,3,4,2,1,0:T(8,128)} %get-tuple-element.461, f32[64,4,8]{2,1,0:T(4,128)S(1)} %dynamic-slice_bitcast_fusion.4, ...), kind=kOutput, calls=%fused_computation.47.clone.1 | convolution fusion | flops 271581184 | bytes 38806784 | tf_op jit(solution)/shard_map/while/body/eval_jaxpr/skgct,scktd->skgd/dot_general | solution.py:52
  332.9 17.1 %gather_fusion = bf16[256,4,128,128]{3,2,1,0:T(8,128)(2,1)} fusion(bf16[64,4,128,128]{3,2,1,0:T(8,128)(2,1)} %get-tuple-element.464, s32[1024]{0:T(1024)S(1)} %pad_clamp_fusion.5), kind=kCustom, calls=%fused_computation.1.clone.1 | custom fusion | bytes 67109888 | tf_op jit(solution)/shard_map/while/body/eval_jaxpr/gather | solution.py:51
  350.2 15.2 %fusion.63 = f32[4,64,4,8,128]{4,3,2,1,0:T(8,128)} fusion(f32[4,64,4,8,128]{4,3,2,1,0:T(8,128)} %get-tuple-element.450, s32[]{:T(128)} %get-tuple-element.448, bf16[64,4,4,128,128]{4,3,2,1,0:T(8,128)(2,1)} %bitcast.115, f32[4,64,4,8,4,128]{5,3,4,2,1,0:T(8,128)} %get-tuple-element.461, f32[64,4,8]{2,1,0:T(4,128)S(1)} %dynamic-slice_bitcast_fusion.4, ...), kind=kOutput, calls=%fused_computation.47.clone.1 | convolution fusion | flops 271581184 | bytes 38806784 | tf_op jit(solution)/shard_map/while/body/eval_jaxpr/skgct,scktd->skgd/dot_general | solution.py:52
  368.8 17.0 %gather_fusion = bf16[256,4,128,128]{3,2,1,0:T(8,128)(2,1)} fusion(bf16[64,4,128,128]{3,2,1,0:T(8,128)(2,1)} %get-tuple-element.464, s32[1024]{0:T(1024)S(1)} %pad_clamp_fusion.5), kind=kCustom, calls=%fused_computation.1.clone.1 | custom fusion | bytes 67109888 | tf_op jit(solution)/shard_map/while/body/eval_jaxpr/gather | solution.py:51
  386.0 15.2 %fusion.63 = f32[4,64,4,8,128]{4,3,2,1,0:T(8,128)} fusion(f32[4,64,4,8,128]{4,3,2,1,0:T(8,128)} %get-tuple-element.450, s32[]{:T(128)} %get-tuple-element.448, bf16[64,4,4,128,128]{4,3,2,1,0:T(8,128)(2,1)} %bitcast.115, f32[4,64,4,8,4,128]{5,3,4,2,1,0:T(8,128)} %get-tuple-element.461, f32[64,4,8]{2,1,0:T(4,128)S(1)} %dynamic-slice_bitcast_fusion.4, ...), kind=kOutput, calls=%fused_computation.47.clone.1 | convolution fusion | flops 271581184 | bytes 38806784 | tf_op jit(solution)/shard_map/while/body/eval_jaxpr/skgct,scktd->skgd/dot_general | solution.py:52
  404.5 58.7 %psum.15 = f32[256,4,8]{0,2,1:T(8,128)S(1)} all-reduce(f32[256,4,8]{0,2,1:T(8,128)S(1)} %copy.33), channel_id=1, replica_groups=mesh['seq'=16,'head'=2] {'seq'}, use_global_device_ids=true, to_apply=%region_10.11 | all-reduce | flops 8192 | bytes 65536 | tf_op jit(solution)/shard_map/psum | solution.py:84
  463.4 49.8 %all-reduce.2.cloned.1.call-done = f32[256,4,8,128]{3,2,1,0:T(8,128)} async-done(((f32[256,4,8,128]{3,2,1,0:T(8,128)}), f32[256,4,8,128]{3,2,1,0:T(8,128)}) %all-reduce.2.cloned.1.call-update) | async-done | bytes 4194320 | tf_op jit(solution)/shard_map/psum | solution.py:84
  518.8 13.9 %reduce-scatter.2.cloned.1.call-done = f32[128,512]{1,0:T(8,128)} async-done(((f32[256,512]{1,0:T(8,128)}), f32[128,512]{1,0:T(8,128)}) %reduce-scatter.2.cloned.1.call-update) | async-done | bytes 262160 | tf_op jit(solution)/shard_map/reduce_scatter | solution.py:91
  (117 shorter events, 33.8 us)
Async XLA Ops:
  6.5 47.2 %all-gather.2.cloned.1.call-start = ((), (), s32[]{:S(2)}) async-start(), calls=%async_computation.1 | async-start | bytes 2228224 | tf_op jit(solution)/shard_map/all_gather | solution.py:60
  7.3 506.0 %all-reduce.2.cloned.1.call-start = ((), (), s32[]{:S(2)}) async-start(), calls=%async_computation.2 | async-start | bytes 8388608 | tf_op jit(solution)/shard_map/psum | solution.py:84
  404.2 128.4 %reduce-scatter.2.cloned.1.call-start = ((), (), s32[]{:S(2)}) async-start(), calls=%async_computation.3 | async-start | bytes 786432 | tf_op jit(solution)/shard_map/reduce_scatter | solution.py:91
  513.3 3.4 copy-start
Sparse Core Ops, SparseCore 0:
  9.5 44.1 all-gather.1
  404.4 108.8 all-reduce.1
  518.9 13.7 reduce-scatter.1
where the time goes:
time: 541 us
  local copies, waits for them, and re-layouts  154 us (28%)
  matrix products  127 us (23%)
  blocking collectives  123 us (23%)
  waiting for transfers between devices  97.2 us (18%)
  other arithmetic  24.8 us (5%)
  between operations  13.2 us (2%)
    gather x4, local copies, waits for them, and re-layouts, weigh_block(): values = value_pages[index]  68.4 us
    gather x4, local copies, waits for them, and re-layouts, block_scores(): keys = key_pages[index]  68.4 us
    pmax x1, blocking collectives, shards(): largest = lax.pmax(maxima, 'seq')  64.8 us
    dot_general x4, matrix products, block_scores(): jnp.einsum('skgd,scktd->skgct', grouped, keys, preferred_element_type=jnp...  63.9 us
    dot_general x4, matrix products, weigh_block(): jnp.einsum('skgct,scktd->skgd', weights.astype(jnp.bfloat16), values, pre...  60.8 us
    psum x1, blocking collectives, shards(): summed_outputs, summed_totals = lax.psum((outputs, totals), 'seq')  58.7 us
    psum x1, waiting for transfers between devices, shards(): summed_outputs, summed_totals = lax.psum((outputs, totals), 'seq')  49.8 us
    all_gather x1, waiting for transfers between devices, shards(): all_queries = lax.all_gather(queries, 'seq', axis=0, tiled=True)  32.8 us
  transfers between devices with their start and end apart: 3, of which 3 were waited for; matrix products, arithmetic and copies ran while one was open for 3% of the time, Pallas kernels for 0%

commit v1 on v0

v1 whole, which is shorter than its diff:
```python
import functools
import math

import jax
import jax.numpy as jnp
from jax import lax
from jax.experimental import pallas as pl
from jax.experimental.pallas import tpu as pltpu
from jax.sharding import PartitionSpec as P

CAP = 4
TILE = 16
LEAD = 2
NONE = -1e30
PLANES = 3
LANES = 128


def call(body, out_shape, in_specs, out_specs, flops, moved, **kw):
    return pl.pallas_call(
        body,
        out_shape=out_shape,
        in_specs=in_specs,
        out_specs=out_specs,
        cost_estimate=pl.CostEstimate(flops=flops, bytes_accessed=moved, transcendentals=0),
        **kw,
    )


SMEM = pl.BlockSpec(memory_space=pltpu.SMEM)
VMEM = pl.BlockSpec(memory_space=pltpu.VMEM)
ANY = pl.BlockSpec(memory_space=pl.ANY)


def list_kernel(pages, pairs, idx_ref, lst_ref, gp_ref, ng_ref, cnt, base):
    @pl.loop(0, pages + 1)
    def _(p):
        cnt[p] = 0

    slots = lst_ref.shape[0]

    @pl.loop(0, slots // 8)
    def _(i):
        for u in range(8):
            lst_ref[i * 8 + u] = pairs

    @pl.loop(0, gp_ref.shape[0])
    def _(i):
        gp_ref[i] = 0

    @pl.loop(0, pairs // 4)
    def _(i):
        for u in range(4):
            p = idx_ref[i * 4 + u]
            cnt[p] = cnt[p] + 1

    def place(p, g):
        base[p] = g * TILE
        n = (cnt[p] + (TILE - 1)) // TILE

        def mark(i, c):
            gp_ref[g + i] = p
            return c

        lax.fori_loop(0, n, mark, 0)
        return g + n

    end = lax.fori_loop(0, pages, place, LEAD)
    ng_ref[0] = end - LEAD
    base[pages] = slots - 1

    @pl.loop(0, pairs // 4)
    def _(i):
        for u in range(4):
            t = i * 4 + u
            p = idx_ref[t]
            d = base[p]
            real = p < pages
            lst_ref[d] = jnp.where(real, t, pairs)
            base[p] = jnp.where(real, d + 1, d)


def split3(x):
    parts = []
    for _ in range(PLANES):
        part = x.astype(jnp.bfloat16)
        parts.append(part)
        x = x - part.astype(jnp.float32)
    return jnp.concatenate(parts, axis=0)


def join3(block, heads):
    x = block.astype(jnp.float32)
    return (x[:heads] + x[heads : 2 * heads]) + x[2 * heads :]


def attention_kernel(nq, kv, group, scale, lst, gp, ng, valid, *refs):
    q_refs = refs[:nq]
    cache = refs[nq]
    outs = refs[nq + 1 : 2 * nq + 1]
    rest = refs[2 * nq + 1 :]
    kbuf, vbuf, ksem, vsem = rest[:4]
    rest = rest[4:]
    q32, osc, lsc, ssc, psc = (rest[i * kv : (i + 1) * kv] for i in range(5))
    per = q_refs[0].shape[0]
    heads = kv * group
    kcopy = pltpu.make_async_copy(cache.at[0], kbuf, ksem)
    vcopy = pltpu.make_async_copy(cache.at[1], vbuf, vsem)
    kcopy.start()
    vcopy.start()
    for a in range(nq):

        @pl.loop(0, per)
        def _(s):
            row = q_refs[a][s].astype(jnp.float32)
            for k in range(kv):
                q32[k][a * per + s] = row[k * group : (k + 1) * group]

    kcopy.wait()
    vcopy.wait()

    @pl.loop(0, ng[0] + LEAD)
    def _(i):
        t3 = [lst[i * TILE + u] for u in range(TILE)]
        t2 = [lst[(i + 1) * TILE + u] for u in range(TILE)]
        t1 = [lst[(i + 2) * TILE + u] // CAP for u in range(TILE)]
        p3 = gp[i]
        p1 = gp[i + 2]
        for k in range(kv):
            o = jnp.dot(psc[k][...], vbuf[p3, k], preferred_element_type=jnp.float32)
            for u in range(TILE):
                osc[k][t3[u]] = o[u * group : (u + 1) * group]
        for k in range(kv):
            s = ssc[k][...]
            m = jnp.max(s, axis=1, keepdims=True)
            w = jnp.exp2(s - m)
            total = jnp.sum(w, axis=1, keepdims=True)
            psc[k][...] = (w * (1.0 / total)).astype(jnp.bfloat16)
            lse = jnp.broadcast_to(m + jnp.log2(total), s.shape)
            for u in range(TILE):
                lsc[k][t2[u]] = lse[u * group : (u + 1) * group]
        for k in range(kv):
            rows = jnp.concatenate([q32[k][t1[u]] for u in range(TILE)], axis=0)
            s = lax.dot_general(
                rows.astype(jnp.bfloat16),
                kbuf[p1, k],
                (((1,), (1,)), ((), ())),
                preferred_element_type=jnp.float32,
            )
            ssc[k][...] = s * scale

    lane = lax.broadcasted_iota(jnp.int32, (heads, LANES), 1)
    for a in range(nq):

        def finish(s, stats):
            b = a * per + s
            n = valid[b]
            os, ls = [], []
            for k in range(kv):
                l = [jnp.where(n > r, lsc[k][b * CAP + r], NONE) for r in range(CAP)]
                o = [jnp.where(n > r, osc[k][b * CAP + r], 0.0) for r in range(CAP)]
                top = functools.reduce(jnp.maximum, l)
                w = [jnp.exp2(x - top) for x in l]
                total = sum(w[1:], w[0])
                acc = w[0] * o[0]
                for r in range(1, CAP):
                    acc = acc + w[r] * o[r]
                os.append(acc * (1.0 / total))
                ls.append(top + jnp.log2(total))
            outs[a][pl.ds(pl.multiple_of(s * heads, heads), heads), :] = jnp.concatenate(os, axis=0).astype(jnp.bfloat16)
            return jnp.where(lane == s, jnp.concatenate(ls, axis=0), stats)

        stats = lax.fori_loop(0, per, finish, jnp.full((heads, LANES), NONE, jnp.float32))
        outs[a][per * heads :, :] = split3(stats)


def merge_kernel(per, heads, keep, recv, *outs):
    rows = per * heads
    la = join3(keep[rows:, :], heads)
    lb = join3(recv[rows:, :], heads)
    diff = la - lb
    weight = 1.0 / (1.0 + jnp.exp2(-diff))
    each = per // len(outs)
    for s in range(per):
        sl = slice(s * heads, (s + 1) * heads)
        x = keep[sl, :].astype(jnp.float32)
        y = recv[sl, :].astype(jnp.float32)
        z = y + weight[:, s : s + 1] * (x - y)
        at = s % each
        outs[s // each][at * heads : (at + 1) * heads, :] = z.astype(jnp.bfloat16)
    if len(outs) > 1:
        stats = jnp.maximum(la, lb) + jnp.log2(1.0 + jnp.exp2(-jnp.abs(diff)))
        for i, out in enumerate(outs):
            part = stats if i == 0 else jnp.concatenate([stats[:, i * each :], stats[:, : i * each]], axis=1)
            out[each * heads :, :] = split3(part)


def merge(keep, recv, per, heads, last):
    if last:
        shapes = [jax.ShapeDtypeStruct((per * heads, LANES), jnp.bfloat16)]
    else:
        shapes = [jax.ShapeDtypeStruct(((per // 2 + PLANES) * heads, LANES), jnp.bfloat16)] * 2
    return call(
        functools.partial(merge_kernel, per, heads),
        shapes,
        [VMEM] * 2,
        [VMEM] * len(shapes),
        keep.size * 8,
        keep.size * 6,
        name="merge",
        compiler_params=pltpu.CompilerParams(vmem_limit_bytes=8 * 2**20),
    )(keep, recv)


def shards(n, nh, queries, cache, page_table, page_count, out_weight):
    me = lax.axis_index("seq")
    my_head = lax.axis_index("head")
    _, pages, kv, page_len, head_dim = cache.shape
    local, heads, _ = queries.shape
    group = heads // kv
    batch, slots = page_table.shape
    bits = [1 << i for i in range(n.bit_length() - 1)]
    outer = bits[1:]
    halves = 2
    half = local // halves
    orders = [outer, outer[1::-1] + outer[2:]]

    def swap(x, bit):
        return lax.ppermute(x, "seq", [(i, i ^ bit) for i in range(n)])

    per = half * n // 2
    rel = []
    for a in range(halves):
        for c in range(2):
            for s in range(n // 2):
                j = c * bits[0]
                for at, bit in enumerate(orders[a]):
                    if (s >> (len(outer) - 1 - at)) & 1:
                        j |= bit
                rel.append((j, a))
    rel_j = jnp.array([j for j, _ in rel], jnp.int32)
    rel_a = jnp.array([a for _, a in rel], jnp.int32)
    true_block = (rel_j ^ me) * halves + rel_a

    table = page_table.reshape(-1, half, slots)[true_block].reshape(batch, slots)
    counts = page_count.reshape(-1, half)[true_block].reshape(batch)
    position = jnp.arange(slots, dtype=jnp.int32)
    present = (position[None, :] < counts[:, None]) & (table // pages == me)
    upper = (position[:, None] <= position[None, :]).astype(jnp.float32)
    ranks = jnp.dot(present.astype(jnp.float32), upper).astype(jnp.int32) - 1
    onehot = present[:, None, :] & (ranks[:, None, :] == jnp.arange(CAP, dtype=jnp.int32)[None, :, None])
    valid = jnp.sum(present.astype(jnp.int32), axis=1)
    index = jnp.sum(jnp.where(onehot, table[:, None, :] - me * pages, 0), axis=2)
    index = jnp.where(jnp.arange(CAP)[None, :] < valid[:, None], index, pages).reshape(-1)

    pairs = batch * CAP
    most = pages + pairs // TILE + 2 * LEAD
    lst, gp, ng = call(
        functools.partial(list_kernel, pages, pairs),
        [jax.ShapeDtypeStruct((s,), jnp.int32) for s in (most * TILE, most, 1)],
        [SMEM],
        [SMEM] * 3,
        10**9,
        10**6,
        scratch_shapes=[pltpu.SMEM((pages + 1,), jnp.int32)] * 2,
        name="lists",
        compiler_params=pltpu.CompilerParams(vmem_limit_bytes=2**20),
    )(index)

    got = [queries[a * half : (a + 1) * half] for a in range(halves)]
    for at in reversed(range(len(outer))):
        new = [swap(x, orders[a][at]) for a, x in enumerate(got)]
        got = [jnp.concatenate([x, y], axis=0) for x, y in zip(got, new)]
    q_parts = []
    for x in got:
        q_parts += [x, swap(x, bits[0])]

    nq = 2 * halves
    tile = (pairs + 1, group, head_dim)
    scratch = [pltpu.VMEM(cache.shape[1:], cache.dtype)] * 2 + [pltpu.SemaphoreType.DMA] * 2
    scratch += [pltpu.VMEM((batch + 1, group, head_dim), jnp.float32)] * kv
    scratch += [pltpu.VMEM(tile, jnp.float32)] * (2 * kv)
    scratch += [pltpu.VMEM((TILE * group, page_len), jnp.float32)] * kv
    scratch += [pltpu.VMEM((TILE * group, page_len), jnp.bfloat16)] * kv
    parts = call(
        functools.partial(attention_kernel, nq, kv, group, math.log2(math.e) / math.sqrt(head_dim)),
        [jax.ShapeDtypeStruct(((per + PLANES) * heads, LANES), jnp.bfloat16)] * nq,
        [SMEM] * 4 + [VMEM] * nq + [ANY],
        [VMEM] * nq,
        4 * pairs * heads * page_len * head_dim,
        cache.size * 2,
        scratch_shapes=scratch,
        name="attention",
        compiler_params=pltpu.CompilerParams(vmem_limit_bytes=63 * 2**20),
    )(lst, gp, ng, valid, *q_parts, cache)

    keep = [parts[2 * a] for a in range(halves)]
    send = [parts[2 * a + 1] for a in range(halves)]
    now = per
    att = [None] * halves
    for at in range(len(bits)):
        took = [swap(send[a], ([bits[0]] + orders[a])[at]) for a in range(halves)]
        for a in range(halves):
            last = at == len(bits) - 1
            res = merge(keep[a], took[a], now, heads, last)
            if last:
                att[a] = res[0].reshape(half, heads * head_dim)
            else:
                keep[a], send[a] = res
        now //= 2

    for at in reversed(range(len(outer))):
        new = [swap(x, orders[a][at]) for a, x in enumerate(att)]
        att = [jnp.concatenate([x, y], axis=0) for x, y in zip(att, new)]
    rows = []
    for x in att:
        rows += [x, swap(x, bits[0])]
    product = jnp.dot(jnp.concatenate(rows, axis=0), out_weight, preferred_element_type=jnp.float32)

    width = product.shape[1]
    place = {ja: i for i, ja in enumerate(rel)}
    inverse = jnp.array([place[(j, a)] for j in range(n) for a in range(halves)], jnp.int32).reshape(n, halves)
    source = inverse[jnp.arange(n, dtype=jnp.int32) ^ me].reshape(nh, -1)
    blocks = product.reshape(n * halves, half, width)
    out = blocks[source[my_head]].reshape(batch // nh, width)
    for step in range(1, nh):
        give = blocks[source[my_head ^ step]].astype(jnp.bfloat16).reshape(batch // nh, width)
        took = lax.ppermute(give, "head", [(i, i ^ step) for i in range(nh)])
        out = out + took.astype(jnp.float32)
    return out.astype(jnp.bfloat16)


def solution(mesh):
    n, nh = mesh.shape["seq"], mesh.shape["head"]
    return jax.shard_map(
        functools.partial(shards, n, nh),
        mesh=mesh,
        in_specs=(
            P("seq", "head", None),
            P(None, "seq", "head", None, None),
            P(),
            P(),
            P("head", "seq"),
        ),
        out_specs=P("head", "seq"),
        check_vma=False,
    )
```

time: 541 us -> 147 us (0.27)
  local copies, waits for them, and re-layouts: 154 us -> 11.3 us
  matrix products: 127 us -> 1.49 us
  blocking collectives: 123 us -> 0 us
  Pallas kernels: 0 us -> 59.9 us
  waiting for transfers between devices: 97.2 us -> 45 us
  starting transfers between devices: 0.08 us -> 26 us
  other arithmetic: 24.8 us -> 2.55 us
  between operations: 13.2 us -> 0.44 us
    gather x8 -> x5, local copies, waits for them, and re-layouts: 137 us -> 2.86 us  [the longest x1 0.58 us: shards(): page_table.reshape(-1, half, slots)[true_block].reshape(batch, slots)]
    dot_general x13 -> x2, matrix products: 127 us -> 1.49 us  [the longest x1 1.29 us: shards(): jnp.dot(jnp.concatenate(rows, axis=0), out_weight, preferred_element_type...]
    pmax x1 -> x0, blocking collectives: 64.8 us -> none  [shards(): largest = lax.pmax(maxima, 'seq')]
    pallas_call x0 -> x10, Pallas kernels: none -> 59.9 us  [the longest x1 40.1 us: shards(): call(functools.partial(attention_kernel, nq, kv, group, math.log2(math.e)...]
    psum x1 -> x0, blocking collectives: 58.7 us -> none  [shards(): summed_outputs, summed_totals = lax.psum((outputs, totals), 'seq')]
    psum x1 -> x0, waiting for transfers between devices: 49.8 us -> none  [shards(): summed_outputs, summed_totals = lax.psum((outputs, totals), 'seq')]
    ppermute x0 -> x25, waiting for transfers between devices: none -> 45 us  [the longest x24 41.7 us: swap(): return lax.ppermute(x, 'seq', [(i, i ^ bit) for i in range(n)])]
    all_gather x1 -> x0, waiting for transfers between devices: 32.8 us -> none  [shards(): all_queries = lax.all_gather(queries, 'seq', axis=0, tiled=True)]
  transfers between devices with their start and end apart: 3 -> 25, of which waited for: 3 -> 20; matrix products, arithmetic and copies ran while one was open for 3% -> 5% of each run, Pallas kernels for 0% -> 13%
where the time goes in v1:
time: 147 us
  Pallas kernels  59.9 us (41%)
  waiting for transfers between devices  45 us (31%)
  starting transfers between devices  26 us (18%)
  local copies, waits for them, and re-layouts  11.3 us (8%)
  other arithmetic  2.55 us (2%)
  matrix products  1.49 us (1%)
    ppermute x24, waiting for transfers between devices, swap(): return lax.ppermute(x, 'seq', [(i, i ^ bit) for i in range(n)])  41.7 us
    pallas_call x1, Pallas kernels, shards(): call(functools.partial(attention_kernel, nq, kv, group, math.log2(math.e)...  40.1 us
    ppermute x24, starting transfers between devices, swap(): return lax.ppermute(x, 'seq', [(i, i ^ bit) for i in range(n)])  24.5 us
    pallas_call x1, Pallas kernels, shards(): call(functools.partial(list_kernel, pages, pairs), [jax.ShapeDtypeStruct(...  17.7 us
    unnamed x32, local copies, waits for them, and re-layouts  5.99 us
    ppermute x1, waiting for transfers between devices, shards(): took = lax.ppermute(give, 'head', [(i, i ^ step) for i in range(nh)])  3.35 us
  transfers between devices with their start and end apart: 25, of which 20 were waited for; matrix products, arithmetic and copies ran while one was open for 5% of the time, Pallas kernels for 13%

profile of v1, /device:TPU:0, one launch (start us, length us, event | category | flops | bytes accessed | tf_op | source)
XLA Modules:
  0.0 146.7 jit_solution(1583074926658474324)
XLA Ops:
  0.9 4.1 %collective-permute-start = (bf16[8,32,128]{2,1,0:T(8,128)(2,1)S(1)}, bf16[8,32,128]{2,1,0:T(8,128)(2,1)S(1)}, u32[]{:S(2)}, u32[]{:S(2)}) collective-permute-start(bf16[8,32,128]{2,1,0:T(8,128)(2,1)S(1)} %get-tuple-element.44), channel_id=1, source_target_pairs={{0,16},{2,18},{4,20},{6,22},{8,24},{10,26},{12,28},{14,30},{16,0},... | collective-permute-start | bytes 196616 | tf_op jit(solution)/shard_map/ppermute | solution.py:229
  8.9 1.9 %collective-permute-start.1 = (bf16[16,32,128]{2,1,0:T(8,128)(2,1)S(1)}, bf16[16,32,128]{2,1,0:T(8,128)(2,1)S(1)}, u32[]{:S(2)}, u32[]{:S(2)}) collective-permute-start(bf16[16,32,128]{2,1,0:T(8,128)(2,1)S(1)} %pad_maximum_fusion.8), channel_id=1, source_target_pairs={{0,8},{2,10},{4,12},{6,14},{8,0},{10,2},{12,4},{14,6},{16,24},{18,... | collective-permute-start | bytes 393224 | tf_op jit(solution)/shard_map/ppermute | solution.py:229
  11.5 1.8 %collective-permute-start.5 = (bf16[16,32,128]{2,1,0:T(8,128)(2,1)S(1)}, bf16[16,32,128]{2,1,0:T(8,128)(2,1)S(1)}, u32[]{:S(2)}, u32[]{:S(2)}) collective-permute-start(bf16[16,32,128]{2,1,0:T(8,128)(2,1)S(1)} %pad_maximum_fusion.9), channel_id=1, source_target_pairs={{0,4},{2,6},{4,0},{6,2},{8,12},{10,14},{12,8},{14,10},{16,20},{18,... | collective-permute-start | bytes 393224 | tf_op jit(solution)/shard_map/ppermute | solution.py:229
  14.4 1.7 %collective-permute-start.2 = (bf16[32,32,128]{2,1,0:T(8,128)(2,1)S(1)}, bf16[32,32,128]{2,1,0:T(8,128)(2,1)S(1)}, u32[]{:S(2)}, u32[]{:S(2)}) collective-permute-start(bf16[32,32,128]{2,1,0:T(8,128)(2,1)S(1)} %pad_maximum_fusion.4), channel_id=1, source_target_pairs={{0,4},{2,6},{4,0},{6,2},{8,12},{10,14},{12,8},{14,10},{16,20},{18,... | collective-permute-start | bytes 786440 | tf_op jit(solution)/shard_map/ppermute | solution.py:229
  18.1 4.3 %collective-permute-done.2 = bf16[32,32,128]{2,1,0:T(8,128)(2,1)S(1)} collective-permute-done((bf16[32,32,128]{2,1,0:T(8,128)(2,1)S(1)}, bf16[32,32,128]{2,1,0:T(8,128)(2,1)S(1)}, u32[]{:S(2)}, u32[]{:S(2)}) %collective-permute-start.2) | collective-permute-done | bytes 262176 | tf_op jit(solution)/shard_map/ppermute | solution.py:229
  25.3 17.7 %lists.1 = (s32[2112]{0:T(1024)S(1)}, s32[132]{0:T(256)S(1)}, s32[1]{0:T(128)}) custom-call(s32[1024]{0:T(1024)S(1)} %select_n.69.idx_ref), custom_call_target="tpu_custom_call" | custom-call | flops 1000000000 | bytes 1000000 | tf_op jit(solution)/shard_map/lists/pallas_call | solution.py:258
  45.7 40.1 %attention.1 = (bf16[2144,128]{1,0:T(8,128)(2,1)}, bf16[2144,128]{1,0:T(8,128)(2,1)}, bf16[2144,128]{1,0:T(8,128)(2,1)}, bf16[2144,128]{1,0:T(8,128)(2,1)}) custom-call(s32[2112]{0:T(1024)} %copy-done.2, s32[132]{0:T(256)} %copy-done.3, s32[1]{0:T(128)} %get-tuple-element.26.ng, s32[256]{0:T(256)} %copy-done.9, bf16[64,32,128]{2,1,0:T(8,128)(2,1)} %copy-done.4, ...), custom_call_target="tpu_custom_call" | custom-call | flops 2147483648 | bytes 16777216 | tf_op jit(solution)/shard_map/attention/pallas_call | solution.py:285
  86.5 1.7 %collective-permute-done.8.recv = bf16[2144,128]{1,0:T(8,128)(2,1)S(1)} collective-permute-done((bf16[2144,128]{1,0:T(8,128)(2,1)}, bf16[2144,128]{1,0:T(8,128)(2,1)S(1)}, u32[]{:S(2)}, u32[]{:S(2)}) %collective-permute-start.8) | collective-permute-done | bytes 548896 | tf_op jit(solution)/shard_map/ppermute | solution.py:229
  89.7 3.1 %collective-permute-start.9 = (bf16[1120,128]{1,0:T(8,128)(2,1)S(1)}, bf16[1120,128]{1,0:T(8,128)(2,1)S(1)}, u32[]{:S(2)}, u32[]{:S(2)}) collective-permute-start(bf16[1120,128]{1,0:T(8,128)(2,1)S(1)} %get-tuple-element.30), channel_id=1, source_target_pairs={{0,4},{2,6},{4,0},{6,2},{8,12},{10,14},{12,8},{14,10},{16,20},{18,... | collective-permute-start | bytes 860168 | tf_op jit(solution)/shard_map/ppermute | solution.py:229
  94.8 5.3 %collective-permute-done.9.recv = bf16[1120,128]{1,0:T(8,128)(2,1)S(1)} collective-permute-done((bf16[1120,128]{1,0:T(8,128)(2,1)S(1)}, bf16[1120,128]{1,0:T(8,128)(2,1)S(1)}, u32[]{:S(2)}, u32[]{:S(2)}) %collective-permute-start.9) | collective-permute-done | bytes 286752 | tf_op jit(solution)/shard_map/ppermute | solution.py:229
  101.8 1.7 %collective-permute-done.17.recv = bf16[1120,128]{1,0:T(8,128)(2,1)S(1)} collective-permute-done((bf16[1120,128]{1,0:T(8,128)(2,1)S(1)}, bf16[1120,128]{1,0:T(8,128)(2,1)S(1)}, u32[]{:S(2)}, u32[]{:S(2)}) %collective-permute-start.17) | collective-permute-done | bytes 286752 | tf_op jit(solution)/shard_map/ppermute | solution.py:229
  103.8 2.6 %collective-permute-done.10.recv = bf16[608,128]{1,0:T(8,128)(2,1)S(1)} collective-permute-done((bf16[608,128]{1,0:T(8,128)(2,1)S(1)}, bf16[608,128]{1,0:T(8,128)(2,1)S(1)}, u32[]{:S(2)}, u32[]{:S(2)}) %collective-permute-start.10) | collective-permute-done | bytes 155680 | tf_op jit(solution)/shard_map/ppermute | solution.py:229
  106.7 1.9 %collective-permute-start.11 = (bf16[352,128]{1,0:T(8,128)(2,1)S(1)}, bf16[352,128]{1,0:T(8,128)(2,1)S(1)}, u32[]{:S(2)}, u32[]{:S(2)}) collective-permute-start(bf16[352,128]{1,0:T(8,128)(2,1)S(1)} %get-tuple-element.34), channel_id=1, source_target_pairs={{0,16},{2,18},{4,20},{6,22},{8,24},{10,26},{12,28},{14,30},{16,0},... | collective-permute-start | bytes 270344 | tf_op jit(solution)/shard_map/ppermute | solution.py:229
  109.2 1.8 %collective-permute-start.19 = (bf16[352,128]{1,0:T(8,128)(2,1)S(1)}, bf16[352,128]{1,0:T(8,128)(2,1)S(1)}, u32[]{:S(2)}, u32[]{:S(2)}) collective-permute-start(bf16[352,128]{1,0:T(8,128)(2,1)S(1)} %get-tuple-element.42), channel_id=1, source_target_pairs={{0,16},{2,18},{4,20},{6,22},{8,24},{10,26},{12,28},{14,30},{16,0},... | collective-permute-start | bytes 270344 | tf_op jit(solution)/shard_map/ppermute | solution.py:229
  111.0 5.0 %collective-permute-done.11.recv = bf16[352,128]{1,0:T(8,128)(2,1)S(1)} collective-permute-done((bf16[352,128]{1,0:T(8,128)(2,1)S(1)}, bf16[352,128]{1,0:T(8,128)(2,1)S(1)}, u32[]{:S(2)}, u32[]{:S(2)}) %collective-permute-start.11) | collective-permute-done | bytes 90144 | tf_op jit(solution)/shard_map/ppermute | solution.py:229
  116.3 2.1 %collective-permute-done.19.recv = bf16[352,128]{1,0:T(8,128)(2,1)S(1)} collective-permute-done((bf16[352,128]{1,0:T(8,128)(2,1)S(1)}, bf16[352,128]{1,0:T(8,128)(2,1)S(1)}, u32[]{:S(2)}, u32[]{:S(2)}) %collective-permute-start.19) | collective-permute-done | bytes 90144 | tf_op jit(solution)/shard_map/ppermute | solution.py:229
  119.5 3.5 %collective-permute-done.12 = bf16[8,4096]{1,0:T(8,128)(2,1)S(1)} collective-permute-done((bf16[8,4096]{1,0:T(8,128)(2,1)S(1)}, bf16[8,4096]{1,0:T(8,128)(2,1)S(1)}, u32[]{:S(2)}, u32[]{:S(2)}) %collective-permute-start.12) | collective-permute-done | bytes 65568 | tf_op jit(solution)/shard_map/ppermute | solution.py:229
  124.8 3.2 %collective-permute-done.13 = bf16[16,4096]{1,0:T(8,128)(2,1)S(1)} collective-permute-done((bf16[16,4096]{1,0:T(8,128)(2,1)S(1)}, bf16[16,4096]{1,0:T(8,128)(2,1)S(1)}, u32[]{:S(2)}, u32[]{:S(2)}) %collective-permute-start.13) | collective-permute-done | bytes 131104 | tf_op jit(solution)/shard_map/ppermute | solution.py:229
  130.0 1.9 %collective-permute-start.22 = (bf16[32,4096]{1,0:T(8,128)(2,1)S(1)}, bf16[32,4096]{1,0:T(8,128)(2,1)S(1)}, u32[]{:S(2)}, u32[]{:S(2)}) collective-permute-start(bf16[32,4096]{1,0:T(8,128)(2,1)S(1)} %pad_maximum_fusion.7), channel_id=1, source_target_pairs={{0,8},{2,10},{4,12},{6,14},{8,0},{10,2},{12,4},{14,6},{16,24},{18,... | collective-permute-start | bytes 786440 | tf_op jit(solution)/shard_map/ppermute | solution.py:229
  131.9 2.5 %collective-permute-done.14 = bf16[32,4096]{1,0:T(8,128)(2,1)S(1)} collective-permute-done((bf16[32,4096]{1,0:T(8,128)(2,1)S(1)}, bf16[32,4096]{1,0:T(8,128)(2,1)S(1)}, u32[]{:S(2)}, u32[]{:S(2)}) %collective-permute-start.14) | collective-permute-done | bytes 262176 | tf_op jit(solution)/shard_map/ppermute | solution.py:229
  134.6 1.8 %collective-permute-done.22 = bf16[32,4096]{1,0:T(8,128)(2,1)S(1)} collective-permute-done((bf16[32,4096]{1,0:T(8,128)(2,1)S(1)}, bf16[32,4096]{1,0:T(8,128)(2,1)S(1)}, u32[]{:S(2)}, u32[]{:S(2)}) %collective-permute-start.22) | collective-permute-done | bytes 262176 | tf_op jit(solution)/shard_map/ppermute | solution.py:229
  136.7 1.7 %collective-permute-done.23 = bf16[64,4096]{1,0:T(8,128)(2,1)S(1)} collective-permute-done((bf16[64,4096]{1,0:T(8,128)(2,1)S(1)}, bf16[64,4096]{1,0:T(8,128)(2,1)S(1)}, u32[]{:S(2)}, u32[]{:S(2)}) %collective-permute-start.23) | collective-permute-done | bytes 524320 | tf_op jit(solution)/shard_map/ppermute | solution.py:229
  140.5 1.6 %collective-permute-start.24 = (bf16[128,512]{1,0:T(8,128)(2,1)S(1)}, bf16[128,512]{1,0:T(8,128)(2,1)S(1)}, u32[]{:S(2)}, u32[]{:S(2)}) collective-permute-start(bf16[128,512]{1,0:T(8,128)(2,1)S(1)} %bitcast.27), channel_id=1, source_target_pairs={{0,1},{1,0},{2,3},{3,2},{4,5},{5,4},{6,7},{7,6},{8,9},{9,8},{10,11... | collective-permute-start | bytes 393224 | tf_op jit(solution)/shard_map/ppermute | solution.py:328
  142.6 3.4 %collective-permute-done.24 = bf16[128,512]{1,0:T(8,128)(2,1)S(1)} collective-permute-done((bf16[128,512]{1,0:T(8,128)(2,1)S(1)}, bf16[128,512]{1,0:T(8,128)(2,1)S(1)}, u32[]{:S(2)}, u32[]{:S(2)}) %collective-permute-start.24) | collective-permute-done | bytes 131104 | tf_op jit(solution)/shard_map/ppermute | solution.py:328
  (111 shorter events, 29.8 us)
Async XLA Ops:
  0.9 8.0 %collective-permute-start = (bf16[8,32,128]{2,1,0:T(8,128)(2,1)S(1)}, bf16[8,32,128]{2,1,0:T(8,128)(2,1)S(1)}, u32[]{:S(2)}, u32[]{:S(2)}) collective-permute-start(bf16[8,32,128]{2,1,0:T(8,128)(2,1)S(1)} %get-tuple-element.44), channel_id=1, source_target_pairs={{0,16},{2,18},{4,20},{6,22},{8,24},{10,26},{12,28},{14,30},{16,0},... | collective-permute-start | bytes 196616 | tf_op jit(solution)/shard_map/ppermute | solution.py:229
  5.0 6.5 %collective-permute-start.4 = (bf16[8,32,128]{2,1,0:T(8,128)(2,1)S(1)}, bf16[8,32,128]{2,1,0:T(8,128)(2,1)S(1)}, u32[]{:S(2)}, u32[]{:S(2)}) collective-permute-start(bf16[8,32,128]{2,1,0:T(8,128)(2,1)S(1)} %get-tuple-element.43), channel_id=1, source_target_pairs={{0,16},{2,18},{4,20},{6,22},{8,24},{10,26},{12,28},{14,30},{16,0},... | collective-permute-start | bytes 196616 | tf_op jit(solution)/shard_map/ppermute | solution.py:229
  8.9 5.5 %collective-permute-start.1 = (bf16[16,32,128]{2,1,0:T(8,128)(2,1)S(1)}, bf16[16,32,128]{2,1,0:T(8,128)(2,1)S(1)}, u32[]{:S(2)}, u32[]{:S(2)}) collective-permute-start(bf16[16,32,128]{2,1,0:T(8,128)(2,1)S(1)} %pad_maximum_fusion.8), channel_id=1, source_target_pairs={{0,8},{2,10},{4,12},{6,14},{8,0},{10,2},{12,4},{14,6},{16,24},{18,... | collective-permute-start | bytes 393224 | tf_op jit(solution)/shard_map/ppermute | solution.py:229
  11.5 5.8 %collective-permute-start.5 = (bf16[16,32,128]{2,1,0:T(8,128)(2,1)S(1)}, bf16[16,32,128]{2,1,0:T(8,128)(2,1)S(1)}, u32[]{:S(2)}, u32[]{:S(2)}) collective-permute-start(bf16[16,32,128]{2,1,0:T(8,128)(2,1)S(1)} %pad_maximum_fusion.9), channel_id=1, source_target_pairs={{0,4},{2,6},{4,0},{6,2},{8,12},{10,14},{12,8},{14,10},{16,20},{18,... | collective-permute-start | bytes 393224 | tf_op jit(solution)/shard_map/ppermute | solution.py:229
  14.4 7.9 %collective-permute-start.2 = (bf16[32,32,128]{2,1,0:T(8,128)(2,1)S(1)}, bf16[32,32,128]{2,1,0:T(8,128)(2,1)S(1)}, u32[]{:S(2)}, u32[]{:S(2)}) collective-permute-start(bf16[32,32,128]{2,1,0:T(8,128)(2,1)S(1)} %pad_maximum_fusion.4), channel_id=1, source_target_pairs={{0,4},{2,6},{4,0},{6,2},{8,12},{10,14},{12,8},{14,10},{16,20},{18,... | collective-permute-start | bytes 786440 | tf_op jit(solution)/shard_map/ppermute | solution.py:229
  17.3 6.7 %collective-permute-start.6 = (bf16[32,32,128]{2,1,0:T(8,128)(2,1)S(1)}, bf16[32,32,128]{2,1,0:T(8,128)(2,1)S(1)}, u32[]{:S(2)}, u32[]{:S(2)}) collective-permute-start(bf16[32,32,128]{2,1,0:T(8,128)(2,1)S(1)} %pad_maximum_fusion.5), channel_id=1, source_target_pairs={{0,8},{2,10},{4,12},{6,14},{8,0},{10,2},{12,4},{14,6},{16,24},{18,... | collective-permute-start | bytes 786440 | tf_op jit(solution)/shard_map/ppermute | solution.py:229
  22.4 21.7 %collective-permute-start.3 = (bf16[64,32,128]{2,1,0:T(8,128)(2,1)S(1)}, bf16[64,32,128]{2,1,0:T(8,128)(2,1)S(1)}, u32[]{:S(2)}, u32[]{:S(2)}) collective-permute-start(bf16[64,32,128]{2,1,0:T(8,128)(2,1)S(1)} %pad_maximum_fusion.refs_0_), channel_id=1, source_target_pairs={{0,2},{2,0},{4,6},{6,4},{8,10},{10,8},{12,14},{14,12},{16,18},{18,... | collective-permute-start | bytes 1572872 | tf_op jit(solution)/shard_map/ppermute | solution.py:229
  24.1 20.0 %collective-permute-start.7 = (bf16[64,32,128]{2,1,0:T(8,128)(2,1)S(1)}, bf16[64,32,128]{2,1,0:T(8,128)(2,1)S(1)}, u32[]{:S(2)}, u32[]{:S(2)}) collective-permute-start(bf16[64,32,128]{2,1,0:T(8,128)(2,1)S(1)} %pad_maximum_fusion.1.refs_2_), channel_id=1, source_target_pairs={{0,2},{2,0},{4,6},{6,4},{8,10},{10,8},{12,14},{14,12},{16,18},{18,... | collective-permute-start | bytes 1572872 | tf_op jit(solution)/shard_map/ppermute | solution.py:229
  85.8 2.4 %collective-permute-start.8 = (bf16[2144,128]{1,0:T(8,128)(2,1)}, bf16[2144,128]{1,0:T(8,128)(2,1)S(1)}, u32[]{:S(2)}, u32[]{:S(2)}) collective-permute-start(bf16[2144,128]{1,0:T(8,128)(2,1)} %get-tuple-element.28), channel_id=1, source_target_pairs={{0,2},{2,0},{4,6},{6,4},{8,10},{10,8},{12,14},{14,12},{16,18},{18,... | collective-permute-start | bytes 1646600 | tf_op jit(solution)/shard_map/ppermute | solution.py:229
  86.4 6.4 %collective-permute-start.16 = (bf16[2144,128]{1,0:T(8,128)(2,1)}, bf16[2144,128]{1,0:T(8,128)(2,1)S(1)}, u32[]{:S(2)}, u32[]{:S(2)}) collective-permute-start(bf16[2144,128]{1,0:T(8,128)(2,1)} %get-tuple-element.36), channel_id=1, source_target_pairs={{0,2},{2,0},{4,6},{6,4},{8,10},{10,8},{12,14},{14,12},{16,18},{18,... | collective-permute-start | bytes 1646600 | tf_op jit(solution)/shard_map/ppermute | solution.py:229
  89.7 10.4 %collective-permute-start.9 = (bf16[1120,128]{1,0:T(8,128)(2,1)S(1)}, bf16[1120,128]{1,0:T(8,128)(2,1)S(1)}, u32[]{:S(2)}, u32[]{:S(2)}) collective-permute-start(bf16[1120,128]{1,0:T(8,128)(2,1)S(1)} %get-tuple-element.30), channel_id=1, source_target_pairs={{0,4},{2,6},{4,0},{6,2},{8,12},{10,14},{12,8},{14,10},{16,20},{18,... | collective-permute-start | bytes 860168 | tf_op jit(solution)/shard_map/ppermute | solution.py:229
  94.3 9.2 %collective-permute-start.17 = (bf16[1120,128]{1,0:T(8,128)(2,1)S(1)}, bf16[1120,128]{1,0:T(8,128)(2,1)S(1)}, u32[]{:S(2)}, u32[]{:S(2)}) collective-permute-start(bf16[1120,128]{1,0:T(8,128)(2,1)S(1)} %get-tuple-element.38), channel_id=1, source_target_pairs={{0,8},{2,10},{4,12},{6,14},{8,0},{10,2},{12,4},{14,6},{16,24},{18,... | collective-permute-start | bytes 860168 | tf_op jit(solution)/shard_map/ppermute | solution.py:229
  100.4 6.1 %collective-permute-start.10 = (bf16[608,128]{1,0:T(8,128)(2,1)S(1)}, bf16[608,128]{1,0:T(8,128)(2,1)S(1)}, u32[]{:S(2)}, u32[]{:S(2)}) collective-permute-start(bf16[608,128]{1,0:T(8,128)(2,1)S(1)} %get-tuple-element.32), channel_id=1, source_target_pairs={{0,8},{2,10},{4,12},{6,14},{8,0},{10,2},{12,4},{14,6},{16,24},{18,... | collective-permute-start | bytes 466952 | tf_op jit(solution)/shard_map/ppermute | solution.py:229
  103.7 5.3 %collective-permute-start.18 = (bf16[608,128]{1,0:T(8,128)(2,1)S(1)}, bf16[608,128]{1,0:T(8,128)(2,1)S(1)}, u32[]{:S(2)}, u32[]{:S(2)}) collective-permute-start(bf16[608,128]{1,0:T(8,128)(2,1)S(1)} %get-tuple-element.40), channel_id=1, source_target_pairs={{0,4},{2,6},{4,0},{6,2},{8,12},{10,14},{12,8},{14,10},{16,20},{18,... | collective-permute-start | bytes 466952 | tf_op jit(solution)/shard_map/ppermute | solution.py:229
  106.7 9.4 %collective-permute-start.11 = (bf16[352,128]{1,0:T(8,128)(2,1)S(1)}, bf16[352,128]{1,0:T(8,128)(2,1)S(1)}, u32[]{:S(2)}, u32[]{:S(2)}) collective-permute-start(bf16[352,128]{1,0:T(8,128)(2,1)S(1)} %get-tuple-element.34), channel_id=1, source_target_pairs={{0,16},{2,18},{4,20},{6,22},{8,24},{10,26},{12,28},{14,30},{16,0},... | collective-permute-start | bytes 270344 | tf_op jit(solution)/shard_map/ppermute | solution.py:229
  109.2 9.2 %collective-permute-start.19 = (bf16[352,128]{1,0:T(8,128)(2,1)S(1)}, bf16[352,128]{1,0:T(8,128)(2,1)S(1)}, u32[]{:S(2)}, u32[]{:S(2)}) collective-permute-start(bf16[352,128]{1,0:T(8,128)(2,1)S(1)} %get-tuple-element.42), channel_id=1, source_target_pairs={{0,16},{2,18},{4,20},{6,22},{8,24},{10,26},{12,28},{14,30},{16,0},... | collective-permute-start | bytes 270344 | tf_op jit(solution)/shard_map/ppermute | solution.py:229
  116.2 6.7 %collective-permute-start.12 = (bf16[8,4096]{1,0:T(8,128)(2,1)S(1)}, bf16[8,4096]{1,0:T(8,128)(2,1)S(1)}, u32[]{:S(2)}, u32[]{:S(2)}) collective-permute-start(bf16[8,4096]{1,0:T(8,128)(2,1)S(1)} %reshape.181), channel_id=1, source_target_pairs={{0,16},{2,18},{4,20},{6,22},{8,24},{10,26},{12,28},{14,30},{16,0},... | collective-permute-start | bytes 196616 | tf_op jit(solution)/shard_map/ppermute | solution.py:229
  118.6 5.2 %collective-permute-start.20 = (bf16[8,4096]{1,0:T(8,128)(2,1)S(1)}, bf16[8,4096]{1,0:T(8,128)(2,1)S(1)}, u32[]{:S(2)}, u32[]{:S(2)}) collective-permute-start(bf16[8,4096]{1,0:T(8,128)(2,1)S(1)} %reshape.182), channel_id=1, source_target_pairs={{0,16},{2,18},{4,20},{6,22},{8,24},{10,26},{12,28},{14,30},{16,0},... | collective-permute-start | bytes 196616 | tf_op jit(solution)/shard_map/ppermute | solution.py:229
  123.0 5.1 %collective-permute-start.13 = (bf16[16,4096]{1,0:T(8,128)(2,1)S(1)}, bf16[16,4096]{1,0:T(8,128)(2,1)S(1)}, u32[]{:S(2)}, u32[]{:S(2)}) collective-permute-start(bf16[16,4096]{1,0:T(8,128)(2,1)S(1)} %pad_maximum_fusion.10), channel_id=1, source_target_pairs={{0,8},{2,10},{4,12},{6,14},{8,0},{10,2},{12,4},{14,6},{16,24},{18,... | collective-permute-start | bytes 393224 | tf_op jit(solution)/shard_map/ppermute | solution.py:229
  123.8 6.1 %collective-permute-start.21 = (bf16[16,4096]{1,0:T(8,128)(2,1)S(1)}, bf16[16,4096]{1,0:T(8,128)(2,1)S(1)}, u32[]{:S(2)}, u32[]{:S(2)}) collective-permute-start(bf16[16,4096]{1,0:T(8,128)(2,1)S(1)} %pad_maximum_fusion.11), channel_id=1, source_target_pairs={{0,4},{2,6},{4,0},{6,2},{8,12},{10,14},{12,8},{14,10},{16,20},{18,... | collective-permute-start | bytes 393224 | tf_op jit(solution)/shard_map/ppermute | solution.py:229
  128.0 6.4 %collective-permute-start.14 = (bf16[32,4096]{1,0:T(8,128)(2,1)S(1)}, bf16[32,4096]{1,0:T(8,128)(2,1)S(1)}, u32[]{:S(2)}, u32[]{:S(2)}) collective-permute-start(bf16[32,4096]{1,0:T(8,128)(2,1)S(1)} %pad_maximum_fusion.6), channel_id=1, source_target_pairs={{0,4},{2,6},{4,0},{6,2},{8,12},{10,14},{12,8},{14,10},{16,20},{18,... | collective-permute-start | bytes 786440 | tf_op jit(solution)/shard_map/ppermute | solution.py:229
  130.0 6.4 %collective-permute-start.22 = (bf16[32,4096]{1,0:T(8,128)(2,1)S(1)}, bf16[32,4096]{1,0:T(8,128)(2,1)S(1)}, u32[]{:S(2)}, u32[]{:S(2)}) collective-permute-start(bf16[32,4096]{1,0:T(8,128)(2,1)S(1)} %pad_maximum_fusion.7), channel_id=1, source_target_pairs={{0,8},{2,10},{4,12},{6,14},{8,0},{10,2},{12,4},{14,6},{16,24},{18,... | collective-permute-start | bytes 786440 | tf_op jit(solution)/shard_map/ppermute | solution.py:229
  134.5 2.1 %collective-permute-start.15 = (bf16[64,4096]{1,0:T(8,128)(2,1)S(1)}, bf16[64,4096]{1,0:T(8,128)(2,1)S(1)}, u32[]{:S(2)}, u32[]{:S(2)}) collective-permute-start(bf16[64,4096]{1,0:T(8,128)(2,1)S(1)} %pad_maximum_fusion.2), channel_id=1, source_target_pairs={{0,2},{2,0},{4,6},{6,4},{8,10},{10,8},{12,14},{14,12},{16,18},{18,... | collective-permute-start | bytes 1572872 | tf_op jit(solution)/shard_map/ppermute | solution.py:229
  140.5 5.5 %collective-permute-start.24 = (bf16[128,512]{1,0:T(8,128)(2,1)S(1)}, bf16[128,512]{1,0:T(8,128)(2,1)S(1)}, u32[]{:S(2)}, u32[]{:S(2)}) collective-permute-start(bf16[128,512]{1,0:T(8,128)(2,1)S(1)} %bitcast.27), channel_id=1, source_target_pairs={{0,1},{1,0},{2,3},{3,2},{4,5},{5,4},{6,7},{7,6},{8,9},{9,8},{10,11... | collective-permute-start | bytes 393224 | tf_op jit(solution)/shard_map/ppermute | solution.py:328
  (12 other events, 124.6 us)

commit v2 on v1

v2 whole, which is shorter than its diff:
```python
import functools
import math

import jax
import jax.numpy as jnp
from jax import lax
from jax.experimental import pallas as pl
from jax.experimental.pallas import tpu as pltpu
from jax.sharding import PartitionSpec as P

CAP = 4
TILE = 16
SEGMENTS = 4
TOGETHER = 2
UNROLL = 4
LEAD = 2 * TOGETHER
NONE = -1e30
PLANES = 3
LANES = 128


def call(body, out_shape, in_specs, out_specs, flops, moved, **kw):
    return pl.pallas_call(
        body,
        out_shape=out_shape,
        in_specs=in_specs,
        out_specs=out_specs,
        cost_estimate=pl.CostEstimate(flops=flops, bytes_accessed=moved, transcendentals=0),
        **kw,
    )


SMEM = pl.BlockSpec(memory_space=pltpu.SMEM)
VMEM = pl.BlockSpec(memory_space=pltpu.VMEM)
ANY = pl.BlockSpec(memory_space=pl.ANY)


def list_kernel(pages, me_ref, table_ref, count_ref, lst_ref, gp_ref, start_ref, valid_ref):
    batch, slots = table_ref.shape
    most = gp_ref.shape[1]
    f32, bf16, i32 = jnp.float32, jnp.bfloat16, jnp.int32

    def iota(shape, axis):
        return lax.broadcasted_iota(i32, shape, axis)

    def ones_where(mask):
        return jnp.where(mask, 1.0, 0.0).astype(bf16)

    def dot(x, y, dims=((1,), (0,)), **kw):
        return lax.dot_general(x, y, (dims, ((), ())), preferred_element_type=f32, **kw)

    page = table_ref[...] - me_ref[0] * pages
    present = (iota((batch, slots), 1) < count_ref[...]) & (page >= 0) & (page < pages)
    here = ones_where(present)
    upto = dot(here, ones_where(iota((slots, slots), 0) <= iota((slots, slots), 1)))
    valid_ref[...] = dot(jnp.ones((8, slots), bf16), here, ((1,), (1,)))[:1].astype(i32)
    hot = []
    for r in range(CAP):
        mine = present & (upto == r + 1.0)
        chosen = jnp.max(jnp.where(mine, page, -1), axis=1, keepdims=True)
        hot.append(jnp.where(iota((batch, pages), 1) == chosen, 1.0, 0.0))
    every = sum(hot[1:], hot[0]).astype(bf16)
    before = dot(ones_where(iota((batch, batch), 0) > iota((batch, batch), 1)), every)

    def groups(n):
        return jnp.floor((n + (TILE - 1.0)) * (1.0 / TILE))

    exact = dict(precision=lax.Precision.HIGHEST)
    row = groups(dot(jnp.ones((8, batch), bf16), every))
    under = jnp.where(iota((pages, pages), 0) < iota((pages, pages), 1), 1.0, 0.0)
    base = dot(row, under, **exact)[:1] + LEAD
    place = base * TILE + before
    col = groups(dot(every, jnp.ones((batch, LANES), bf16), ((0,), (0,))))
    over = jnp.where(iota((pages, pages), 1) < iota((pages, pages), 0), 1.0, 0.0)
    base_col = dot(over, col, **exact)[:, :1] + LEAD
    at_most = jnp.where(base_col <= iota((pages, most), 1).astype(f32), 1.0, 0.0)
    gp_ref[...] = jnp.maximum(jnp.sum(at_most, axis=0, keepdims=True) - 1.0, 0.0).astype(i32)

    bound = iota((pages, LANES), 1) * (pages // SEGMENTS)
    start_ref[...] = jnp.sum(jnp.where(iota((pages, LANES), 0) < bound, col, 0.0), axis=0, keepdims=True).astype(i32)

    size = lst_ref.shape[1]
    total = jnp.zeros((8, size), f32)
    for r in range(CAP):
        to = jnp.sum(jnp.where(hot[r] > 0.0, place + 1.0, 0.0), axis=1, keepdims=True).astype(i32) - 1
        onto = ones_where(iota((batch, size), 1) == to)
        pair = iota((8, batch), 1) * CAP + r
        which = iota((8, batch), 0)
        parts = jnp.where(which == 0, pair // 64, jnp.where(which == 1, pair % 64, 1)).astype(f32)
        total = total + dot(parts.astype(bf16), onto)
    found = total[0:1] * 64.0 + total[1:2]
    lst_ref[...] = jnp.where(total[2:3] > 0.5, found, float(batch * CAP)).astype(i32)


def make_lists(me, table, counts, pages):
    batch, slots = table.shape
    most = -(-(pages + batch * CAP // TILE + 2 * LEAD + TOGETHER) // 8) * 8
    shapes = [(1, most * TILE), (1, most), (1, LANES), (1, batch)]
    return call(
        functools.partial(list_kernel, pages),
        [jax.ShapeDtypeStruct(s, jnp.int32) for s in shapes],
        [SMEM, VMEM, VMEM],
        [VMEM] * 4,
        10**8,
        10**6,
        name="lists",
        compiler_params=pltpu.CompilerParams(vmem_limit_bytes=16 * 2**20),
    )(me.reshape(1), table, counts.reshape(batch, 1))


def split3(x):
    parts = []
    for _ in range(PLANES):
        part = x.astype(jnp.bfloat16)
        parts.append(part)
        x = x - part.astype(jnp.float32)
    return jnp.concatenate(parts, axis=0)


def join3(block, heads):
    x = block.astype(jnp.float32)
    return (x[:heads] + x[heads : 2 * heads]) + x[2 * heads :]


def attention_kernel(nq, kv, group, scale, lst, gp, start, valid, *refs):
    q_refs = refs[:nq]
    cache = refs[nq]
    outs = refs[nq + 1 : 2 * nq + 1]
    kbuf, vbuf, sems, q32, osc, lsc, ssc, msc, psc = refs[2 * nq + 1 :]
    per = q_refs[0].shape[0]
    heads = kv * group
    pairs = nq * per * CAP
    head_dim = vbuf.shape[-1]
    chunk = kbuf.shape[0] // SEGMENTS
    ones = jnp.ones(vbuf.shape[-2:-1] + (LANES,), jnp.bfloat16)

    def copies(g):
        at = pl.ds(g * chunk, chunk)
        return (
            pltpu.make_async_copy(cache.at[0, at], kbuf.at[at], sems.at[0, g]),
            pltpu.make_async_copy(cache.at[1, at], vbuf.at[at], sems.at[1, g]),
        )

    for g in range(SEGMENTS):
        for c in copies(g):
            c.start()

    def convert(a, i):
        for u in range(8):
            row = q_refs[a][i * 8 + u].astype(jnp.float32)
            q32[a * per + i * 8 + u] = row.reshape(kv, group, head_dim)

    for a in range(nq):
        pl.loop(0, per // 8)(functools.partial(convert, a))
    q32[nq * per] = jnp.zeros((kv, group, head_dim), jnp.float32)
    osc[pairs + 1] = jnp.zeros((heads, head_dim), jnp.bfloat16)
    lsc[pairs + 1] = jnp.full((kv, group, LANES), NONE, jnp.float32)

    def step(j):
        def entries(stage, v):
            i = (j + stage) * TOGETHER + v
            return gp[0, i], [lst[0, i * TILE + u] for u in range(TILE)]

        for v in range(TOGETHER):
            page, t = entries(0, v)
            os = []
            for k in range(kv):
                values = jnp.concatenate([vbuf[page, k], ones], axis=1)
                o = jnp.dot(psc[v, k], values, preferred_element_type=jnp.float32)
                total = o[:, head_dim:]
                os.append(o[:, :head_dim] * (1.0 / total))
                lse = msc[v, k] + jnp.log2(total)
                for u in range(TILE):
                    lsc[t[u], k] = lse[u * group : (u + 1) * group]
            for u in range(TILE):
                tiles = [o[u * group : (u + 1) * group] for o in os]
                osc[t[u]] = jnp.concatenate(tiles, axis=0).astype(jnp.bfloat16)
        for v in range(TOGETHER):
            for k in range(kv):
                s = ssc[v, k]
                m = jnp.broadcast_to(jnp.max(s, axis=1, keepdims=True), s.shape)
                psc[v, k] = jnp.exp2(s - m).astype(jnp.bfloat16)
                msc[v, k] = m
        for v in range(TOGETHER):
            page, t = entries(2, v)
            b = [x // CAP for x in t]
            for k in range(kv):
                rows = jnp.concatenate([q32[x, k] for x in b], axis=0)
                s = lax.dot_general(
                    rows.astype(jnp.bfloat16),
                    kbuf[page, k],
                    (((1,), (1,)), ((), ())),
                    preferred_element_type=jnp.float32,
                )
                ssc[v, k] = s * scale

    for g in range(SEGMENTS):
        for c in copies(g):
            c.wait()
        end = start[0, g + 1]
        if g == SEGMENTS - 1:
            end = end + (3 * TOGETHER - 1)
        pl.loop(start[0, g] // TOGETHER, end // TOGETHER)(step)

    lane = lax.broadcasted_iota(jnp.int32, (heads, LANES), 1)
    for a in range(nq):

        def finish(s, stats):
            b = a * per + s
            n = valid[0, b]
            t = [jnp.where(n > r, b * CAP + r, pairs + 1) for r in range(CAP)]
            l = [lsc[x].reshape(heads, LANES) for x in t]
            top = functools.reduce(jnp.maximum, l)
            w = [jnp.exp2(x - top) for x in l]
            total = sum(w[1:], w[0])
            terms = [x * osc[y].astype(jnp.float32) for x, y in zip(w, t)]
            o = sum(terms[1:], terms[0]) * (1.0 / total)
            outs[a][pl.ds(pl.multiple_of(s * heads, heads), heads), :] = o.astype(jnp.bfloat16)
            return jnp.where(lane == s, top + jnp.log2(total), stats)

        stats = lax.fori_loop(0, per, finish, jnp.full((heads, LANES), NONE, jnp.float32), unroll=UNROLL)
        outs[a][per * heads :, :] = split3(stats)


def merge_kernel(per, heads, keep, recv, *outs):
    rows = per * heads
    la = join3(keep[rows:, :], heads)
    lb = join3(recv[rows:, :], heads)
    diff = la - lb
    weight = 1.0 / (1.0 + jnp.exp2(-diff))
    each = per // len(outs)
    for s in range(per):
        sl = slice(s * heads, (s + 1) * heads)
        x = keep[sl, :].astype(jnp.float32)
        y = recv[sl, :].astype(jnp.float32)
        z = y + weight[:, s : s + 1] * (x - y)
        at = s % each
        outs[s // each][at * heads : (at + 1) * heads, :] = z.astype(jnp.bfloat16)
    if len(outs) > 1:
        stats = jnp.maximum(la, lb) + jnp.log2(1.0 + jnp.exp2(-jnp.abs(diff)))
        for i, out in enumerate(outs):
            part = stats if i == 0 else jnp.concatenate([stats[:, i * each :], stats[:, : i * each]], axis=1)
            out[each * heads :, :] = split3(part)


def merge(keep, recv, per, heads, last):
    if last:
        shapes = [jax.ShapeDtypeStruct((per * heads, LANES), jnp.bfloat16)]
    else:
        shapes = [jax.ShapeDtypeStruct(((per // 2 + PLANES) * heads, LANES), jnp.bfloat16)] * 2
    return call(
        functools.partial(merge_kernel, per, heads),
        shapes,
        [VMEM] * 2,
        [VMEM] * len(shapes),
        keep.size * 8,
        keep.size * 6,
        name="merge",
        compiler_params=pltpu.CompilerParams(vmem_limit_bytes=8 * 2**20),
    )(keep, recv)


def attend(lst, gp, start, valid, q_parts, cache):
    nq = len(q_parts)
    per, heads, head_dim = q_parts[0].shape
    _, pages, kv, page_len, _ = cache.shape
    group = heads // kv
    batch = nq * per
    pairs = batch * CAP
    scratch = [pltpu.VMEM(cache.shape[1:], cache.dtype)] * 2 + [pltpu.SemaphoreType.DMA((2, SEGMENTS))]
    scratch += [pltpu.VMEM((batch + 1, kv, group, head_dim), jnp.float32)]
    scratch += [pltpu.VMEM((pairs + 2, heads, head_dim), jnp.bfloat16)]
    scratch += [pltpu.VMEM((pairs + 2, kv, group, LANES), jnp.float32)]
    scratch += [pltpu.VMEM((TOGETHER, kv, TILE * group, page_len), jnp.float32)] * 2
    scratch += [pltpu.VMEM((TOGETHER, kv, TILE * group, page_len), jnp.bfloat16)]
    return call(
        functools.partial(attention_kernel, nq, kv, group, math.log2(math.e) / math.sqrt(head_dim)),
        [jax.ShapeDtypeStruct(((per + PLANES) * heads, LANES), jnp.bfloat16)] * nq,
        [SMEM] * 4 + [VMEM] * nq + [ANY],
        [VMEM] * nq,
        4 * pairs * heads * page_len * head_dim,
        cache.size * 2,
        scratch_shapes=scratch,
        name="attention",
        compiler_params=pltpu.CompilerParams(vmem_limit_bytes=47 * 2**20),
    )(lst, gp, start, valid, *q_parts, cache)


def shards(n, nh, queries, cache, page_table, page_count, out_weight):
    me = lax.axis_index("seq")
    my_head = lax.axis_index("head")
    _, pages, kv, page_len, head_dim = cache.shape
    local, heads, _ = queries.shape
    group = heads // kv
    batch, slots = page_table.shape
    bits = [1 << i for i in range(n.bit_length() - 1)]
    outer = bits[1:]
    halves = 2
    half = local // halves
    orders = [outer, outer[1::-1] + outer[2:]]

    def swap(x, bit):
        return lax.ppermute(x, "seq", [(i, i ^ bit) for i in range(n)])

    per = half * n // 2
    rel = []
    for a in range(halves):
        for c in range(2):
            for s in range(n // 2):
                j = c * bits[0]
                for at, bit in enumerate(orders[a]):
                    if (s >> (len(outer) - 1 - at)) & 1:
                        j |= bit
                rel.append((j, a))
    rel_j = jnp.array([j for j, _ in rel], jnp.int32)
    rel_a = jnp.array([a for _, a in rel], jnp.int32)
    true_block = (rel_j ^ me) * halves + rel_a

    table = page_table.reshape(-1, half, slots)[true_block].reshape(batch, slots)
    counts = page_count.reshape(-1, half)[true_block].reshape(batch)

    got = [queries[a * half : (a + 1) * half] for a in range(halves)]
    lists = None
    for at in reversed(range(len(outer))):
        new = [swap(x, orders[a][at]) for a, x in enumerate(got)]
        if at == 0:
            lists = make_lists(me, table, counts, pages)
            new, lists = lax.optimization_barrier((new, lists))
        elif at == len(outer) - 1:
            new, table, counts = lax.optimization_barrier((new, table, counts))
        got = [jnp.concatenate([x, y], axis=0) for x, y in zip(got, new)]
    q_parts = []
    for x in got:
        q_parts += [x, swap(x, bits[0])]

    parts = attend(*lists, q_parts, cache)

    keep = [parts[2 * a] for a in range(halves)]
    send = [parts[2 * a + 1] for a in range(halves)]
    now = per
    att = [None] * halves
    for at in range(len(bits)):
        took = [swap(send[a], ([bits[0]] + orders[a])[at]) for a in range(halves)]
        for a in range(halves):
            last = at == len(bits) - 1
            res = merge(keep[a], took[a], now, heads, last)
            if last:
                att[a] = res[0].reshape(half, heads * head_dim)
            else:
                keep[a], send[a] = res
        now //= 2

    for at in reversed(range(len(outer))):
        new = [swap(x, orders[a][at]) for a, x in enumerate(att)]
        att = [jnp.concatenate([x, y], axis=0) for x, y in zip(att, new)]
    rows = []
    for x in att:
        rows += [x, swap(x, bits[0])]
    product = jnp.dot(jnp.concatenate(rows, axis=0), out_weight, preferred_element_type=jnp.float32)

    width = product.shape[1]
    place = {ja: i for i, ja in enumerate(rel)}
    inverse = jnp.array([place[(j, a)] for j in range(n) for a in range(halves)], jnp.int32).reshape(n, halves)
    source = inverse[jnp.arange(n, dtype=jnp.int32) ^ me].reshape(nh, -1)
    blocks = product.reshape(n * halves, half, width)
    out = blocks[source[my_head]].reshape(batch // nh, width)
    for step in range(1, nh):
        give = blocks[source[my_head ^ step]].astype(jnp.bfloat16).reshape(batch // nh, width)
        took = lax.ppermute(give, "head", [(i, i ^ step) for i in range(nh)])
        out = out + took.astype(jnp.float32)
    return out.astype(jnp.bfloat16)


def solution(mesh):
    n, nh = mesh.shape["seq"], mesh.shape["head"]
    return jax.shard_map(
        functools.partial(shards, n, nh),
        mesh=mesh,
        in_specs=(
            P("seq", "head", None),
            P(None, "seq", "head", None, None),
            P(),
            P(),
            P("head", "seq"),
        ),
        out_specs=P("head", "seq"),
        check_vma=False,
    )
```

time: 147 us -> 115 us (0.78)
  Pallas kernels: 59.9 us -> 33.1 us
  local copies, waits for them, and re-layouts: 11.3 us -> 6.08 us
  waiting for transfers between devices: 45 us -> 46.6 us
    pallas_call x2, Pallas kernels: 57.8 us -> 31 us  [the longest x1 28.8 us: attend(): call(functools.partial(attention_kernel, nq, kv, group, math.log2(math.e)...]
    unnamed x32 -> x14, local copies, waits for them, and re-layouts: 5.99 us -> 1.19 us
    ppermute x24, waiting for transfers between devices: 41.7 us -> 43.3 us  [swap(): return lax.ppermute(x, 'seq', [(i, i ^ bit) for i in range(n)])]
  transfers between devices with their start and end apart: 25 -> 25, of which waited for: 20 -> 18; matrix products, arithmetic and copies ran while one was open for 5% -> 5% of each run, Pallas kernels for 13% -> 4%
where the time goes in v2:
time: 115 us; the launch traced here: 114 us
  waiting for transfers between devices  46.6 us (41%)
  Pallas kernels  33.1 us (29%)
  starting transfers between devices  24.7 us (21%)
  local copies, waits for them, and re-layouts  6.08 us (5%)
  other arithmetic  1.72 us (1%)
  matrix products  1.24 us (1%)
    ppermute x24, waiting for transfers between devices, swap(): return lax.ppermute(x, 'seq', [(i, i ^ bit) for i in range(n)])  43.3 us
    pallas_call x1, Pallas kernels, attend(): call(functools.partial(attention_kernel, nq, kv, group, math.log2(math.e)...  28.8 us
    ppermute x24, starting transfers between devices, swap(): return lax.ppermute(x, 'seq', [(i, i ^ bit) for i in range(n)])  23.1 us
    ppermute x1, waiting for transfers between devices, shards(): took = lax.ppermute(give, 'head', [(i, i ^ step) for i in range(nh)])  3.31 us
  transfers between devices with their start and end apart: 25, of which 18 were waited for; matrix products, arithmetic and copies ran while one was open for 5% of the time, Pallas kernels for 4%

profile of v2, /device:TPU:0, one launch (start us, length us, event | category | flops | bytes accessed | tf_op | source)
XLA Modules:
  0.0 113.7 jit_solution(17341240849711396622)
XLA Ops:
  0.9 4.1 %collective-permute-start = (bf16[8,32,128]{2,1,0:T(8,128)(2,1)S(1)}, bf16[8,32,128]{2,1,0:T(8,128)(2,1)S(1)}, u32[]{:S(2)}, u32[]{:S(2)}) collective-permute-start(bf16[8,32,128]{2,1,0:T(8,128)(2,1)S(1)} %get-tuple-element.66), channel_id=1, source_target_pairs={{0,16},{2,18},{4,20},{6,22},{8,24},{10,26},{12,28},{14,30},{16,0},... | collective-permute-start | bytes 196616 | tf_op jit(solution)/shard_map/ppermute | solution.py:303
  8.8 2.7 %collective-permute-done.1 = bf16[8,32,128]{2,1,0:T(8,128)(2,1)S(1)} collective-permute-done((bf16[8,32,128]{2,1,0:T(8,128)(2,1)S(1)}, bf16[8,32,128]{2,1,0:T(8,128)(2,1)S(1)}, u32[]{:S(2)}, u32[]{:S(2)}) %collective-permute-start.1) | collective-permute-done | bytes 65568 | tf_op jit(solution)/shard_map/ppermute | solution.py:303
  12.1 1.6 %collective-permute-start.4 = (bf16[16,32,128]{2,1,0:T(8,128)(2,1)S(1)}, bf16[16,32,128]{2,1,0:T(8,128)(2,1)S(1)}, u32[]{:S(2)}, u32[]{:S(2)}) collective-permute-start(bf16[16,32,128]{2,1,0:T(8,128)(2,1)S(1)} %pad_maximum_fusion.9), channel_id=1, source_target_pairs={{0,4},{2,6},{4,0},{6,2},{8,12},{10,14},{12,8},{14,10},{16,20},{18,... | collective-permute-start | bytes 393224 | tf_op jit(solution)/shard_map/ppermute | solution.py:303
  13.7 2.8 %collective-permute-done.2 = bf16[16,32,128]{2,1,0:T(8,128)(2,1)S(1)} collective-permute-done((bf16[16,32,128]{2,1,0:T(8,128)(2,1)S(1)}, bf16[16,32,128]{2,1,0:T(8,128)(2,1)S(1)}, u32[]{:S(2)}, u32[]{:S(2)}) %collective-permute-start.2) | collective-permute-done | bytes 131104 | tf_op jit(solution)/shard_map/ppermute | solution.py:303
  16.6 2.0 %collective-permute-start.3 = (bf16[32,32,128]{2,1,0:T(8,128)(2,1)S(1)}, bf16[32,32,128]{2,1,0:T(8,128)(2,1)S(1)}, u32[]{:S(2)}, u32[]{:S(2)}) collective-permute-start(bf16[32,32,128]{2,1,0:T(8,128)(2,1)S(1)} %pad_maximum_fusion.4), channel_id=1, source_target_pairs={{0,4},{2,6},{4,0},{6,2},{8,12},{10,14},{12,8},{14,10},{16,20},{18,... | collective-permute-start | bytes 786440 | tf_op jit(solution)/shard_map/ppermute | solution.py:303
  19.4 2.1 %lists.1 = (s32[1,2304]{1,0:T(1,128)S(1)}, s32[1,144]{1,0:T(1,128)S(1)}, s32[1,128]{1,0:T(1,128)S(1)}, s32[1,256]{1,0:T(1,128)S(1)}) custom-call(s32[1]{0:T(128)} %bitcast.2.me_ref, s32[256,64]{1,0:T(8,128)S(1)} %bitcast.25, s32[256,1]{1,0:T(8,128)S(1)} %copy.10.count_ref), custom_call_target="tpu_custom_call" | custom-call | flops 100000000 | bytes 1000000 | tf_op jit(solution)/shard_map/lists/pallas_call | solution.py:99
  21.5 2.5 %collective-permute-done.3 = bf16[32,32,128]{2,1,0:T(8,128)(2,1)S(1)} collective-permute-done((bf16[32,32,128]{2,1,0:T(8,128)(2,1)S(1)}, bf16[32,32,128]{2,1,0:T(8,128)(2,1)S(1)}, u32[]{:S(2)}, u32[]{:S(2)}) %collective-permute-start.3) | collective-permute-done | bytes 262176 | tf_op jit(solution)/shard_map/ppermute | solution.py:303
  24.0 1.6 %collective-permute-done.5 = bf16[32,32,128]{2,1,0:T(8,128)(2,1)S(1)} collective-permute-done((bf16[32,32,128]{2,1,0:T(8,128)(2,1)S(1)}, bf16[32,32,128]{2,1,0:T(8,128)(2,1)S(1)}, u32[]{:S(2)}, u32[]{:S(2)}) %collective-permute-start.5) | collective-permute-done | bytes 262176 | tf_op jit(solution)/shard_map/ppermute | solution.py:303
  28.4 28.8 %attention.1 = (bf16[2144,128]{1,0:T(8,128)(2,1)S(1)}, bf16[2144,128]{1,0:T(8,128)(2,1)S(1)}, bf16[2144,128]{1,0:T(8,128)(2,1)S(1)}, bf16[2144,128]{1,0:T(8,128)(2,1)S(1)}) custom-call(s32[1,2304]{1,0:T(1,128)S(1)} %get-tuple-element.43.lst, s32[1,144]{1,0:T(1,128)S(1)} %get-tuple-element.44.gp, s32[1,128]{1,0:T(1,128)S(1)} %get-tuple-element.45.start, ...), custom_call_target="tpu_custom_call" | custom-call | flops 2147483648 | bytes 16777216 | tf_op jit(solution)/shard_map/attention/pallas_call | solution.py:276
  57.8 1.4 %collective-permute-done.8.recv = bf16[2144,128]{1,0:T(8,128)(2,1)S(1)} collective-permute-done((bf16[2144,128]{1,0:T(8,128)(2,1)S(1)}, bf16[2144,128]{1,0:T(8,128)(2,1)S(1)}, u32[]{:S(2)}, u32[]{:S(2)}) %collective-permute-start.8) | collective-permute-done | bytes 548896 | tf_op jit(solution)/shard_map/ppermute | solution.py:303
  60.7 7.9 %collective-permute-done.9.recv = bf16[1120,128]{1,0:T(8,128)(2,1)S(1)} collective-permute-done((bf16[1120,128]{1,0:T(8,128)(2,1)S(1)}, bf16[1120,128]{1,0:T(8,128)(2,1)S(1)}, u32[]{:S(2)}, u32[]{:S(2)}) %collective-permute-start.9) | collective-permute-done | bytes 286752 | tf_op jit(solution)/shard_map/ppermute | solution.py:303
  71.3 2.9 %collective-permute-done.10.recv = bf16[608,128]{1,0:T(8,128)(2,1)S(1)} collective-permute-done((bf16[608,128]{1,0:T(8,128)(2,1)S(1)}, bf16[608,128]{1,0:T(8,128)(2,1)S(1)}, u32[]{:S(2)}, u32[]{:S(2)}) %collective-permute-start.10) | collective-permute-done | bytes 155680 | tf_op jit(solution)/shard_map/ppermute | solution.py:303
  74.4 1.7 %collective-permute-start.11 = (bf16[352,128]{1,0:T(8,128)(2,1)S(1)}, bf16[352,128]{1,0:T(8,128)(2,1)S(1)}, u32[]{:S(2)}, u32[]{:S(2)}) collective-permute-start(bf16[352,128]{1,0:T(8,128)(2,1)S(1)} %get-tuple-element.56), channel_id=1, source_target_pairs={{0,16},{2,18},{4,20},{6,22},{8,24},{10,26},{12,28},{14,30},{16,0},... | collective-permute-start | bytes 270344 | tf_op jit(solution)/shard_map/ppermute | solution.py:303
  76.3 2.3 %collective-permute-start.19 = (bf16[352,128]{1,0:T(8,128)(2,1)S(1)}, bf16[352,128]{1,0:T(8,128)(2,1)S(1)}, u32[]{:S(2)}, u32[]{:S(2)}) collective-permute-start(bf16[352,128]{1,0:T(8,128)(2,1)S(1)} %get-tuple-element.64), channel_id=1, source_target_pairs={{0,16},{2,18},{4,20},{6,22},{8,24},{10,26},{12,28},{14,30},{16,0},... | collective-permute-start | bytes 270344 | tf_op jit(solution)/shard_map/ppermute | solution.py:303
  78.5 5.3 %collective-permute-done.11.recv = bf16[352,128]{1,0:T(8,128)(2,1)S(1)} collective-permute-done((bf16[352,128]{1,0:T(8,128)(2,1)S(1)}, bf16[352,128]{1,0:T(8,128)(2,1)S(1)}, u32[]{:S(2)}, u32[]{:S(2)}) %collective-permute-start.11) | collective-permute-done | bytes 90144 | tf_op jit(solution)/shard_map/ppermute | solution.py:303
  85.5 1.8 %collective-permute-start.20 = (bf16[8,4096]{1,0:T(8,128)(2,1)S(1)}, bf16[8,4096]{1,0:T(8,128)(2,1)S(1)}, u32[]{:S(2)}, u32[]{:S(2)}) collective-permute-start(bf16[8,4096]{1,0:T(8,128)(2,1)S(1)} %reshape.118), channel_id=1, source_target_pairs={{0,16},{2,18},{4,20},{6,22},{8,24},{10,26},{12,28},{14,30},{16,0},... | collective-permute-start | bytes 196616 | tf_op jit(solution)/shard_map/ppermute | solution.py:303
  87.3 2.4 %collective-permute-done.12 = bf16[8,4096]{1,0:T(8,128)(2,1)S(1)} collective-permute-done((bf16[8,4096]{1,0:T(8,128)(2,1)S(1)}, bf16[8,4096]{1,0:T(8,128)(2,1)S(1)}, u32[]{:S(2)}, u32[]{:S(2)}) %collective-permute-start.12) | collective-permute-done | bytes 65568 | tf_op jit(solution)/shard_map/ppermute | solution.py:303
  91.9 3.1 %collective-permute-done.13 = bf16[16,4096]{1,0:T(8,128)(2,1)S(1)} collective-permute-done((bf16[16,4096]{1,0:T(8,128)(2,1)S(1)}, bf16[16,4096]{1,0:T(8,128)(2,1)S(1)}, u32[]{:S(2)}, u32[]{:S(2)}) %collective-permute-start.13) | collective-permute-done | bytes 131104 | tf_op jit(solution)/shard_map/ppermute | solution.py:303
  95.0 1.4 %collective-permute-start.14 = (bf16[32,4096]{1,0:T(8,128)(2,1)S(1)}, bf16[32,4096]{1,0:T(8,128)(2,1)S(1)}, u32[]{:S(2)}, u32[]{:S(2)}) collective-permute-start(bf16[32,4096]{1,0:T(8,128)(2,1)S(1)} %pad_maximum_fusion.6), channel_id=1, source_target_pairs={{0,4},{2,6},{4,0},{6,2},{8,12},{10,14},{12,8},{14,10},{16,20},{18,... | collective-permute-start | bytes 786440 | tf_op jit(solution)/shard_map/ppermute | solution.py:303
  98.5 3.0 %collective-permute-done.14 = bf16[32,4096]{1,0:T(8,128)(2,1)S(1)} collective-permute-done((bf16[32,4096]{1,0:T(8,128)(2,1)S(1)}, bf16[32,4096]{1,0:T(8,128)(2,1)S(1)}, u32[]{:S(2)}, u32[]{:S(2)}) %collective-permute-start.14) | collective-permute-done | bytes 262176 | tf_op jit(solution)/shard_map/ppermute | solution.py:303
  101.6 2.0 %collective-permute-done.22 = bf16[32,4096]{1,0:T(8,128)(2,1)S(1)} collective-permute-done((bf16[32,4096]{1,0:T(8,128)(2,1)S(1)}, bf16[32,4096]{1,0:T(8,128)(2,1)S(1)}, u32[]{:S(2)}, u32[]{:S(2)}) %collective-permute-start.22) | collective-permute-done | bytes 262176 | tf_op jit(solution)/shard_map/ppermute | solution.py:303
  103.8 1.7 %collective-permute-done.23 = bf16[64,4096]{1,0:T(8,128)(2,1)S(1)} collective-permute-done((bf16[64,4096]{1,0:T(8,128)(2,1)S(1)}, bf16[64,4096]{1,0:T(8,128)(2,1)S(1)}, u32[]{:S(2)}, u32[]{:S(2)}) %collective-permute-start.23) | collective-permute-done | bytes 524320 | tf_op jit(solution)/shard_map/ppermute | solution.py:303
  107.6 1.6 %collective-permute-start.24 = (bf16[128,512]{1,0:T(8,128)(2,1)S(1)}, bf16[128,512]{1,0:T(8,128)(2,1)S(1)}, u32[]{:S(2)}, u32[]{:S(2)}) collective-permute-start(bf16[128,512]{1,0:T(8,128)(2,1)S(1)} %bitcast.27), channel_id=1, source_target_pairs={{0,1},{1,0},{2,3},{3,2},{4,5},{5,4},{6,7},{7,6},{8,9},{9,8},{10,11... | collective-permute-start | bytes 393224 | tf_op jit(solution)/shard_map/ppermute | solution.py:369
  109.7 3.3 %collective-permute-done.24 = bf16[128,512]{1,0:T(8,128)(2,1)S(1)} collective-permute-done((bf16[128,512]{1,0:T(8,128)(2,1)S(1)}, bf16[128,512]{1,0:T(8,128)(2,1)S(1)}, u32[]{:S(2)}, u32[]{:S(2)}) %collective-permute-start.24) | collective-permute-done | bytes 131104 | tf_op jit(solution)/shard_map/ppermute | solution.py:369
  (83 shorter events, 23.4 us)
Async XLA Ops:
  0.9 7.9 %collective-permute-start = (bf16[8,32,128]{2,1,0:T(8,128)(2,1)S(1)}, bf16[8,32,128]{2,1,0:T(8,128)(2,1)S(1)}, u32[]{:S(2)}, u32[]{:S(2)}) collective-permute-start(bf16[8,32,128]{2,1,0:T(8,128)(2,1)S(1)} %get-tuple-element.66), channel_id=1, source_target_pairs={{0,16},{2,18},{4,20},{6,22},{8,24},{10,26},{12,28},{14,30},{16,0},... | collective-permute-start | bytes 196616 | tf_op jit(solution)/shard_map/ppermute | solution.py:303
  5.0 6.5 %collective-permute-start.1 = (bf16[8,32,128]{2,1,0:T(8,128)(2,1)S(1)}, bf16[8,32,128]{2,1,0:T(8,128)(2,1)S(1)}, u32[]{:S(2)}, u32[]{:S(2)}) collective-permute-start(bf16[8,32,128]{2,1,0:T(8,128)(2,1)S(1)} %get-tuple-element.65), channel_id=1, source_target_pairs={{0,16},{2,18},{4,20},{6,22},{8,24},{10,26},{12,28},{14,30},{16,0},... | collective-permute-start | bytes 196616 | tf_op jit(solution)/shard_map/ppermute | solution.py:303
  11.5 5.0 %collective-permute-start.2 = (bf16[16,32,128]{2,1,0:T(8,128)(2,1)S(1)}, bf16[16,32,128]{2,1,0:T(8,128)(2,1)S(1)}, u32[]{:S(2)}, u32[]{:S(2)}) collective-permute-start(bf16[16,32,128]{2,1,0:T(8,128)(2,1)S(1)} %pad_maximum_fusion.8), channel_id=1, source_target_pairs={{0,8},{2,10},{4,12},{6,14},{8,0},{10,2},{12,4},{14,6},{16,24},{18,... | collective-permute-start | bytes 393224 | tf_op jit(solution)/shard_map/ppermute | solution.py:303
  12.1 6.5 %collective-permute-start.4 = (bf16[16,32,128]{2,1,0:T(8,128)(2,1)S(1)}, bf16[16,32,128]{2,1,0:T(8,128)(2,1)S(1)}, u32[]{:S(2)}, u32[]{:S(2)}) collective-permute-start(bf16[16,32,128]{2,1,0:T(8,128)(2,1)S(1)} %pad_maximum_fusion.9), channel_id=1, source_target_pairs={{0,4},{2,6},{4,0},{6,2},{8,12},{10,14},{12,8},{14,10},{16,20},{18,... | collective-permute-start | bytes 393224 | tf_op jit(solution)/shard_map/ppermute | solution.py:303
  16.6 7.5 %collective-permute-start.3 = (bf16[32,32,128]{2,1,0:T(8,128)(2,1)S(1)}, bf16[32,32,128]{2,1,0:T(8,128)(2,1)S(1)}, u32[]{:S(2)}, u32[]{:S(2)}) collective-permute-start(bf16[32,32,128]{2,1,0:T(8,128)(2,1)S(1)} %pad_maximum_fusion.4), channel_id=1, source_target_pairs={{0,4},{2,6},{4,0},{6,2},{8,12},{10,14},{12,8},{14,10},{16,20},{18,... | collective-permute-start | bytes 786440 | tf_op jit(solution)/shard_map/ppermute | solution.py:303
  18.6 7.0 %collective-permute-start.5 = (bf16[32,32,128]{2,1,0:T(8,128)(2,1)S(1)}, bf16[32,32,128]{2,1,0:T(8,128)(2,1)S(1)}, u32[]{:S(2)}, u32[]{:S(2)}) collective-permute-start(bf16[32,32,128]{2,1,0:T(8,128)(2,1)S(1)} %pad_maximum_fusion.5), channel_id=1, source_target_pairs={{0,8},{2,10},{4,12},{6,14},{8,0},{10,2},{12,4},{14,6},{16,24},{18,... | collective-permute-start | bytes 786440 | tf_op jit(solution)/shard_map/ppermute | solution.py:303
  25.6 2.0 %collective-permute-start.6 = (bf16[64,32,128]{2,1,0:T(8,128)(2,1)S(1)}, bf16[64,32,128]{2,1,0:T(8,128)(2,1)S(1)}, u32[]{:S(2)}, u32[]{:S(2)}) collective-permute-start(bf16[64,32,128]{2,1,0:T(8,128)(2,1)S(1)} %pad_maximum_fusion.refs_0_), channel_id=1, source_target_pairs={{0,2},{2,0},{4,6},{6,4},{8,10},{10,8},{12,14},{14,12},{16,18},{18,... | collective-permute-start | bytes 1572872 | tf_op jit(solution)/shard_map/ppermute | solution.py:303
  25.8 2.6 %collective-permute-start.7 = (bf16[64,32,128]{2,1,0:T(8,128)(2,1)S(1)}, bf16[64,32,128]{2,1,0:T(8,128)(2,1)S(1)}, u32[]{:S(2)}, u32[]{:S(2)}) collective-permute-start(bf16[64,32,128]{2,1,0:T(8,128)(2,1)S(1)} %pad_maximum_fusion.1.refs_2_), channel_id=1, source_target_pairs={{0,2},{2,0},{4,6},{6,4},{8,10},{10,8},{12,14},{14,12},{16,18},{18,... | collective-permute-start | bytes 1572872 | tf_op jit(solution)/shard_map/ppermute | solution.py:303
  57.2 2.0 %collective-permute-start.8 = (bf16[2144,128]{1,0:T(8,128)(2,1)S(1)}, bf16[2144,128]{1,0:T(8,128)(2,1)S(1)}, u32[]{:S(2)}, u32[]{:S(2)}) collective-permute-start(bf16[2144,128]{1,0:T(8,128)(2,1)S(1)} %get-tuple-element.50), channel_id=1, source_target_pairs={{0,2},{2,0},{4,6},{6,4},{8,10},{10,8},{12,14},{14,12},{16,18},{18,... | collective-permute-start | bytes 1646600 | tf_op jit(solution)/shard_map/ppermute | solution.py:303
  57.3 2.7 %collective-permute-start.16 = (bf16[2144,128]{1,0:T(8,128)(2,1)S(1)}, bf16[2144,128]{1,0:T(8,128)(2,1)S(1)}, u32[]{:S(2)}, u32[]{:S(2)}) collective-permute-start(bf16[2144,128]{1,0:T(8,128)(2,1)S(1)} %get-tuple-element.58), channel_id=1, source_target_pairs={{0,2},{2,0},{4,6},{6,4},{8,10},{10,8},{12,14},{14,12},{16,18},{18,... | collective-permute-start | bytes 1646600 | tf_op jit(solution)/shard_map/ppermute | solution.py:303
  59.7 8.9 %collective-permute-start.9 = (bf16[1120,128]{1,0:T(8,128)(2,1)S(1)}, bf16[1120,128]{1,0:T(8,128)(2,1)S(1)}, u32[]{:S(2)}, u32[]{:S(2)}) collective-permute-start(bf16[1120,128]{1,0:T(8,128)(2,1)S(1)} %get-tuple-element.52), channel_id=1, source_target_pairs={{0,4},{2,6},{4,0},{6,2},{8,12},{10,14},{12,8},{14,10},{16,20},{18,... | collective-permute-start | bytes 860168 | tf_op jit(solution)/shard_map/ppermute | solution.py:303
  60.5 9.4 %collective-permute-start.17 = (bf16[1120,128]{1,0:T(8,128)(2,1)S(1)}, bf16[1120,128]{1,0:T(8,128)(2,1)S(1)}, u32[]{:S(2)}, u32[]{:S(2)}) collective-permute-start(bf16[1120,128]{1,0:T(8,128)(2,1)S(1)} %get-tuple-element.60), channel_id=1, source_target_pairs={{0,8},{2,10},{4,12},{6,14},{8,0},{10,2},{12,4},{14,6},{16,24},{18,... | collective-permute-start | bytes 860168 | tf_op jit(solution)/shard_map/ppermute | solution.py:303
  68.9 5.3 %collective-permute-start.10 = (bf16[608,128]{1,0:T(8,128)(2,1)S(1)}, bf16[608,128]{1,0:T(8,128)(2,1)S(1)}, u32[]{:S(2)}, u32[]{:S(2)}) collective-permute-start(bf16[608,128]{1,0:T(8,128)(2,1)S(1)} %get-tuple-element.54), channel_id=1, source_target_pairs={{0,8},{2,10},{4,12},{6,14},{8,0},{10,2},{12,4},{14,6},{16,24},{18,... | collective-permute-start | bytes 466952 | tf_op jit(solution)/shard_map/ppermute | solution.py:303
  70.1 5.9 %collective-permute-start.18 = (bf16[608,128]{1,0:T(8,128)(2,1)S(1)}, bf16[608,128]{1,0:T(8,128)(2,1)S(1)}, u32[]{:S(2)}, u32[]{:S(2)}) collective-permute-start(bf16[608,128]{1,0:T(8,128)(2,1)S(1)} %get-tuple-element.62), channel_id=1, source_target_pairs={{0,4},{2,6},{4,0},{6,2},{8,12},{10,14},{12,8},{14,10},{16,20},{18,... | collective-permute-start | bytes 466952 | tf_op jit(solution)/shard_map/ppermute | solution.py:303
  74.4 9.5 %collective-permute-start.11 = (bf16[352,128]{1,0:T(8,128)(2,1)S(1)}, bf16[352,128]{1,0:T(8,128)(2,1)S(1)}, u32[]{:S(2)}, u32[]{:S(2)}) collective-permute-start(bf16[352,128]{1,0:T(8,128)(2,1)S(1)} %get-tuple-element.56), channel_id=1, source_target_pairs={{0,16},{2,18},{4,20},{6,22},{8,24},{10,26},{12,28},{14,30},{16,0},... | collective-permute-start | bytes 270344 | tf_op jit(solution)/shard_map/ppermute | solution.py:303
  76.3 9.1 %collective-permute-start.19 = (bf16[352,128]{1,0:T(8,128)(2,1)S(1)}, bf16[352,128]{1,0:T(8,128)(2,1)S(1)}, u32[]{:S(2)}, u32[]{:S(2)}) collective-permute-start(bf16[352,128]{1,0:T(8,128)(2,1)S(1)} %get-tuple-element.64), channel_id=1, source_target_pairs={{0,16},{2,18},{4,20},{6,22},{8,24},{10,26},{12,28},{14,30},{16,0},... | collective-permute-start | bytes 270344 | tf_op jit(solution)/shard_map/ppermute | solution.py:303
  84.0 5.6 %collective-permute-start.12 = (bf16[8,4096]{1,0:T(8,128)(2,1)S(1)}, bf16[8,4096]{1,0:T(8,128)(2,1)S(1)}, u32[]{:S(2)}, u32[]{:S(2)}) collective-permute-start(bf16[8,4096]{1,0:T(8,128)(2,1)S(1)} %reshape.117), channel_id=1, source_target_pairs={{0,16},{2,18},{4,20},{6,22},{8,24},{10,26},{12,28},{14,30},{16,0},... | collective-permute-start | bytes 196616 | tf_op jit(solution)/shard_map/ppermute | solution.py:303
  85.5 5.4 %collective-permute-start.20 = (bf16[8,4096]{1,0:T(8,128)(2,1)S(1)}, bf16[8,4096]{1,0:T(8,128)(2,1)S(1)}, u32[]{:S(2)}, u32[]{:S(2)}) collective-permute-start(bf16[8,4096]{1,0:T(8,128)(2,1)S(1)} %reshape.118), channel_id=1, source_target_pairs={{0,16},{2,18},{4,20},{6,22},{8,24},{10,26},{12,28},{14,30},{16,0},... | collective-permute-start | bytes 196616 | tf_op jit(solution)/shard_map/ppermute | solution.py:303
  89.7 5.3 %collective-permute-start.13 = (bf16[16,4096]{1,0:T(8,128)(2,1)S(1)}, bf16[16,4096]{1,0:T(8,128)(2,1)S(1)}, u32[]{:S(2)}, u32[]{:S(2)}) collective-permute-start(bf16[16,4096]{1,0:T(8,128)(2,1)S(1)} %pad_maximum_fusion.10), channel_id=1, source_target_pairs={{0,8},{2,10},{4,12},{6,14},{8,0},{10,2},{12,4},{14,6},{16,24},{18,... | collective-permute-start | bytes 393224 | tf_op jit(solution)/shard_map/ppermute | solution.py:303
  90.9 6.1 %collective-permute-start.21 = (bf16[16,4096]{1,0:T(8,128)(2,1)S(1)}, bf16[16,4096]{1,0:T(8,128)(2,1)S(1)}, u32[]{:S(2)}, u32[]{:S(2)}) collective-permute-start(bf16[16,4096]{1,0:T(8,128)(2,1)S(1)} %pad_maximum_fusion.11), channel_id=1, source_target_pairs={{0,4},{2,6},{4,0},{6,2},{8,12},{10,14},{12,8},{14,10},{16,20},{18,... | collective-permute-start | bytes 393224 | tf_op jit(solution)/shard_map/ppermute | solution.py:303
  95.0 6.4 %collective-permute-start.14 = (bf16[32,4096]{1,0:T(8,128)(2,1)S(1)}, bf16[32,4096]{1,0:T(8,128)(2,1)S(1)}, u32[]{:S(2)}, u32[]{:S(2)}) collective-permute-start(bf16[32,4096]{1,0:T(8,128)(2,1)S(1)} %pad_maximum_fusion.6), channel_id=1, source_target_pairs={{0,4},{2,6},{4,0},{6,2},{8,12},{10,14},{12,8},{14,10},{16,20},{18,... | collective-permute-start | bytes 786440 | tf_op jit(solution)/shard_map/ppermute | solution.py:303
  97.1 6.4 %collective-permute-start.22 = (bf16[32,4096]{1,0:T(8,128)(2,1)S(1)}, bf16[32,4096]{1,0:T(8,128)(2,1)S(1)}, u32[]{:S(2)}, u32[]{:S(2)}) collective-permute-start(bf16[32,4096]{1,0:T(8,128)(2,1)S(1)} %pad_maximum_fusion.7), channel_id=1, source_target_pairs={{0,8},{2,10},{4,12},{6,14},{8,0},{10,2},{12,4},{14,6},{16,24},{18,... | collective-permute-start | bytes 786440 | tf_op jit(solution)/shard_map/ppermute | solution.py:303
  101.5 2.2 %collective-permute-start.15 = (bf16[64,4096]{1,0:T(8,128)(2,1)S(1)}, bf16[64,4096]{1,0:T(8,128)(2,1)S(1)}, u32[]{:S(2)}, u32[]{:S(2)}) collective-permute-start(bf16[64,4096]{1,0:T(8,128)(2,1)S(1)} %pad_maximum_fusion.2), channel_id=1, source_target_pairs={{0,2},{2,0},{4,6},{6,4},{8,10},{10,8},{12,14},{14,12},{16,18},{18,... | collective-permute-start | bytes 1572872 | tf_op jit(solution)/shard_map/ppermute | solution.py:303
  107.6 5.5 %collective-permute-start.24 = (bf16[128,512]{1,0:T(8,128)(2,1)S(1)}, bf16[128,512]{1,0:T(8,128)(2,1)S(1)}, u32[]{:S(2)}, u32[]{:S(2)}) collective-permute-start(bf16[128,512]{1,0:T(8,128)(2,1)S(1)} %bitcast.27), channel_id=1, source_target_pairs={{0,1},{1,0},{2,3},{3,2},{4,5},{5,4},{6,7},{7,6},{8,9},{9,8},{10,11... | collective-permute-start | bytes 393224 | tf_op jit(solution)/shard_map/ppermute | solution.py:369
  (3 other events, 16.2 us)

commit v3 on v2

--- a/solution.py
+++ b/solution.py
@@ -11,7 +11,7 @@
 CAP = 4
 TILE = 16
 SEGMENTS = 4
-TOGETHER = 2
+TOGETHER = 4
 UNROLL = 4
 LEAD = 2 * TOGETHER
 NONE = -1e30
@@ -108,18 +108,35 @@
     )(me.reshape(1), table, counts.reshape(batch, 1))
 
 
-def split3(x):
+def stat_rows(count, heads):
+    return heads if PLANES * count <= LANES else PLANES * heads
+
+
+def split3(x, count):
     parts = []
     for _ in range(PLANES):
-        part = x.astype(jnp.bfloat16)
+        part = x.astype(jnp.bfloat16).astype(jnp.float32)
         parts.append(part)
-        x = x - part.astype(jnp.float32)
-    return jnp.concatenate(parts, axis=0)
-
-
-def join3(block, heads):
+        x = x - part
+    if PLANES * count > LANES:
+        x = jnp.concatenate(parts, axis=0)
+        if x.shape[1] < LANES:
+            x = jnp.concatenate([x, jnp.zeros((x.shape[0], LANES - x.shape[1]), jnp.float32)], axis=1)
+        return x.astype(jnp.bfloat16)
+    parts = [p[:, :count] for p in parts]
+    rest = LANES - PLANES * count
+    if rest:
+        parts.append(jnp.zeros((x.shape[0], rest), jnp.float32))
+    return jnp.concatenate(parts, axis=1).astype(jnp.bfloat16)
+
+
+def join3(block, count, heads):
     x = block.astype(jnp.float32)
-    return (x[:heads] + x[heads : 2 * heads]) + x[2 * heads :]
+    if PLANES * count > LANES:
+        parts = [x[p * heads : (p + 1) * heads, :count] for p in range(PLANES)]
+    else:
+        parts = [x[:, p * count : (p + 1) * count] for p in range(PLANES)]
+    return (parts[0] + parts[1]) + parts[2]
 
 
 def attention_kernel(nq, kv, group, scale, lst, gp, start, valid, *refs):
@@ -141,9 +158,8 @@
             pltpu.make_async_copy(cache.at[1, at], vbuf.at[at], sems.at[1, g]),
         )
 
-    for g in range(SEGMENTS):
-        for c in copies(g):
-            c.start()
+    for c in copies(0):
+        c.start()
 
     def convert(a, i):
         for u in range(8):
@@ -197,6 +213,9 @@
     for g in range(SEGMENTS):
         for c in copies(g):
             c.wait()
+        if g + 1 < SEGMENTS:
+            for c in copies(g + 1):
+                c.start()
         end = start[0, g + 1]
         if g == SEGMENTS - 1:
             end = end + (3 * TOGETHER - 1)
@@ -219,13 +238,13 @@
             return jnp.where(lane == s, top + jnp.log2(total), stats)
 
         stats = lax.fori_loop(0, per, finish, jnp.full((heads, LANES), NONE, jnp.float32), unroll=UNROLL)
-        outs[a][per * heads :, :] = split3(stats)
+        outs[a][per * heads :, :] = split3(stats, per)
 
 
 def merge_kernel(per, heads, keep, recv, *outs):
     rows = per * heads
-    la = join3(keep[rows:, :], heads)
-    lb = join3(recv[rows:, :], heads)
+    la = join3(keep[rows:, :], per, heads)
+    lb = join3(recv[rows:, :], per, heads)
     diff = la - lb
     weight = 1.0 / (1.0 + jnp.exp2(-diff))
     each = per // len(outs)
@@ -239,15 +258,14 @@
     if len(outs) > 1:
         stats = jnp.maximum(la, lb) + jnp.log2(1.0 + jnp.exp2(-jnp.abs(diff)))
         for i, out in enumerate(outs):
-            part = stats if i == 0 else jnp.concatenate([stats[:, i * each :], stats[:, : i * each]], axis=1)
-            out[each * heads :, :] = split3(part)
+            out[each * heads :, :] = split3(stats[:, i * each : (i + 1) * each], each)
 
 
 def merge(keep, recv, per, heads, last):
     if last:
         shapes = [jax.ShapeDtypeStruct((per * heads, LANES), jnp.bfloat16)]
     else:
-        shapes = [jax.ShapeDtypeStruct(((per // 2 + PLANES) * heads, LANES), jnp.bfloat16)] * 2
+        shapes = [jax.ShapeDtypeStruct((per // 2 * heads + stat_rows(per // 2, heads), LANES), jnp.bfloat16)] * 2
     return call(
         functools.partial(merge_kernel, per, heads),
         shapes,
@@ -275,7 +293,7 @@
     scratch += [pltpu.VMEM((TOGETHER, kv, TILE * group, page_len), jnp.bfloat16)]
     return call(
         functools.partial(attention_kernel, nq, kv, group, math.log2(math.e) / math.sqrt(head_dim)),
-        [jax.ShapeDtypeStruct(((per + PLANES) * heads, LANES), jnp.bfloat16)] * nq,
+        [jax.ShapeDtypeStruct((per * heads + stat_rows(per, heads), LANES), jnp.bfloat16)] * nq,
         [SMEM] * 4 + [VMEM] * nq + [ANY],
         [VMEM] * nq,
         4 * pairs * heads * page_len * head_dim,

time: 115 us -> 111 us (0.965); the launches traced: 114 us -> 111 us
  Pallas kernels: 33.1 us -> 31.5 us
    pallas_call x1, Pallas kernels: 28.8 us -> 26.7 us  [attend(): call(functools.partial(attention_kernel, nq, kv, group, math.log2(math.e)...]
  transfers between devices with their start and end apart: 25 -> 25, of which waited for: 18 -> 19; matrix products, arithmetic and copies ran while one was open for 5% -> 5% of each run, Pallas kernels for 4% -> 4%
where the time goes in v3:
time: 111 us
  waiting for transfers between devices  46.6 us (42%)
  Pallas kernels  31.5 us (28%)
  starting transfers between devices  23.6 us (21%)
  local copies, waits for them, and re-layouts  6.08 us (5%)
  other arithmetic  1.72 us (2%)
  matrix products  1.24 us (1%)
    ppermute x24, waiting for transfers between devices, swap(): return lax.ppermute(x, 'seq', [(i, i ^ bit) for i in range(n)])  43.3 us
    pallas_call x1, Pallas kernels, attend(): call(functools.partial(attention_kernel, nq, kv, group, math.log2(math.e)...  26.7 us
    ppermute x24, starting transfers between devices, swap(): return lax.ppermute(x, 'seq', [(i, i ^ bit) for i in range(n)])  22.1 us
    ppermute x1, waiting for transfers between devices, shards(): took = lax.ppermute(give, 'head', [(i, i ^ step) for i in range(nh)])  3.35 us
    pallas_call x8, Pallas kernels, merge(): call(functools.partial(merge_kernel, per, heads), shapes, [VMEM] * 2, [VM...  2.58 us
  transfers between devices with their start and end apart: 25, of which 19 were waited for; matrix products, arithmetic and copies ran while one was open for 5% of the time, Pallas kernels for 4%

profile of v3, /device:TPU:0, one launch (start us, length us, event | category | flops | bytes accessed | tf_op | source)
XLA Modules:
  0.0 111.1 jit_solution(9068197944002035039)
XLA Ops:
  0.9 4.1 %collective-permute-start = (bf16[8,32,128]{2,1,0:T(8,128)(2,1)S(1)}, bf16[8,32,128]{2,1,0:T(8,128)(2,1)S(1)}, u32[]{:S(2)}, u32[]{:S(2)}) collective-permute-start(bf16[8,32,128]{2,1,0:T(8,128)(2,1)S(1)} %get-tuple-element.66), channel_id=1, source_target_pairs={{0,16},{2,18},{4,20},{6,22},{8,24},{10,26},{12,28},{14,30},{16,0},... | collective-permute-start | bytes 196616 | tf_op jit(solution)/shard_map/ppermute | solution.py:321
  8.8 2.7 %collective-permute-done.1 = bf16[8,32,128]{2,1,0:T(8,128)(2,1)S(1)} collective-permute-done((bf16[8,32,128]{2,1,0:T(8,128)(2,1)S(1)}, bf16[8,32,128]{2,1,0:T(8,128)(2,1)S(1)}, u32[]{:S(2)}, u32[]{:S(2)}) %collective-permute-start.1) | collective-permute-done | bytes 65568 | tf_op jit(solution)/shard_map/ppermute | solution.py:321
  12.1 1.6 %collective-permute-start.4 = (bf16[16,32,128]{2,1,0:T(8,128)(2,1)S(1)}, bf16[16,32,128]{2,1,0:T(8,128)(2,1)S(1)}, u32[]{:S(2)}, u32[]{:S(2)}) collective-permute-start(bf16[16,32,128]{2,1,0:T(8,128)(2,1)S(1)} %pad_maximum_fusion.9), channel_id=1, source_target_pairs={{0,4},{2,6},{4,0},{6,2},{8,12},{10,14},{12,8},{14,10},{16,20},{18,... | collective-permute-start | bytes 393224 | tf_op jit(solution)/shard_map/ppermute | solution.py:321
  13.7 2.8 %collective-permute-done.2 = bf16[16,32,128]{2,1,0:T(8,128)(2,1)S(1)} collective-permute-done((bf16[16,32,128]{2,1,0:T(8,128)(2,1)S(1)}, bf16[16,32,128]{2,1,0:T(8,128)(2,1)S(1)}, u32[]{:S(2)}, u32[]{:S(2)}) %collective-permute-start.2) | collective-permute-done | bytes 131104 | tf_op jit(solution)/shard_map/ppermute | solution.py:321
  16.6 2.0 %collective-permute-start.3 = (bf16[32,32,128]{2,1,0:T(8,128)(2,1)S(1)}, bf16[32,32,128]{2,1,0:T(8,128)(2,1)S(1)}, u32[]{:S(2)}, u32[]{:S(2)}) collective-permute-start(bf16[32,32,128]{2,1,0:T(8,128)(2,1)S(1)} %pad_maximum_fusion.4), channel_id=1, source_target_pairs={{0,4},{2,6},{4,0},{6,2},{8,12},{10,14},{12,8},{14,10},{16,20},{18,... | collective-permute-start | bytes 786440 | tf_op jit(solution)/shard_map/ppermute | solution.py:321
  19.4 2.1 %lists.1 = (s32[1,2432]{1,0:T(1,128)S(1)}, s32[1,152]{1,0:T(1,128)S(1)}, s32[1,128]{1,0:T(1,128)S(1)}, s32[1,256]{1,0:T(1,128)S(1)}) custom-call(s32[1]{0:T(128)} %bitcast.2.me_ref, s32[256,64]{1,0:T(8,128)S(1)} %bitcast.25, s32[256,1]{1,0:T(8,128)S(1)} %copy.10.count_ref), custom_call_target="tpu_custom_call" | custom-call | flops 100000000 | bytes 1000000 | tf_op jit(solution)/shard_map/lists/pallas_call | solution.py:99
  21.5 2.5 %collective-permute-done.3 = bf16[32,32,128]{2,1,0:T(8,128)(2,1)S(1)} collective-permute-done((bf16[32,32,128]{2,1,0:T(8,128)(2,1)S(1)}, bf16[32,32,128]{2,1,0:T(8,128)(2,1)S(1)}, u32[]{:S(2)}, u32[]{:S(2)}) %collective-permute-start.3) | collective-permute-done | bytes 262176 | tf_op jit(solution)/shard_map/ppermute | solution.py:321
  24.0 1.6 %collective-permute-done.5 = bf16[32,32,128]{2,1,0:T(8,128)(2,1)S(1)} collective-permute-done((bf16[32,32,128]{2,1,0:T(8,128)(2,1)S(1)}, bf16[32,32,128]{2,1,0:T(8,128)(2,1)S(1)}, u32[]{:S(2)}, u32[]{:S(2)}) %collective-permute-start.5) | collective-permute-done | bytes 262176 | tf_op jit(solution)/shard_map/ppermute | solution.py:321
  28.4 26.7 %attention.1 = (bf16[2144,128]{1,0:T(8,128)(2,1)S(1)}, bf16[2144,128]{1,0:T(8,128)(2,1)S(1)}, bf16[2144,128]{1,0:T(8,128)(2,1)S(1)}, bf16[2144,128]{1,0:T(8,128)(2,1)S(1)}) custom-call(s32[1,2432]{1,0:T(1,128)S(1)} %get-tuple-element.43.lst, s32[1,152]{1,0:T(1,128)S(1)} %get-tuple-element.44.gp, s32[1,128]{1,0:T(1,128)S(1)} %get-tuple-element.45.start, ...), custom_call_target="tpu_custom_call" | custom-call | flops 2147483648 | bytes 16777216 | tf_op jit(solution)/shard_map/attention/pallas_call | solution.py:294
  55.7 1.4 %collective-permute-done.8.recv = bf16[2144,128]{1,0:T(8,128)(2,1)S(1)} collective-permute-done((bf16[2144,128]{1,0:T(8,128)(2,1)S(1)}, bf16[2144,128]{1,0:T(8,128)(2,1)S(1)}, u32[]{:S(2)}, u32[]{:S(2)}) %collective-permute-start.8) | collective-permute-done | bytes 548896 | tf_op jit(solution)/shard_map/ppermute | solution.py:321
  58.6 1.4 %collective-permute-start.17 = (bf16[1056,128]{1,0:T(8,128)(2,1)S(1)}, bf16[1056,128]{1,0:T(8,128)(2,1)S(1)}, u32[]{:S(2)}, u32[]{:S(2)}) collective-permute-start(bf16[1056,128]{1,0:T(8,128)(2,1)S(1)} %get-tuple-element.60), channel_id=1, source_target_pairs={{0,8},{2,10},{4,12},{6,14},{8,0},{10,2},{12,4},{14,6},{16,24},{18,... | collective-permute-start | bytes 811016 | tf_op jit(solution)/shard_map/ppermute | solution.py:321
  60.0 6.2 %collective-permute-done.9.recv = bf16[1056,128]{1,0:T(8,128)(2,1)S(1)} collective-permute-done((bf16[1056,128]{1,0:T(8,128)(2,1)S(1)}, bf16[1056,128]{1,0:T(8,128)(2,1)S(1)}, u32[]{:S(2)}, u32[]{:S(2)}) %collective-permute-start.9) | collective-permute-done | bytes 270368 | tf_op jit(solution)/shard_map/ppermute | solution.py:321
  69.5 2.2 %collective-permute-done.10.recv = bf16[544,128]{1,0:T(8,128)(2,1)S(1)} collective-permute-done((bf16[544,128]{1,0:T(8,128)(2,1)S(1)}, bf16[544,128]{1,0:T(8,128)(2,1)S(1)}, u32[]{:S(2)}, u32[]{:S(2)}) %collective-permute-start.10) | collective-permute-done | bytes 139296 | tf_op jit(solution)/shard_map/ppermute | solution.py:321
  72.0 2.7 %collective-permute-start.11 = (bf16[288,128]{1,0:T(8,128)(2,1)S(1)}, bf16[288,128]{1,0:T(8,128)(2,1)S(1)}, u32[]{:S(2)}, u32[]{:S(2)}) collective-permute-start(bf16[288,128]{1,0:T(8,128)(2,1)S(1)} %get-tuple-element.56), channel_id=1, source_target_pairs={{0,16},{2,18},{4,20},{6,22},{8,24},{10,26},{12,28},{14,30},{16,0},... | collective-permute-start | bytes 221192 | tf_op jit(solution)/shard_map/ppermute | solution.py:321
  76.3 4.7 %collective-permute-done.11.recv = bf16[288,128]{1,0:T(8,128)(2,1)S(1)} collective-permute-done((bf16[288,128]{1,0:T(8,128)(2,1)S(1)}, bf16[288,128]{1,0:T(8,128)(2,1)S(1)}, u32[]{:S(2)}, u32[]{:S(2)}) %collective-permute-start.11) | collective-permute-done | bytes 73760 | tf_op jit(solution)/shard_map/ppermute | solution.py:321
  82.8 1.8 %collective-permute-start.20 = (bf16[8,4096]{1,0:T(8,128)(2,1)S(1)}, bf16[8,4096]{1,0:T(8,128)(2,1)S(1)}, u32[]{:S(2)}, u32[]{:S(2)}) collective-permute-start(bf16[8,4096]{1,0:T(8,128)(2,1)S(1)} %reshape.118), channel_id=1, source_target_pairs={{0,16},{2,18},{4,20},{6,22},{8,24},{10,26},{12,28},{14,30},{16,0},... | collective-permute-start | bytes 196616 | tf_op jit(solution)/shard_map/ppermute | solution.py:321
  84.6 2.6 %collective-permute-done.12 = bf16[8,4096]{1,0:T(8,128)(2,1)S(1)} collective-permute-done((bf16[8,4096]{1,0:T(8,128)(2,1)S(1)}, bf16[8,4096]{1,0:T(8,128)(2,1)S(1)}, u32[]{:S(2)}, u32[]{:S(2)}) %collective-permute-start.12) | collective-permute-done | bytes 65568 | tf_op jit(solution)/shard_map/ppermute | solution.py:321
  89.1 3.1 %collective-permute-done.13 = bf16[16,4096]{1,0:T(8,128)(2,1)S(1)} collective-permute-done((bf16[16,4096]{1,0:T(8,128)(2,1)S(1)}, bf16[16,4096]{1,0:T(8,128)(2,1)S(1)}, u32[]{:S(2)}, u32[]{:S(2)}) %collective-permute-start.13) | collective-permute-done | bytes 131104 | tf_op jit(solution)/shard_map/ppermute | solution.py:321
  92.3 2.1 %collective-permute-done.21 = bf16[16,4096]{1,0:T(8,128)(2,1)S(1)} collective-permute-done((bf16[16,4096]{1,0:T(8,128)(2,1)S(1)}, bf16[16,4096]{1,0:T(8,128)(2,1)S(1)}, u32[]{:S(2)}, u32[]{:S(2)}) %collective-permute-start.21) | collective-permute-done | bytes 131104 | tf_op jit(solution)/shard_map/ppermute | solution.py:321
  95.1 3.5 %collective-permute-done.14 = bf16[32,4096]{1,0:T(8,128)(2,1)S(1)} collective-permute-done((bf16[32,4096]{1,0:T(8,128)(2,1)S(1)}, bf16[32,4096]{1,0:T(8,128)(2,1)S(1)}, u32[]{:S(2)}, u32[]{:S(2)}) %collective-permute-start.14) | collective-permute-done | bytes 262176 | tf_op jit(solution)/shard_map/ppermute | solution.py:321
  98.8 2.1 %collective-permute-done.22 = bf16[32,4096]{1,0:T(8,128)(2,1)S(1)} collective-permute-done((bf16[32,4096]{1,0:T(8,128)(2,1)S(1)}, bf16[32,4096]{1,0:T(8,128)(2,1)S(1)}, u32[]{:S(2)}, u32[]{:S(2)}) %collective-permute-start.22) | collective-permute-done | bytes 262176 | tf_op jit(solution)/shard_map/ppermute | solution.py:321
  101.2 1.7 %collective-permute-done.23 = bf16[64,4096]{1,0:T(8,128)(2,1)S(1)} collective-permute-done((bf16[64,4096]{1,0:T(8,128)(2,1)S(1)}, bf16[64,4096]{1,0:T(8,128)(2,1)S(1)}, u32[]{:S(2)}, u32[]{:S(2)}) %collective-permute-start.23) | collective-permute-done | bytes 524320 | tf_op jit(solution)/shard_map/ppermute | solution.py:321
  104.9 1.6 %collective-permute-start.24 = (bf16[128,512]{1,0:T(8,128)(2,1)S(1)}, bf16[128,512]{1,0:T(8,128)(2,1)S(1)}, u32[]{:S(2)}, u32[]{:S(2)}) collective-permute-start(bf16[128,512]{1,0:T(8,128)(2,1)S(1)} %bitcast.27), channel_id=1, source_target_pairs={{0,1},{1,0},{2,3},{3,2},{4,5},{5,4},{6,7},{7,6},{8,9},{9,8},{10,11... | collective-permute-start | bytes 393224 | tf_op jit(solution)/shard_map/ppermute | solution.py:387
  107.0 3.3 %collective-permute-done.24 = bf16[128,512]{1,0:T(8,128)(2,1)S(1)} collective-permute-done((bf16[128,512]{1,0:T(8,128)(2,1)S(1)}, bf16[128,512]{1,0:T(8,128)(2,1)S(1)}, u32[]{:S(2)}, u32[]{:S(2)}) %collective-permute-start.24) | collective-permute-done | bytes 131104 | tf_op jit(solution)/shard_map/ppermute | solution.py:387
  (83 shorter events, 23.9 us)
Async XLA Ops:
  0.9 7.9 %collective-permute-start = (bf16[8,32,128]{2,1,0:T(8,128)(2,1)S(1)}, bf16[8,32,128]{2,1,0:T(8,128)(2,1)S(1)}, u32[]{:S(2)}, u32[]{:S(2)}) collective-permute-start(bf16[8,32,128]{2,1,0:T(8,128)(2,1)S(1)} %get-tuple-element.66), channel_id=1, source_target_pairs={{0,16},{2,18},{4,20},{6,22},{8,24},{10,26},{12,28},{14,30},{16,0},... | collective-permute-start | bytes 196616 | tf_op jit(solution)/shard_map/ppermute | solution.py:321
  5.0 6.5 %collective-permute-start.1 = (bf16[8,32,128]{2,1,0:T(8,128)(2,1)S(1)}, bf16[8,32,128]{2,1,0:T(8,128)(2,1)S(1)}, u32[]{:S(2)}, u32[]{:S(2)}) collective-permute-start(bf16[8,32,128]{2,1,0:T(8,128)(2,1)S(1)} %get-tuple-element.65), channel_id=1, source_target_pairs={{0,16},{2,18},{4,20},{6,22},{8,24},{10,26},{12,28},{14,30},{16,0},... | collective-permute-start | bytes 196616 | tf_op jit(solution)/shard_map/ppermute | solution.py:321
  11.5 5.0 %collective-permute-start.2 = (bf16[16,32,128]{2,1,0:T(8,128)(2,1)S(1)}, bf16[16,32,128]{2,1,0:T(8,128)(2,1)S(1)}, u32[]{:S(2)}, u32[]{:S(2)}) collective-permute-start(bf16[16,32,128]{2,1,0:T(8,128)(2,1)S(1)} %pad_maximum_fusion.8), channel_id=1, source_target_pairs={{0,8},{2,10},{4,12},{6,14},{8,0},{10,2},{12,4},{14,6},{16,24},{18,... | collective-permute-start | bytes 393224 | tf_op jit(solution)/shard_map/ppermute | solution.py:321
  12.1 6.5 %collective-permute-start.4 = (bf16[16,32,128]{2,1,0:T(8,128)(2,1)S(1)}, bf16[16,32,128]{2,1,0:T(8,128)(2,1)S(1)}, u32[]{:S(2)}, u32[]{:S(2)}) collective-permute-start(bf16[16,32,128]{2,1,0:T(8,128)(2,1)S(1)} %pad_maximum_fusion.9), channel_id=1, source_target_pairs={{0,4},{2,6},{4,0},{6,2},{8,12},{10,14},{12,8},{14,10},{16,20},{18,... | collective-permute-start | bytes 393224 | tf_op jit(solution)/shard_map/ppermute | solution.py:321
  16.6 7.5 %collective-permute-start.3 = (bf16[32,32,128]{2,1,0:T(8,128)(2,1)S(1)}, bf16[32,32,128]{2,1,0:T(8,128)(2,1)S(1)}, u32[]{:S(2)}, u32[]{:S(2)}) collective-permute-start(bf16[32,32,128]{2,1,0:T(8,128)(2,1)S(1)} %pad_maximum_fusion.4), channel_id=1, source_target_pairs={{0,4},{2,6},{4,0},{6,2},{8,12},{10,14},{12,8},{14,10},{16,20},{18,... | collective-permute-start | bytes 786440 | tf_op jit(solution)/shard_map/ppermute | solution.py:321
  18.6 7.0 %collective-permute-start.5 = (bf16[32,32,128]{2,1,0:T(8,128)(2,1)S(1)}, bf16[32,32,128]{2,1,0:T(8,128)(2,1)S(1)}, u32[]{:S(2)}, u32[]{:S(2)}) collective-permute-start(bf16[32,32,128]{2,1,0:T(8,128)(2,1)S(1)} %pad_maximum_fusion.5), channel_id=1, source_target_pairs={{0,8},{2,10},{4,12},{6,14},{8,0},{10,2},{12,4},{14,6},{16,24},{18,... | collective-permute-start | bytes 786440 | tf_op jit(solution)/shard_map/ppermute | solution.py:321
  25.8 2.6 %collective-permute-start.7 = (bf16[64,32,128]{2,1,0:T(8,128)(2,1)S(1)}, bf16[64,32,128]{2,1,0:T(8,128)(2,1)S(1)}, u32[]{:S(2)}, u32[]{:S(2)}) collective-permute-start(bf16[64,32,128]{2,1,0:T(8,128)(2,1)S(1)} %pad_maximum_fusion.1.refs_2_), channel_id=1, source_target_pairs={{0,2},{2,0},{4,6},{6,4},{8,10},{10,8},{12,14},{14,12},{16,18},{18,... | collective-permute-start | bytes 1572872 | tf_op jit(solution)/shard_map/ppermute | solution.py:321
  55.1 2.0 %collective-permute-start.8 = (bf16[2144,128]{1,0:T(8,128)(2,1)S(1)}, bf16[2144,128]{1,0:T(8,128)(2,1)S(1)}, u32[]{:S(2)}, u32[]{:S(2)}) collective-permute-start(bf16[2144,128]{1,0:T(8,128)(2,1)S(1)} %get-tuple-element.50), channel_id=1, source_target_pairs={{0,2},{2,0},{4,6},{6,4},{8,10},{10,8},{12,14},{14,12},{16,18},{18,... | collective-permute-start | bytes 1646600 | tf_op jit(solution)/shard_map/ppermute | solution.py:321
  55.4 2.8 %collective-permute-start.16 = (bf16[2144,128]{1,0:T(8,128)(2,1)S(1)}, bf16[2144,128]{1,0:T(8,128)(2,1)S(1)}, u32[]{:S(2)}, u32[]{:S(2)}) collective-permute-start(bf16[2144,128]{1,0:T(8,128)(2,1)S(1)} %get-tuple-element.58), channel_id=1, source_target_pairs={{0,2},{2,0},{4,6},{6,4},{8,10},{10,8},{12,14},{14,12},{16,18},{18,... | collective-permute-start | bytes 1646600 | tf_op jit(solution)/shard_map/ppermute | solution.py:321
  57.6 8.6 %collective-permute-start.9 = (bf16[1056,128]{1,0:T(8,128)(2,1)S(1)}, bf16[1056,128]{1,0:T(8,128)(2,1)S(1)}, u32[]{:S(2)}, u32[]{:S(2)}) collective-permute-start(bf16[1056,128]{1,0:T(8,128)(2,1)S(1)} %get-tuple-element.52), channel_id=1, source_target_pairs={{0,4},{2,6},{4,0},{6,2},{8,12},{10,14},{12,8},{14,10},{16,20},{18,... | collective-permute-start | bytes 811016 | tf_op jit(solution)/shard_map/ppermute | solution.py:321
  58.6 9.4 %collective-permute-start.17 = (bf16[1056,128]{1,0:T(8,128)(2,1)S(1)}, bf16[1056,128]{1,0:T(8,128)(2,1)S(1)}, u32[]{:S(2)}, u32[]{:S(2)}) collective-permute-start(bf16[1056,128]{1,0:T(8,128)(2,1)S(1)} %get-tuple-element.60), channel_id=1, source_target_pairs={{0,8},{2,10},{4,12},{6,14},{8,0},{10,2},{12,4},{14,6},{16,24},{18,... | collective-permute-start | bytes 811016 | tf_op jit(solution)/shard_map/ppermute | solution.py:321
  66.6 5.1 %collective-permute-start.10 = (bf16[544,128]{1,0:T(8,128)(2,1)S(1)}, bf16[544,128]{1,0:T(8,128)(2,1)S(1)}, u32[]{:S(2)}, u32[]{:S(2)}) collective-permute-start(bf16[544,128]{1,0:T(8,128)(2,1)S(1)} %get-tuple-element.54), channel_id=1, source_target_pairs={{0,8},{2,10},{4,12},{6,14},{8,0},{10,2},{12,4},{14,6},{16,24},{18,... | collective-permute-start | bytes 417800 | tf_op jit(solution)/shard_map/ppermute | solution.py:321
  68.4 6.3 %collective-permute-start.18 = (bf16[544,128]{1,0:T(8,128)(2,1)S(1)}, bf16[544,128]{1,0:T(8,128)(2,1)S(1)}, u32[]{:S(2)}, u32[]{:S(2)}) collective-permute-start(bf16[544,128]{1,0:T(8,128)(2,1)S(1)} %get-tuple-element.62), channel_id=1, source_target_pairs={{0,4},{2,6},{4,0},{6,2},{8,12},{10,14},{12,8},{14,10},{16,20},{18,... | collective-permute-start | bytes 417800 | tf_op jit(solution)/shard_map/ppermute | solution.py:321
  72.0 9.1 %collective-permute-start.11 = (bf16[288,128]{1,0:T(8,128)(2,1)S(1)}, bf16[288,128]{1,0:T(8,128)(2,1)S(1)}, u32[]{:S(2)}, u32[]{:S(2)}) collective-permute-start(bf16[288,128]{1,0:T(8,128)(2,1)S(1)} %get-tuple-element.56), channel_id=1, source_target_pairs={{0,16},{2,18},{4,20},{6,22},{8,24},{10,26},{12,28},{14,30},{16,0},... | collective-permute-start | bytes 221192 | tf_op jit(solution)/shard_map/ppermute | solution.py:321
  75.0 7.5 %collective-permute-start.19 = (bf16[288,128]{1,0:T(8,128)(2,1)S(1)}, bf16[288,128]{1,0:T(8,128)(2,1)S(1)}, u32[]{:S(2)}, u32[]{:S(2)}) collective-permute-start(bf16[288,128]{1,0:T(8,128)(2,1)S(1)} %get-tuple-element.64), channel_id=1, source_target_pairs={{0,16},{2,18},{4,20},{6,22},{8,24},{10,26},{12,28},{14,30},{16,0},... | collective-permute-start | bytes 221192 | tf_op jit(solution)/shard_map/ppermute | solution.py:321
  81.3 5.9 %collective-permute-start.12 = (bf16[8,4096]{1,0:T(8,128)(2,1)S(1)}, bf16[8,4096]{1,0:T(8,128)(2,1)S(1)}, u32[]{:S(2)}, u32[]{:S(2)}) collective-permute-start(bf16[8,4096]{1,0:T(8,128)(2,1)S(1)} %reshape.117), channel_id=1, source_target_pairs={{0,16},{2,18},{4,20},{6,22},{8,24},{10,26},{12,28},{14,30},{16,0},... | collective-permute-start | bytes 196616 | tf_op jit(solution)/shard_map/ppermute | solution.py:321
  82.8 5.2 %collective-permute-start.20 = (bf16[8,4096]{1,0:T(8,128)(2,1)S(1)}, bf16[8,4096]{1,0:T(8,128)(2,1)S(1)}, u32[]{:S(2)}, u32[]{:S(2)}) collective-permute-start(bf16[8,4096]{1,0:T(8,128)(2,1)S(1)} %reshape.118), channel_id=1, source_target_pairs={{0,16},{2,18},{4,20},{6,22},{8,24},{10,26},{12,28},{14,30},{16,0},... | collective-permute-start | bytes 196616 | tf_op jit(solution)/shard_map/ppermute | solution.py:321
  87.2 5.0 %collective-permute-start.13 = (bf16[16,4096]{1,0:T(8,128)(2,1)S(1)}, bf16[16,4096]{1,0:T(8,128)(2,1)S(1)}, u32[]{:S(2)}, u32[]{:S(2)}) collective-permute-start(bf16[16,4096]{1,0:T(8,128)(2,1)S(1)} %pad_maximum_fusion.10), channel_id=1, source_target_pairs={{0,8},{2,10},{4,12},{6,14},{8,0},{10,2},{12,4},{14,6},{16,24},{18,... | collective-permute-start | bytes 393224 | tf_op jit(solution)/shard_map/ppermute | solution.py:321
  88.0 6.4 %collective-permute-start.21 = (bf16[16,4096]{1,0:T(8,128)(2,1)S(1)}, bf16[16,4096]{1,0:T(8,128)(2,1)S(1)}, u32[]{:S(2)}, u32[]{:S(2)}) collective-permute-start(bf16[16,4096]{1,0:T(8,128)(2,1)S(1)} %pad_maximum_fusion.11), channel_id=1, source_target_pairs={{0,4},{2,6},{4,0},{6,2},{8,12},{10,14},{12,8},{14,10},{16,20},{18,... | collective-permute-start | bytes 393224 | tf_op jit(solution)/shard_map/ppermute | solution.py:321
  92.2 6.4 %collective-permute-start.14 = (bf16[32,4096]{1,0:T(8,128)(2,1)S(1)}, bf16[32,4096]{1,0:T(8,128)(2,1)S(1)}, u32[]{:S(2)}, u32[]{:S(2)}) collective-permute-start(bf16[32,4096]{1,0:T(8,128)(2,1)S(1)} %pad_maximum_fusion.6), channel_id=1, source_target_pairs={{0,4},{2,6},{4,0},{6,2},{8,12},{10,14},{12,8},{14,10},{16,20},{18,... | collective-permute-start | bytes 786440 | tf_op jit(solution)/shard_map/ppermute | solution.py:321
  94.5 6.4 %collective-permute-start.22 = (bf16[32,4096]{1,0:T(8,128)(2,1)S(1)}, bf16[32,4096]{1,0:T(8,128)(2,1)S(1)}, u32[]{:S(2)}, u32[]{:S(2)}) collective-permute-start(bf16[32,4096]{1,0:T(8,128)(2,1)S(1)} %pad_maximum_fusion.7), channel_id=1, source_target_pairs={{0,8},{2,10},{4,12},{6,14},{8,0},{10,2},{12,4},{14,6},{16,24},{18,... | collective-permute-start | bytes 786440 | tf_op jit(solution)/shard_map/ppermute | solution.py:321
  98.7 2.4 %collective-permute-start.15 = (bf16[64,4096]{1,0:T(8,128)(2,1)S(1)}, bf16[64,4096]{1,0:T(8,128)(2,1)S(1)}, u32[]{:S(2)}, u32[]{:S(2)}) collective-permute-start(bf16[64,4096]{1,0:T(8,128)(2,1)S(1)} %pad_maximum_fusion.2), channel_id=1, source_target_pairs={{0,2},{2,0},{4,6},{6,4},{8,10},{10,8},{12,14},{14,12},{16,18},{18,... | collective-permute-start | bytes 1572872 | tf_op jit(solution)/shard_map/ppermute | solution.py:321
  100.9 2.0 %collective-permute-start.23 = (bf16[64,4096]{1,0:T(8,128)(2,1)S(1)}, bf16[64,4096]{1,0:T(8,128)(2,1)S(1)}, u32[]{:S(2)}, u32[]{:S(2)}) collective-permute-start(bf16[64,4096]{1,0:T(8,128)(2,1)S(1)} %pad_maximum_fusion.3), channel_id=1, source_target_pairs={{0,2},{2,0},{4,6},{6,4},{8,10},{10,8},{12,14},{14,12},{16,18},{18,... | collective-permute-start | bytes 1572872 | tf_op jit(solution)/shard_map/ppermute | solution.py:321
  104.9 5.5 %collective-permute-start.24 = (bf16[128,512]{1,0:T(8,128)(2,1)S(1)}, bf16[128,512]{1,0:T(8,128)(2,1)S(1)}, u32[]{:S(2)}, u32[]{:S(2)}) collective-permute-start(bf16[128,512]{1,0:T(8,128)(2,1)S(1)} %bitcast.27), channel_id=1, source_target_pairs={{0,1},{1,0},{2,3},{3,2},{4,5},{5,4},{6,7},{7,6},{8,9},{9,8},{10,11... | collective-permute-start | bytes 393224 | tf_op jit(solution)/shard_map/ppermute | solution.py:387
  (3 other events, 16.4 us)

commit v4 on v3

--- a/solution.py
+++ b/solution.py
@@ -241,36 +241,37 @@
         outs[a][per * heads :, :] = split3(stats, per)
 
 
-def merge_kernel(per, heads, keep, recv, *outs):
+def merge_kernel(per, heads, last, keep, recv, *outs):
     rows = per * heads
+    half = per // 2
     la = join3(keep[rows:, :], per, heads)
     lb = join3(recv[rows:, :], per, heads)
+    if last:
+        lb = jnp.concatenate([lb[:, half:], lb[:, :half]], axis=1)
     diff = la - lb
     weight = 1.0 / (1.0 + jnp.exp2(-diff))
     each = per // len(outs)
     for s in range(per):
-        sl = slice(s * heads, (s + 1) * heads)
-        x = keep[sl, :].astype(jnp.float32)
-        y = recv[sl, :].astype(jnp.float32)
+        other = (s + half) % per if last else s
+        x = keep[s * heads : (s + 1) * heads, :].astype(jnp.float32)
+        y = recv[other * heads : (other + 1) * heads, :].astype(jnp.float32)
         z = y + weight[:, s : s + 1] * (x - y)
         at = s % each
         outs[s // each][at * heads : (at + 1) * heads, :] = z.astype(jnp.bfloat16)
-    if len(outs) > 1:
+    if not last:
         stats = jnp.maximum(la, lb) + jnp.log2(1.0 + jnp.exp2(-jnp.abs(diff)))
         for i, out in enumerate(outs):
             out[each * heads :, :] = split3(stats[:, i * each : (i + 1) * each], each)
 
 
-def merge(keep, recv, per, heads, last):
-    if last:
-        shapes = [jax.ShapeDtypeStruct((per * heads, LANES), jnp.bfloat16)]
-    else:
-        shapes = [jax.ShapeDtypeStruct((per // 2 * heads + stat_rows(per // 2, heads), LANES), jnp.bfloat16)] * 2
+def merge(keep, recv, per, heads, pieces, last):
+    each = per // pieces
+    rows = each * heads + (0 if last else stat_rows(each, heads))
     return call(
-        functools.partial(merge_kernel, per, heads),
-        shapes,
+        functools.partial(merge_kernel, per, heads, last),
+        [jax.ShapeDtypeStruct((rows, LANES), jnp.bfloat16)] * pieces,
         [VMEM] * 2,
-        [VMEM] * len(shapes),
+        [VMEM] * pieces,
         keep.size * 8,
         keep.size * 6,
         name="merge",
@@ -356,28 +357,30 @@
     keep = [parts[2 * a] for a in range(halves)]
     send = [parts[2 * a + 1] for a in range(halves)]
     now = per
-    att = [None] * halves
     for at in range(len(bits)):
+        last = at == len(bits) - 1
         took = [swap(send[a], ([bits[0]] + orders[a])[at]) for a in range(halves)]
+        pieces = 2 if at < len(bits) - 2 else 1
         for a in range(halves):
-            last = at == len(bits) - 1
-            res = merge(keep[a], took[a], now, heads, last)
-            if last:
-                att[a] = res[0].reshape(half, heads * head_dim)
-            else:
-                keep[a], send[a] = res
-        now //= 2
-
-    for at in reversed(range(len(outer))):
+            res = merge(keep[a], took[a], now, heads, pieces, last)
+            keep[a], send[a] = res[0], res[-1]
+        now //= pieces
+    att = [x.reshape(now, heads * head_dim) for x in keep]
+
+    for at in reversed(range(len(outer) - 1)):
         new = [swap(x, orders[a][at]) for a, x in enumerate(att)]
         att = [jnp.concatenate([x, y], axis=0) for x, y in zip(att, new)]
-    rows = []
-    for x in att:
-        rows += [x, swap(x, bits[0])]
-    product = jnp.dot(jnp.concatenate(rows, axis=0), out_weight, preferred_element_type=jnp.float32)
+    others = [swap(x, bits[0]) for x in att]
+    product = jnp.concatenate(
+        [
+            jnp.dot(jnp.concatenate(x, axis=0), out_weight, preferred_element_type=jnp.float32)
+            for x in (att, others)
+        ],
+        axis=0,
+    )
 
     width = product.shape[1]
-    place = {ja: i for i, ja in enumerate(rel)}
+    place = {(j, a): ((j & 1) * halves + a) * (n // 2) + i % (n // 2) for i, (j, a) in enumerate(rel)}
     inverse = jnp.array([place[(j, a)] for j in range(n) for a in range(halves)], jnp.int32).reshape(n, halves)
     source = inverse[jnp.arange(n, dtype=jnp.int32) ^ me].reshape(nh, -1)
     blocks = product.reshape(n * halves, half, width)

time: 111 us -> 109 us (0.982)
  waiting for transfers between devices: 46.6 us -> 42.1 us
  starting transfers between devices: 23.6 us -> 25.3 us
    ppermute x24 -> x22, waiting for transfers between devices: 43.3 us -> 38.6 us  [swap(): return lax.ppermute(x, 'seq', [(i, i ^ bit) for i in range(n)])]
    ppermute x24 -> x22, starting transfers between devices: 22.1 us -> 23.8 us  [swap(): return lax.ppermute(x, 'seq', [(i, i ^ bit) for i in range(n)])]
  transfers between devices with their start and end apart: 25 -> 23, of which waited for: 19 -> 18; matrix products, arithmetic and copies ran while one was open for 5% -> 6% of each run, Pallas kernels for 4% -> 5%
where the time goes in v4:
time: 109 us
  waiting for transfers between devices  42.1 us (39%)
  Pallas kernels  31.7 us (29%)
  starting transfers between devices  25.3 us (23%)
  local copies, waits for them, and re-layouts  5.94 us (5%)
  other arithmetic  1.74 us (2%)
  matrix products  1.49 us (1%)
    ppermute x22, waiting for transfers between devices, swap(): return lax.ppermute(x, 'seq', [(i, i ^ bit) for i in range(n)])  38.6 us
    pallas_call x1, Pallas kernels, attend(): call(functools.partial(attention_kernel, nq, kv, group, math.log2(math.e)...  26.7 us
    ppermute x22, starting transfers between devices, swap(): return lax.ppermute(x, 'seq', [(i, i ^ bit) for i in range(n)])  23.8 us
    ppermute x1, waiting for transfers between devices, shards(): took = lax.ppermute(give, 'head', [(i, i ^ step) for i in range(nh)])  3.47 us
    pallas_call x8, Pallas kernels, merge(): call(functools.partial(merge_kernel, per, heads, last), [jax.ShapeDtypeSt...  2.8 us
  transfers between devices with their start and end apart: 23, of which 18 were waited for; matrix products, arithmetic and copies ran while one was open for 6% of the time, Pallas kernels for 5%

profile of v4, /device:TPU:0, one launch (start us, length us, event | category | flops | bytes accessed | tf_op | source)
XLA Modules:
  0.0 108.6 jit_solution(1989535350156740102)
XLA Ops:
  0.9 4.1 %collective-permute-start = (bf16[8,32,128]{2,1,0:T(8,128)(2,1)S(1)}, bf16[8,32,128]{2,1,0:T(8,128)(2,1)S(1)}, u32[]{:S(2)}, u32[]{:S(2)}) collective-permute-start(bf16[8,32,128]{2,1,0:T(8,128)(2,1)S(1)} %get-tuple-element.58), channel_id=1, source_target_pairs={{0,16},{2,18},{4,20},{6,22},{8,24},{10,26},{12,28},{14,30},{16,0},... | collective-permute-start | bytes 196616 | tf_op jit(solution)/shard_map/ppermute | solution.py:322
  8.8 2.7 %collective-permute-done.1 = bf16[8,32,128]{2,1,0:T(8,128)(2,1)S(1)} collective-permute-done((bf16[8,32,128]{2,1,0:T(8,128)(2,1)S(1)}, bf16[8,32,128]{2,1,0:T(8,128)(2,1)S(1)}, u32[]{:S(2)}, u32[]{:S(2)}) %collective-permute-start.1) | collective-permute-done | bytes 65568 | tf_op jit(solution)/shard_map/ppermute | solution.py:322
  11.5 1.8 %collective-permute-start.4 = (bf16[16,32,128]{2,1,0:T(8,128)(2,1)S(1)}, bf16[16,32,128]{2,1,0:T(8,128)(2,1)S(1)}, u32[]{:S(2)}, u32[]{:S(2)}) collective-permute-start(bf16[16,32,128]{2,1,0:T(8,128)(2,1)S(1)} %pad_maximum_fusion.9), channel_id=1, source_target_pairs={{0,4},{2,6},{4,0},{6,2},{8,12},{10,14},{12,8},{14,10},{16,20},{18,... | collective-permute-start | bytes 393224 | tf_op jit(solution)/shard_map/ppermute | solution.py:322
  13.7 3.0 %collective-permute-done.4 = bf16[16,32,128]{2,1,0:T(8,128)(2,1)S(1)} collective-permute-done((bf16[16,32,128]{2,1,0:T(8,128)(2,1)S(1)}, bf16[16,32,128]{2,1,0:T(8,128)(2,1)S(1)}, u32[]{:S(2)}, u32[]{:S(2)}) %collective-permute-start.4) | collective-permute-done | bytes 131104 | tf_op jit(solution)/shard_map/ppermute | solution.py:322
  19.4 2.1 %lists.1 = (s32[1,2432]{1,0:T(1,128)S(1)}, s32[1,152]{1,0:T(1,128)S(1)}, s32[1,128]{1,0:T(1,128)S(1)}, s32[1,256]{1,0:T(1,128)S(1)}) custom-call(s32[1]{0:T(128)} %bitcast.2.me_ref, s32[256,64]{1,0:T(8,128)S(1)} %bitcast.26, s32[256,1]{1,0:T(8,128)S(1)} %copy.10.count_ref), custom_call_target="tpu_custom_call" | custom-call | flops 100000000 | bytes 1000000 | tf_op jit(solution)/shard_map/lists/pallas_call | solution.py:99
  21.5 2.5 %collective-permute-done.5 = bf16[32,32,128]{2,1,0:T(8,128)(2,1)S(1)} collective-permute-done((bf16[32,32,128]{2,1,0:T(8,128)(2,1)S(1)}, bf16[32,32,128]{2,1,0:T(8,128)(2,1)S(1)}, u32[]{:S(2)}, u32[]{:S(2)}) %collective-permute-start.5) | collective-permute-done | bytes 262176 | tf_op jit(solution)/shard_map/ppermute | solution.py:322
  26.0 1.3 %collective-permute-done.7.refs_3_ = bf16[64,32,128]{2,1,0:T(8,128)(2,1)S(1)} collective-permute-done((bf16[64,32,128]{2,1,0:T(8,128)(2,1)S(1)}, bf16[64,32,128]{2,1,0:T(8,128)(2,1)S(1)}, u32[]{:S(2)}, u32[]{:S(2)}) %collective-permute-start.7) | collective-permute-done | bytes 524320 | tf_op jit(solution)/shard_map/ppermute | solution.py:322
  28.0 26.7 %attention.1 = (bf16[2144,128]{1,0:T(8,128)(2,1)S(1)}, bf16[2144,128]{1,0:T(8,128)(2,1)S(1)}, bf16[2144,128]{1,0:T(8,128)(2,1)S(1)}, bf16[2144,128]{1,0:T(8,128)(2,1)S(1)}) custom-call(s32[1,2432]{1,0:T(1,128)S(1)} %get-tuple-element.39.lst, s32[1,152]{1,0:T(1,128)S(1)} %get-tuple-element.40.gp, s32[1,128]{1,0:T(1,128)S(1)} %get-tuple-element.41.start, ...), custom_call_target="tpu_custom_call" | custom-call | flops 2147483648 | bytes 16777216 | tf_op jit(solution)/shard_map/attention/pallas_call | solution.py:295
  55.3 1.4 %collective-permute-done.8.recv = bf16[2144,128]{1,0:T(8,128)(2,1)S(1)} collective-permute-done((bf16[2144,128]{1,0:T(8,128)(2,1)S(1)}, bf16[2144,128]{1,0:T(8,128)(2,1)S(1)}, u32[]{:S(2)}, u32[]{:S(2)}) %collective-permute-start.8) | collective-permute-done | bytes 548896 | tf_op jit(solution)/shard_map/ppermute | solution.py:322
  58.7 1.6 %collective-permute-start.15 = (bf16[1056,128]{1,0:T(8,128)(2,1)S(1)}, bf16[1056,128]{1,0:T(8,128)(2,1)S(1)}, u32[]{:S(2)}, u32[]{:S(2)}) collective-permute-start(bf16[1056,128]{1,0:T(8,128)(2,1)S(1)} %get-tuple-element.54), channel_id=1, source_target_pairs={{0,8},{2,10},{4,12},{6,14},{8,0},{10,2},{12,4},{14,6},{16,24},{18,... | collective-permute-start | bytes 811016 | tf_op jit(solution)/shard_map/ppermute | solution.py:322
  60.2 5.5 %collective-permute-done.9.recv = bf16[1056,128]{1,0:T(8,128)(2,1)S(1)} collective-permute-done((bf16[1056,128]{1,0:T(8,128)(2,1)S(1)}, bf16[1056,128]{1,0:T(8,128)(2,1)S(1)}, u32[]{:S(2)}, u32[]{:S(2)}) %collective-permute-start.9) | collective-permute-done | bytes 270368 | tf_op jit(solution)/shard_map/ppermute | solution.py:322
  68.1 1.6 %collective-permute-start.16 = (bf16[544,128]{1,0:T(8,128)(2,1)S(1)}, bf16[544,128]{1,0:T(8,128)(2,1)S(1)}, u32[]{:S(2)}, u32[]{:S(2)}) collective-permute-start(bf16[544,128]{1,0:T(8,128)(2,1)S(1)} %get-tuple-element.56), channel_id=1, source_target_pairs={{0,4},{2,6},{4,0},{6,2},{8,12},{10,14},{12,8},{14,10},{16,20},{18,... | collective-permute-start | bytes 417800 | tf_op jit(solution)/shard_map/ppermute | solution.py:322
  69.7 1.5 %collective-permute-done.10.recv = bf16[544,128]{1,0:T(8,128)(2,1)S(1)} collective-permute-done((bf16[544,128]{1,0:T(8,128)(2,1)S(1)}, bf16[544,128]{1,0:T(8,128)(2,1)S(1)}, u32[]{:S(2)}, u32[]{:S(2)}) %collective-permute-start.10) | collective-permute-done | bytes 139296 | tf_op jit(solution)/shard_map/ppermute | solution.py:322
  71.5 3.1 %collective-permute-start.11 = (bf16[544,128]{1,0:T(8,128)(2,1)S(1)}, bf16[544,128]{1,0:T(8,128)(2,1)S(1)}, u32[]{:S(2)}, u32[]{:S(2)}) collective-permute-start(bf16[544,128]{1,0:T(8,128)(2,1)S(1)} %merge.10.keep), channel_id=1, source_target_pairs={{0,16},{2,18},{4,20},{6,22},{8,24},{10,26},{12,28},{14,30},{16,0},... | collective-permute-start | bytes 417800 | tf_op jit(solution)/shard_map/ppermute | solution.py:322
  74.9 2.0 %collective-permute-start.17 = (bf16[544,128]{1,0:T(8,128)(2,1)S(1)}, bf16[544,128]{1,0:T(8,128)(2,1)S(1)}, u32[]{:S(2)}, u32[]{:S(2)}) collective-permute-start(bf16[544,128]{1,0:T(8,128)(2,1)S(1)} %merge.14.keep), channel_id=1, source_target_pairs={{0,16},{2,18},{4,20},{6,22},{8,24},{10,26},{12,28},{14,30},{16,0},... | collective-permute-start | bytes 417800 | tf_op jit(solution)/shard_map/ppermute | solution.py:322
  76.9 7.0 %collective-permute-done.11.recv = bf16[544,128]{1,0:T(8,128)(2,1)S(1)} collective-permute-done((bf16[544,128]{1,0:T(8,128)(2,1)S(1)}, bf16[544,128]{1,0:T(8,128)(2,1)S(1)}, u32[]{:S(2)}, u32[]{:S(2)}) %collective-permute-start.11) | collective-permute-done | bytes 139296 | tf_op jit(solution)/shard_map/ppermute | solution.py:322
  86.1 1.6 %collective-permute-start.18 = (bf16[16,4096]{1,0:T(8,128)(2,1)S(1)}, bf16[16,4096]{1,0:T(8,128)(2,1)S(1)}, u32[]{:S(2)}, u32[]{:S(2)}) collective-permute-start(bf16[16,4096]{1,0:T(8,128)(2,1)S(1)} %reshape.118), channel_id=1, source_target_pairs={{0,4},{2,6},{4,0},{6,2},{8,12},{10,14},{12,8},{14,10},{16,20},{18,... | collective-permute-start | bytes 393224 | tf_op jit(solution)/shard_map/ppermute | solution.py:322
  87.6 1.7 %collective-permute-done.12 = bf16[16,4096]{1,0:T(8,128)(2,1)S(1)} collective-permute-done((bf16[16,4096]{1,0:T(8,128)(2,1)S(1)}, bf16[16,4096]{1,0:T(8,128)(2,1)S(1)}, u32[]{:S(2)}, u32[]{:S(2)}) %collective-permute-start.12) | collective-permute-done | bytes 131104 | tf_op jit(solution)/shard_map/ppermute | solution.py:322
  89.3 1.3 %collective-permute-start.13 = (bf16[32,4096]{1,0:T(8,128)(2,1)S(1)}, bf16[32,4096]{1,0:T(8,128)(2,1)S(1)}, u32[]{:S(2)}, u32[]{:S(2)}) collective-permute-start(bf16[32,4096]{1,0:T(8,128)(2,1)S(1)} %pad_maximum_fusion.6), channel_id=1, source_target_pairs={{0,4},{2,6},{4,0},{6,2},{8,12},{10,14},{12,8},{14,10},{16,20},{18,... | collective-permute-start | bytes 786440 | tf_op jit(solution)/shard_map/ppermute | solution.py:322
  90.7 1.8 %collective-permute-done.18 = bf16[16,4096]{1,0:T(8,128)(2,1)S(1)} collective-permute-done((bf16[16,4096]{1,0:T(8,128)(2,1)S(1)}, bf16[16,4096]{1,0:T(8,128)(2,1)S(1)}, u32[]{:S(2)}, u32[]{:S(2)}) %collective-permute-start.18) | collective-permute-done | bytes 131104 | tf_op jit(solution)/shard_map/ppermute | solution.py:322
  93.3 3.1 %collective-permute-done.13 = bf16[32,4096]{1,0:T(8,128)(2,1)S(1)} collective-permute-done((bf16[32,4096]{1,0:T(8,128)(2,1)S(1)}, bf16[32,4096]{1,0:T(8,128)(2,1)S(1)}, u32[]{:S(2)}, u32[]{:S(2)}) %collective-permute-start.13) | collective-permute-done | bytes 262176 | tf_op jit(solution)/shard_map/ppermute | solution.py:322
  96.6 2.3 %collective-permute-done.19 = bf16[32,4096]{1,0:T(8,128)(2,1)S(1)} collective-permute-done((bf16[32,4096]{1,0:T(8,128)(2,1)S(1)}, bf16[32,4096]{1,0:T(8,128)(2,1)S(1)}, u32[]{:S(2)}, u32[]{:S(2)}) %collective-permute-start.19) | collective-permute-done | bytes 262176 | tf_op jit(solution)/shard_map/ppermute | solution.py:322
  102.3 1.6 %collective-permute-start.22 = (bf16[128,512]{1,0:T(8,128)(2,1)S(1)}, bf16[128,512]{1,0:T(8,128)(2,1)S(1)}, u32[]{:S(2)}, u32[]{:S(2)}) collective-permute-start(bf16[128,512]{1,0:T(8,128)(2,1)S(1)} %bitcast.28), channel_id=1, source_target_pairs={{0,1},{1,0},{2,3},{3,2},{4,5},{5,4},{6,7},{7,6},{8,9},{9,8},{10,11... | collective-permute-start | bytes 393224 | tf_op jit(solution)/shard_map/ppermute | solution.py:390
  104.4 3.5 %collective-permute-done.22 = bf16[128,512]{1,0:T(8,128)(2,1)S(1)} collective-permute-done((bf16[128,512]{1,0:T(8,128)(2,1)S(1)}, bf16[128,512]{1,0:T(8,128)(2,1)S(1)}, u32[]{:S(2)}, u32[]{:S(2)}) %collective-permute-start.22) | collective-permute-done | bytes 131104 | tf_op jit(solution)/shard_map/ppermute | solution.py:390
  (75 shorter events, 23.3 us)
Async XLA Ops:
  0.9 7.9 %collective-permute-start = (bf16[8,32,128]{2,1,0:T(8,128)(2,1)S(1)}, bf16[8,32,128]{2,1,0:T(8,128)(2,1)S(1)}, u32[]{:S(2)}, u32[]{:S(2)}) collective-permute-start(bf16[8,32,128]{2,1,0:T(8,128)(2,1)S(1)} %get-tuple-element.58), channel_id=1, source_target_pairs={{0,16},{2,18},{4,20},{6,22},{8,24},{10,26},{12,28},{14,30},{16,0},... | collective-permute-start | bytes 196616 | tf_op jit(solution)/shard_map/ppermute | solution.py:322
  5.0 6.5 %collective-permute-start.1 = (bf16[8,32,128]{2,1,0:T(8,128)(2,1)S(1)}, bf16[8,32,128]{2,1,0:T(8,128)(2,1)S(1)}, u32[]{:S(2)}, u32[]{:S(2)}) collective-permute-start(bf16[8,32,128]{2,1,0:T(8,128)(2,1)S(1)} %get-tuple-element.57), channel_id=1, source_target_pairs={{0,16},{2,18},{4,20},{6,22},{8,24},{10,26},{12,28},{14,30},{16,0},... | collective-permute-start | bytes 196616 | tf_op jit(solution)/shard_map/ppermute | solution.py:322
  11.5 5.3 %collective-permute-start.4 = (bf16[16,32,128]{2,1,0:T(8,128)(2,1)S(1)}, bf16[16,32,128]{2,1,0:T(8,128)(2,1)S(1)}, u32[]{:S(2)}, u32[]{:S(2)}) collective-permute-start(bf16[16,32,128]{2,1,0:T(8,128)(2,1)S(1)} %pad_maximum_fusion.9), channel_id=1, source_target_pairs={{0,4},{2,6},{4,0},{6,2},{8,12},{10,14},{12,8},{14,10},{16,20},{18,... | collective-permute-start | bytes 393224 | tf_op jit(solution)/shard_map/ppermute | solution.py:322
  13.3 5.0 %collective-permute-start.2 = (bf16[16,32,128]{2,1,0:T(8,128)(2,1)S(1)}, bf16[16,32,128]{2,1,0:T(8,128)(2,1)S(1)}, u32[]{:S(2)}, u32[]{:S(2)}) collective-permute-start(bf16[16,32,128]{2,1,0:T(8,128)(2,1)S(1)} %pad_maximum_fusion.8), channel_id=1, source_target_pairs={{0,8},{2,10},{4,12},{6,14},{8,0},{10,2},{12,4},{14,6},{16,24},{18,... | collective-permute-start | bytes 393224 | tf_op jit(solution)/shard_map/ppermute | solution.py:322
  16.8 7.2 %collective-permute-start.5 = (bf16[32,32,128]{2,1,0:T(8,128)(2,1)S(1)}, bf16[32,32,128]{2,1,0:T(8,128)(2,1)S(1)}, u32[]{:S(2)}, u32[]{:S(2)}) collective-permute-start(bf16[32,32,128]{2,1,0:T(8,128)(2,1)S(1)} %pad_maximum_fusion.5), channel_id=1, source_target_pairs={{0,8},{2,10},{4,12},{6,14},{8,0},{10,2},{12,4},{14,6},{16,24},{18,... | collective-permute-start | bytes 786440 | tf_op jit(solution)/shard_map/ppermute | solution.py:322
  18.4 6.8 %collective-permute-start.3 = (bf16[32,32,128]{2,1,0:T(8,128)(2,1)S(1)}, bf16[32,32,128]{2,1,0:T(8,128)(2,1)S(1)}, u32[]{:S(2)}, u32[]{:S(2)}) collective-permute-start(bf16[32,32,128]{2,1,0:T(8,128)(2,1)S(1)} %pad_maximum_fusion.4), channel_id=1, source_target_pairs={{0,4},{2,6},{4,0},{6,2},{8,12},{10,14},{12,8},{14,10},{16,20},{18,... | collective-permute-start | bytes 786440 | tf_op jit(solution)/shard_map/ppermute | solution.py:322
  25.2 2.0 %collective-permute-start.7 = (bf16[64,32,128]{2,1,0:T(8,128)(2,1)S(1)}, bf16[64,32,128]{2,1,0:T(8,128)(2,1)S(1)}, u32[]{:S(2)}, u32[]{:S(2)}) collective-permute-start(bf16[64,32,128]{2,1,0:T(8,128)(2,1)S(1)} %pad_maximum_fusion.1.refs_2_), channel_id=1, source_target_pairs={{0,2},{2,0},{4,6},{6,4},{8,10},{10,8},{12,14},{14,12},{16,18},{18,... | collective-permute-start | bytes 1572872 | tf_op jit(solution)/shard_map/ppermute | solution.py:322
  25.4 41.7 %copy-start.1 = (s32[16,2]{1,0:T(8,128)S(1)}, s32[16,2]{1,0:T(8,128)}, u32[]{:S(2)}) copy-start(s32[16,2]{1,0:T(8,128)} %constant.31) | copy-start | bytes 388
  25.4 2.6 %collective-permute-start.6 = (bf16[64,32,128]{2,1,0:T(8,128)(2,1)S(1)}, bf16[64,32,128]{2,1,0:T(8,128)(2,1)S(1)}, u32[]{:S(2)}, u32[]{:S(2)}) collective-permute-start(bf16[64,32,128]{2,1,0:T(8,128)(2,1)S(1)} %pad_maximum_fusion.refs_0_), channel_id=1, source_target_pairs={{0,2},{2,0},{4,6},{6,4},{8,10},{10,8},{12,14},{14,12},{16,18},{18,... | collective-permute-start | bytes 1572872 | tf_op jit(solution)/shard_map/ppermute | solution.py:322
  54.7 2.0 %collective-permute-start.8 = (bf16[2144,128]{1,0:T(8,128)(2,1)S(1)}, bf16[2144,128]{1,0:T(8,128)(2,1)S(1)}, u32[]{:S(2)}, u32[]{:S(2)}) collective-permute-start(bf16[2144,128]{1,0:T(8,128)(2,1)S(1)} %get-tuple-element.46), channel_id=1, source_target_pairs={{0,2},{2,0},{4,6},{6,4},{8,10},{10,8},{12,14},{14,12},{16,18},{18,... | collective-permute-start | bytes 1646600 | tf_op jit(solution)/shard_map/ppermute | solution.py:322
  54.8 3.4 %collective-permute-start.14 = (bf16[2144,128]{1,0:T(8,128)(2,1)S(1)}, bf16[2144,128]{1,0:T(8,128)(2,1)S(1)}, u32[]{:S(2)}, u32[]{:S(2)}) collective-permute-start(bf16[2144,128]{1,0:T(8,128)(2,1)S(1)} %get-tuple-element.52), channel_id=1, source_target_pairs={{0,2},{2,0},{4,6},{6,4},{8,10},{10,8},{12,14},{14,12},{16,18},{18,... | collective-permute-start | bytes 1646600 | tf_op jit(solution)/shard_map/ppermute | solution.py:322
  57.2 8.6 %collective-permute-start.9 = (bf16[1056,128]{1,0:T(8,128)(2,1)S(1)}, bf16[1056,128]{1,0:T(8,128)(2,1)S(1)}, u32[]{:S(2)}, u32[]{:S(2)}) collective-permute-start(bf16[1056,128]{1,0:T(8,128)(2,1)S(1)} %get-tuple-element.48), channel_id=1, source_target_pairs={{0,4},{2,6},{4,0},{6,2},{8,12},{10,14},{12,8},{14,10},{16,20},{18,... | collective-permute-start | bytes 811016 | tf_op jit(solution)/shard_map/ppermute | solution.py:322
  58.7 9.1 %collective-permute-start.15 = (bf16[1056,128]{1,0:T(8,128)(2,1)S(1)}, bf16[1056,128]{1,0:T(8,128)(2,1)S(1)}, u32[]{:S(2)}, u32[]{:S(2)}) collective-permute-start(bf16[1056,128]{1,0:T(8,128)(2,1)S(1)} %get-tuple-element.54), channel_id=1, source_target_pairs={{0,8},{2,10},{4,12},{6,14},{8,0},{10,2},{12,4},{14,6},{16,24},{18,... | collective-permute-start | bytes 811016 | tf_op jit(solution)/shard_map/ppermute | solution.py:322
  66.1 5.1 %collective-permute-start.10 = (bf16[544,128]{1,0:T(8,128)(2,1)S(1)}, bf16[544,128]{1,0:T(8,128)(2,1)S(1)}, u32[]{:S(2)}, u32[]{:S(2)}) collective-permute-start(bf16[544,128]{1,0:T(8,128)(2,1)S(1)} %get-tuple-element.50), channel_id=1, source_target_pairs={{0,8},{2,10},{4,12},{6,14},{8,0},{10,2},{12,4},{14,6},{16,24},{18,... | collective-permute-start | bytes 417800 | tf_op jit(solution)/shard_map/ppermute | solution.py:322
  68.1 6.6 %collective-permute-start.16 = (bf16[544,128]{1,0:T(8,128)(2,1)S(1)}, bf16[544,128]{1,0:T(8,128)(2,1)S(1)}, u32[]{:S(2)}, u32[]{:S(2)}) collective-permute-start(bf16[544,128]{1,0:T(8,128)(2,1)S(1)} %get-tuple-element.56), channel_id=1, source_target_pairs={{0,4},{2,6},{4,0},{6,2},{8,12},{10,14},{12,8},{14,10},{16,20},{18,... | collective-permute-start | bytes 417800 | tf_op jit(solution)/shard_map/ppermute | solution.py:322
  71.5 12.4 %collective-permute-start.11 = (bf16[544,128]{1,0:T(8,128)(2,1)S(1)}, bf16[544,128]{1,0:T(8,128)(2,1)S(1)}, u32[]{:S(2)}, u32[]{:S(2)}) collective-permute-start(bf16[544,128]{1,0:T(8,128)(2,1)S(1)} %merge.10.keep), channel_id=1, source_target_pairs={{0,16},{2,18},{4,20},{6,22},{8,24},{10,26},{12,28},{14,30},{16,0},... | collective-permute-start | bytes 417800 | tf_op jit(solution)/shard_map/ppermute | solution.py:322
  74.9 10.7 %collective-permute-start.17 = (bf16[544,128]{1,0:T(8,128)(2,1)S(1)}, bf16[544,128]{1,0:T(8,128)(2,1)S(1)}, u32[]{:S(2)}, u32[]{:S(2)}) collective-permute-start(bf16[544,128]{1,0:T(8,128)(2,1)S(1)} %merge.14.keep), channel_id=1, source_target_pairs={{0,16},{2,18},{4,20},{6,22},{8,24},{10,26},{12,28},{14,30},{16,0},... | collective-permute-start | bytes 417800 | tf_op jit(solution)/shard_map/ppermute | solution.py:322
  84.3 5.0 %collective-permute-start.12 = (bf16[16,4096]{1,0:T(8,128)(2,1)S(1)}, bf16[16,4096]{1,0:T(8,128)(2,1)S(1)}, u32[]{:S(2)}, u32[]{:S(2)}) collective-permute-start(bf16[16,4096]{1,0:T(8,128)(2,1)S(1)} %reshape.117), channel_id=1, source_target_pairs={{0,8},{2,10},{4,12},{6,14},{8,0},{10,2},{12,4},{14,6},{16,24},{18,... | collective-permute-start | bytes 393224 | tf_op jit(solution)/shard_map/ppermute | solution.py:322
  86.1 6.4 %collective-permute-start.18 = (bf16[16,4096]{1,0:T(8,128)(2,1)S(1)}, bf16[16,4096]{1,0:T(8,128)(2,1)S(1)}, u32[]{:S(2)}, u32[]{:S(2)}) collective-permute-start(bf16[16,4096]{1,0:T(8,128)(2,1)S(1)} %reshape.118), channel_id=1, source_target_pairs={{0,4},{2,6},{4,0},{6,2},{8,12},{10,14},{12,8},{14,10},{16,20},{18,... | collective-permute-start | bytes 393224 | tf_op jit(solution)/shard_map/ppermute | solution.py:322
  89.3 7.1 %collective-permute-start.13 = (bf16[32,4096]{1,0:T(8,128)(2,1)S(1)}, bf16[32,4096]{1,0:T(8,128)(2,1)S(1)}, u32[]{:S(2)}, u32[]{:S(2)}) collective-permute-start(bf16[32,4096]{1,0:T(8,128)(2,1)S(1)} %pad_maximum_fusion.6), channel_id=1, source_target_pairs={{0,4},{2,6},{4,0},{6,2},{8,12},{10,14},{12,8},{14,10},{16,20},{18,... | collective-permute-start | bytes 786440 | tf_op jit(solution)/shard_map/ppermute | solution.py:322
  92.5 6.4 %collective-permute-start.19 = (bf16[32,4096]{1,0:T(8,128)(2,1)S(1)}, bf16[32,4096]{1,0:T(8,128)(2,1)S(1)}, u32[]{:S(2)}, u32[]{:S(2)}) collective-permute-start(bf16[32,4096]{1,0:T(8,128)(2,1)S(1)} %pad_maximum_fusion.7), channel_id=1, source_target_pairs={{0,8},{2,10},{4,12},{6,14},{8,0},{10,2},{12,4},{14,6},{16,24},{18,... | collective-permute-start | bytes 786440 | tf_op jit(solution)/shard_map/ppermute | solution.py:322
  96.5 3.4 %collective-permute-start.20 = (bf16[64,4096]{1,0:T(8,128)(2,1)S(1)}, bf16[64,4096]{1,0:T(8,128)(2,1)S(1)}, u32[]{:S(2)}, u32[]{:S(2)}) collective-permute-start(bf16[64,4096]{1,0:T(8,128)(2,1)S(1)} %pad_maximum_fusion.2), channel_id=1, source_target_pairs={{0,2},{2,0},{4,6},{6,4},{8,10},{10,8},{12,14},{14,12},{16,18},{18,... | collective-permute-start | bytes 1572872 | tf_op jit(solution)/shard_map/ppermute | solution.py:322
  99.0 2.0 %collective-permute-start.21 = (bf16[64,4096]{1,0:T(8,128)(2,1)S(1)}, bf16[64,4096]{1,0:T(8,128)(2,1)S(1)}, u32[]{:S(2)}, u32[]{:S(2)}) collective-permute-start(bf16[64,4096]{1,0:T(8,128)(2,1)S(1)} %pad_maximum_fusion.3), channel_id=1, source_target_pairs={{0,2},{2,0},{4,6},{6,4},{8,10},{10,8},{12,14},{14,12},{16,18},{18,... | collective-permute-start | bytes 1572872 | tf_op jit(solution)/shard_map/ppermute | solution.py:322
  102.3 5.6 %collective-permute-start.22 = (bf16[128,512]{1,0:T(8,128)(2,1)S(1)}, bf16[128,512]{1,0:T(8,128)(2,1)S(1)}, u32[]{:S(2)}, u32[]{:S(2)}) collective-permute-start(bf16[128,512]{1,0:T(8,128)(2,1)S(1)} %bitcast.28), channel_id=1, source_target_pairs={{0,1},{1,0},{2,3},{3,2},{4,5},{5,4},{6,7},{7,6},{8,9},{9,8},{10,11... | collective-permute-start | bytes 393224 | tf_op jit(solution)/shard_map/ppermute | solution.py:390
  (1 other events, 13.1 us)

commit v5 on v4

--- a/solution.py
+++ b/solution.py
@@ -12,7 +12,7 @@
 TILE = 16
 SEGMENTS = 4
 TOGETHER = 4
-UNROLL = 4
+UNROLL = 8
 LEAD = 2 * TOGETHER
 NONE = -1e30
 PLANES = 3

time: 109 us -> 109 us (level)
  no operation moved by 1% of the time
where the time goes in v5:
time: 109 us; the launch traced here: 108 us
  waiting for transfers between devices  42.1 us (39%)
  Pallas kernels  31.3 us (29%)
  starting transfers between devices  25.3 us (23%)
  local copies, waits for them, and re-layouts  5.94 us (5%)
  other arithmetic  1.74 us (2%)
  matrix products  1.49 us (1%)
    ppermute x22, waiting for transfers between devices, swap(): return lax.ppermute(x, 'seq', [(i, i ^ bit) for i in range(n)])  38.7 us
    pallas_call x1, Pallas kernels, attend(): call(functools.partial(attention_kernel, nq, kv, group, math.log2(math.e)...  26.4 us
    ppermute x22, starting transfers between devices, swap(): return lax.ppermute(x, 'seq', [(i, i ^ bit) for i in range(n)])  23.8 us
    ppermute x1, waiting for transfers between devices, shards(): took = lax.ppermute(give, 'head', [(i, i ^ step) for i in range(nh)])  3.46 us
    pallas_call x8, Pallas kernels, merge(): call(functools.partial(merge_kernel, per, heads, last), [jax.ShapeDtypeSt...  2.8 us
  transfers between devices with their start and end apart: 23, of which 18 were waited for; matrix products, arithmetic and copies ran while one was open for 6% of the time, Pallas kernels for 5%

profile of v5, /device:TPU:0, one launch (start us, length us, event | category | flops | bytes accessed | tf_op | source)
XLA Modules:
  0.0 108.3 jit_solution(17486049485813985749)
XLA Ops:
  0.9 4.1 %collective-permute-start = (bf16[8,32,128]{2,1,0:T(8,128)(2,1)S(1)}, bf16[8,32,128]{2,1,0:T(8,128)(2,1)S(1)}, u32[]{:S(2)}, u32[]{:S(2)}) collective-permute-start(bf16[8,32,128]{2,1,0:T(8,128)(2,1)S(1)} %get-tuple-element.58), channel_id=1, source_target_pairs={{0,16},{2,18},{4,20},{6,22},{8,24},{10,26},{12,28},{14,30},{16,0},... | collective-permute-start | bytes 196616 | tf_op jit(solution)/shard_map/ppermute | solution.py:322
  8.8 2.7 %collective-permute-done.1 = bf16[8,32,128]{2,1,0:T(8,128)(2,1)S(1)} collective-permute-done((bf16[8,32,128]{2,1,0:T(8,128)(2,1)S(1)}, bf16[8,32,128]{2,1,0:T(8,128)(2,1)S(1)}, u32[]{:S(2)}, u32[]{:S(2)}) %collective-permute-start.1) | collective-permute-done | bytes 65568 | tf_op jit(solution)/shard_map/ppermute | solution.py:322
  11.5 1.8 %collective-permute-start.4 = (bf16[16,32,128]{2,1,0:T(8,128)(2,1)S(1)}, bf16[16,32,128]{2,1,0:T(8,128)(2,1)S(1)}, u32[]{:S(2)}, u32[]{:S(2)}) collective-permute-start(bf16[16,32,128]{2,1,0:T(8,128)(2,1)S(1)} %pad_maximum_fusion.9), channel_id=1, source_target_pairs={{0,4},{2,6},{4,0},{6,2},{8,12},{10,14},{12,8},{14,10},{16,20},{18,... | collective-permute-start | bytes 393224 | tf_op jit(solution)/shard_map/ppermute | solution.py:322
  13.7 3.0 %collective-permute-done.4 = bf16[16,32,128]{2,1,0:T(8,128)(2,1)S(1)} collective-permute-done((bf16[16,32,128]{2,1,0:T(8,128)(2,1)S(1)}, bf16[16,32,128]{2,1,0:T(8,128)(2,1)S(1)}, u32[]{:S(2)}, u32[]{:S(2)}) %collective-permute-start.4) | collective-permute-done | bytes 131104 | tf_op jit(solution)/shard_map/ppermute | solution.py:322
  19.4 2.1 %lists.1 = (s32[1,2432]{1,0:T(1,128)S(1)}, s32[1,152]{1,0:T(1,128)S(1)}, s32[1,128]{1,0:T(1,128)S(1)}, s32[1,256]{1,0:T(1,128)S(1)}) custom-call(s32[1]{0:T(128)} %bitcast.2.me_ref, s32[256,64]{1,0:T(8,128)S(1)} %bitcast.26, s32[256,1]{1,0:T(8,128)S(1)} %copy.10.count_ref), custom_call_target="tpu_custom_call" | custom-call | flops 100000000 | bytes 1000000 | tf_op jit(solution)/shard_map/lists/pallas_call | solution.py:99
  21.5 2.5 %collective-permute-done.5 = bf16[32,32,128]{2,1,0:T(8,128)(2,1)S(1)} collective-permute-done((bf16[32,32,128]{2,1,0:T(8,128)(2,1)S(1)}, bf16[32,32,128]{2,1,0:T(8,128)(2,1)S(1)}, u32[]{:S(2)}, u32[]{:S(2)}) %collective-permute-start.5) | collective-permute-done | bytes 262176 | tf_op jit(solution)/shard_map/ppermute | solution.py:322
  26.0 1.3 %collective-permute-done.7.refs_3_ = bf16[64,32,128]{2,1,0:T(8,128)(2,1)S(1)} collective-permute-done((bf16[64,32,128]{2,1,0:T(8,128)(2,1)S(1)}, bf16[64,32,128]{2,1,0:T(8,128)(2,1)S(1)}, u32[]{:S(2)}, u32[]{:S(2)}) %collective-permute-start.7) | collective-permute-done | bytes 524320 | tf_op jit(solution)/shard_map/ppermute | solution.py:322
  28.0 26.4 %attention.1 = (bf16[2144,128]{1,0:T(8,128)(2,1)S(1)}, bf16[2144,128]{1,0:T(8,128)(2,1)S(1)}, bf16[2144,128]{1,0:T(8,128)(2,1)S(1)}, bf16[2144,128]{1,0:T(8,128)(2,1)S(1)}) custom-call(s32[1,2432]{1,0:T(1,128)S(1)} %get-tuple-element.39.lst, s32[1,152]{1,0:T(1,128)S(1)} %get-tuple-element.40.gp, s32[1,128]{1,0:T(1,128)S(1)} %get-tuple-element.41.start, ...), custom_call_target="tpu_custom_call" | custom-call | flops 2147483648 | bytes 16777216 | tf_op jit(solution)/shard_map/attention/pallas_call | solution.py:295
  55.0 1.4 %collective-permute-done.8.recv = bf16[2144,128]{1,0:T(8,128)(2,1)S(1)} collective-permute-done((bf16[2144,128]{1,0:T(8,128)(2,1)S(1)}, bf16[2144,128]{1,0:T(8,128)(2,1)S(1)}, u32[]{:S(2)}, u32[]{:S(2)}) %collective-permute-start.8) | collective-permute-done | bytes 548896 | tf_op jit(solution)/shard_map/ppermute | solution.py:322
  58.6 1.3 %collective-permute-start.15 = (bf16[1056,128]{1,0:T(8,128)(2,1)S(1)}, bf16[1056,128]{1,0:T(8,128)(2,1)S(1)}, u32[]{:S(2)}, u32[]{:S(2)}) collective-permute-start(bf16[1056,128]{1,0:T(8,128)(2,1)S(1)} %get-tuple-element.54), channel_id=1, source_target_pairs={{0,8},{2,10},{4,12},{6,14},{8,0},{10,2},{12,4},{14,6},{16,24},{18,... | collective-permute-start | bytes 811016 | tf_op jit(solution)/shard_map/ppermute | solution.py:322
  59.9 5.6 %collective-permute-done.9.recv = bf16[1056,128]{1,0:T(8,128)(2,1)S(1)} collective-permute-done((bf16[1056,128]{1,0:T(8,128)(2,1)S(1)}, bf16[1056,128]{1,0:T(8,128)(2,1)S(1)}, u32[]{:S(2)}, u32[]{:S(2)}) %collective-permute-start.9) | collective-permute-done | bytes 270368 | tf_op jit(solution)/shard_map/ppermute | solution.py:322
  67.6 1.8 %collective-permute-start.16 = (bf16[544,128]{1,0:T(8,128)(2,1)S(1)}, bf16[544,128]{1,0:T(8,128)(2,1)S(1)}, u32[]{:S(2)}, u32[]{:S(2)}) collective-permute-start(bf16[544,128]{1,0:T(8,128)(2,1)S(1)} %get-tuple-element.56), channel_id=1, source_target_pairs={{0,4},{2,6},{4,0},{6,2},{8,12},{10,14},{12,8},{14,10},{16,20},{18,... | collective-permute-start | bytes 417800 | tf_op jit(solution)/shard_map/ppermute | solution.py:322
  69.4 1.5 %collective-permute-done.10.recv = bf16[544,128]{1,0:T(8,128)(2,1)S(1)} collective-permute-done((bf16[544,128]{1,0:T(8,128)(2,1)S(1)}, bf16[544,128]{1,0:T(8,128)(2,1)S(1)}, u32[]{:S(2)}, u32[]{:S(2)}) %collective-permute-start.10) | collective-permute-done | bytes 139296 | tf_op jit(solution)/shard_map/ppermute | solution.py:322
  71.2 3.1 %collective-permute-start.11 = (bf16[544,128]{1,0:T(8,128)(2,1)S(1)}, bf16[544,128]{1,0:T(8,128)(2,1)S(1)}, u32[]{:S(2)}, u32[]{:S(2)}) collective-permute-start(bf16[544,128]{1,0:T(8,128)(2,1)S(1)} %merge.10.keep), channel_id=1, source_target_pairs={{0,16},{2,18},{4,20},{6,22},{8,24},{10,26},{12,28},{14,30},{16,0},... | collective-permute-start | bytes 417800 | tf_op jit(solution)/shard_map/ppermute | solution.py:322
  74.6 2.0 %collective-permute-start.17 = (bf16[544,128]{1,0:T(8,128)(2,1)S(1)}, bf16[544,128]{1,0:T(8,128)(2,1)S(1)}, u32[]{:S(2)}, u32[]{:S(2)}) collective-permute-start(bf16[544,128]{1,0:T(8,128)(2,1)S(1)} %merge.14.keep), channel_id=1, source_target_pairs={{0,16},{2,18},{4,20},{6,22},{8,24},{10,26},{12,28},{14,30},{16,0},... | collective-permute-start | bytes 417800 | tf_op jit(solution)/shard_map/ppermute | solution.py:322
  76.6 7.0 %collective-permute-done.11.recv = bf16[544,128]{1,0:T(8,128)(2,1)S(1)} collective-permute-done((bf16[544,128]{1,0:T(8,128)(2,1)S(1)}, bf16[544,128]{1,0:T(8,128)(2,1)S(1)}, u32[]{:S(2)}, u32[]{:S(2)}) %collective-permute-start.11) | collective-permute-done | bytes 139296 | tf_op jit(solution)/shard_map/ppermute | solution.py:322
  85.7 1.6 %collective-permute-start.18 = (bf16[16,4096]{1,0:T(8,128)(2,1)S(1)}, bf16[16,4096]{1,0:T(8,128)(2,1)S(1)}, u32[]{:S(2)}, u32[]{:S(2)}) collective-permute-start(bf16[16,4096]{1,0:T(8,128)(2,1)S(1)} %reshape.118), channel_id=1, source_target_pairs={{0,4},{2,6},{4,0},{6,2},{8,12},{10,14},{12,8},{14,10},{16,20},{18,... | collective-permute-start | bytes 393224 | tf_op jit(solution)/shard_map/ppermute | solution.py:322
  87.3 1.7 %collective-permute-done.12 = bf16[16,4096]{1,0:T(8,128)(2,1)S(1)} collective-permute-done((bf16[16,4096]{1,0:T(8,128)(2,1)S(1)}, bf16[16,4096]{1,0:T(8,128)(2,1)S(1)}, u32[]{:S(2)}, u32[]{:S(2)}) %collective-permute-start.12) | collective-permute-done | bytes 131104 | tf_op jit(solution)/shard_map/ppermute | solution.py:322
  89.0 1.3 %collective-permute-start.13 = (bf16[32,4096]{1,0:T(8,128)(2,1)S(1)}, bf16[32,4096]{1,0:T(8,128)(2,1)S(1)}, u32[]{:S(2)}, u32[]{:S(2)}) collective-permute-start(bf16[32,4096]{1,0:T(8,128)(2,1)S(1)} %pad_maximum_fusion.6), channel_id=1, source_target_pairs={{0,4},{2,6},{4,0},{6,2},{8,12},{10,14},{12,8},{14,10},{16,20},{18,... | collective-permute-start | bytes 786440 | tf_op jit(solution)/shard_map/ppermute | solution.py:322
  90.3 1.8 %collective-permute-done.18 = bf16[16,4096]{1,0:T(8,128)(2,1)S(1)} collective-permute-done((bf16[16,4096]{1,0:T(8,128)(2,1)S(1)}, bf16[16,4096]{1,0:T(8,128)(2,1)S(1)}, u32[]{:S(2)}, u32[]{:S(2)}) %collective-permute-start.18) | collective-permute-done | bytes 131104 | tf_op jit(solution)/shard_map/ppermute | solution.py:322
  93.0 3.1 %collective-permute-done.13 = bf16[32,4096]{1,0:T(8,128)(2,1)S(1)} collective-permute-done((bf16[32,4096]{1,0:T(8,128)(2,1)S(1)}, bf16[32,4096]{1,0:T(8,128)(2,1)S(1)}, u32[]{:S(2)}, u32[]{:S(2)}) %collective-permute-start.13) | collective-permute-done | bytes 262176 | tf_op jit(solution)/shard_map/ppermute | solution.py:322
  96.3 2.3 %collective-permute-done.19 = bf16[32,4096]{1,0:T(8,128)(2,1)S(1)} collective-permute-done((bf16[32,4096]{1,0:T(8,128)(2,1)S(1)}, bf16[32,4096]{1,0:T(8,128)(2,1)S(1)}, u32[]{:S(2)}, u32[]{:S(2)}) %collective-permute-start.19) | collective-permute-done | bytes 262176 | tf_op jit(solution)/shard_map/ppermute | solution.py:322
  102.0 1.6 %collective-permute-start.22 = (bf16[128,512]{1,0:T(8,128)(2,1)S(1)}, bf16[128,512]{1,0:T(8,128)(2,1)S(1)}, u32[]{:S(2)}, u32[]{:S(2)}) collective-permute-start(bf16[128,512]{1,0:T(8,128)(2,1)S(1)} %bitcast.28), channel_id=1, source_target_pairs={{0,1},{1,0},{2,3},{3,2},{4,5},{5,4},{6,7},{7,6},{8,9},{9,8},{10,11... | collective-permute-start | bytes 393224 | tf_op jit(solution)/shard_map/ppermute | solution.py:390
  104.1 3.5 %collective-permute-done.22 = bf16[128,512]{1,0:T(8,128)(2,1)S(1)} collective-permute-done((bf16[128,512]{1,0:T(8,128)(2,1)S(1)}, bf16[128,512]{1,0:T(8,128)(2,1)S(1)}, u32[]{:S(2)}, u32[]{:S(2)}) %collective-permute-start.22) | collective-permute-done | bytes 131104 | tf_op jit(solution)/shard_map/ppermute | solution.py:390
  (75 shorter events, 23.4 us)
Async XLA Ops:
  0.9 7.9 %collective-permute-start = (bf16[8,32,128]{2,1,0:T(8,128)(2,1)S(1)}, bf16[8,32,128]{2,1,0:T(8,128)(2,1)S(1)}, u32[]{:S(2)}, u32[]{:S(2)}) collective-permute-start(bf16[8,32,128]{2,1,0:T(8,128)(2,1)S(1)} %get-tuple-element.58), channel_id=1, source_target_pairs={{0,16},{2,18},{4,20},{6,22},{8,24},{10,26},{12,28},{14,30},{16,0},... | collective-permute-start | bytes 196616 | tf_op jit(solution)/shard_map/ppermute | solution.py:322
  5.0 6.5 %collective-permute-start.1 = (bf16[8,32,128]{2,1,0:T(8,128)(2,1)S(1)}, bf16[8,32,128]{2,1,0:T(8,128)(2,1)S(1)}, u32[]{:S(2)}, u32[]{:S(2)}) collective-permute-start(bf16[8,32,128]{2,1,0:T(8,128)(2,1)S(1)} %get-tuple-element.57), channel_id=1, source_target_pairs={{0,16},{2,18},{4,20},{6,22},{8,24},{10,26},{12,28},{14,30},{16,0},... | collective-permute-start | bytes 196616 | tf_op jit(solution)/shard_map/ppermute | solution.py:322
  11.5 5.3 %collective-permute-start.4 = (bf16[16,32,128]{2,1,0:T(8,128)(2,1)S(1)}, bf16[16,32,128]{2,1,0:T(8,128)(2,1)S(1)}, u32[]{:S(2)}, u32[]{:S(2)}) collective-permute-start(bf16[16,32,128]{2,1,0:T(8,128)(2,1)S(1)} %pad_maximum_fusion.9), channel_id=1, source_target_pairs={{0,4},{2,6},{4,0},{6,2},{8,12},{10,14},{12,8},{14,10},{16,20},{18,... | collective-permute-start | bytes 393224 | tf_op jit(solution)/shard_map/ppermute | solution.py:322
  13.3 5.0 %collective-permute-start.2 = (bf16[16,32,128]{2,1,0:T(8,128)(2,1)S(1)}, bf16[16,32,128]{2,1,0:T(8,128)(2,1)S(1)}, u32[]{:S(2)}, u32[]{:S(2)}) collective-permute-start(bf16[16,32,128]{2,1,0:T(8,128)(2,1)S(1)} %pad_maximum_fusion.8), channel_id=1, source_target_pairs={{0,8},{2,10},{4,12},{6,14},{8,0},{10,2},{12,4},{14,6},{16,24},{18,... | collective-permute-start | bytes 393224 | tf_op jit(solution)/shard_map/ppermute | solution.py:322
  16.8 7.2 %collective-permute-start.5 = (bf16[32,32,128]{2,1,0:T(8,128)(2,1)S(1)}, bf16[32,32,128]{2,1,0:T(8,128)(2,1)S(1)}, u32[]{:S(2)}, u32[]{:S(2)}) collective-permute-start(bf16[32,32,128]{2,1,0:T(8,128)(2,1)S(1)} %pad_maximum_fusion.5), channel_id=1, source_target_pairs={{0,8},{2,10},{4,12},{6,14},{8,0},{10,2},{12,4},{14,6},{16,24},{18,... | collective-permute-start | bytes 786440 | tf_op jit(solution)/shard_map/ppermute | solution.py:322
  18.4 6.8 %collective-permute-start.3 = (bf16[32,32,128]{2,1,0:T(8,128)(2,1)S(1)}, bf16[32,32,128]{2,1,0:T(8,128)(2,1)S(1)}, u32[]{:S(2)}, u32[]{:S(2)}) collective-permute-start(bf16[32,32,128]{2,1,0:T(8,128)(2,1)S(1)} %pad_maximum_fusion.4), channel_id=1, source_target_pairs={{0,4},{2,6},{4,0},{6,2},{8,12},{10,14},{12,8},{14,10},{16,20},{18,... | collective-permute-start | bytes 786440 | tf_op jit(solution)/shard_map/ppermute | solution.py:322
  25.2 2.0 %collective-permute-start.7 = (bf16[64,32,128]{2,1,0:T(8,128)(2,1)S(1)}, bf16[64,32,128]{2,1,0:T(8,128)(2,1)S(1)}, u32[]{:S(2)}, u32[]{:S(2)}) collective-permute-start(bf16[64,32,128]{2,1,0:T(8,128)(2,1)S(1)} %pad_maximum_fusion.1.refs_2_), channel_id=1, source_target_pairs={{0,2},{2,0},{4,6},{6,4},{8,10},{10,8},{12,14},{14,12},{16,18},{18,... | collective-permute-start | bytes 1572872 | tf_op jit(solution)/shard_map/ppermute | solution.py:322
  25.4 41.2 %copy-start.1 = (s32[16,2]{1,0:T(8,128)S(1)}, s32[16,2]{1,0:T(8,128)}, u32[]{:S(2)}) copy-start(s32[16,2]{1,0:T(8,128)} %constant.31) | copy-start | bytes 388
  25.4 2.6 %collective-permute-start.6 = (bf16[64,32,128]{2,1,0:T(8,128)(2,1)S(1)}, bf16[64,32,128]{2,1,0:T(8,128)(2,1)S(1)}, u32[]{:S(2)}, u32[]{:S(2)}) collective-permute-start(bf16[64,32,128]{2,1,0:T(8,128)(2,1)S(1)} %pad_maximum_fusion.refs_0_), channel_id=1, source_target_pairs={{0,2},{2,0},{4,6},{6,4},{8,10},{10,8},{12,14},{14,12},{16,18},{18,... | collective-permute-start | bytes 1572872 | tf_op jit(solution)/shard_map/ppermute | solution.py:322
  54.4 2.0 %collective-permute-start.8 = (bf16[2144,128]{1,0:T(8,128)(2,1)S(1)}, bf16[2144,128]{1,0:T(8,128)(2,1)S(1)}, u32[]{:S(2)}, u32[]{:S(2)}) collective-permute-start(bf16[2144,128]{1,0:T(8,128)(2,1)S(1)} %get-tuple-element.46), channel_id=1, source_target_pairs={{0,2},{2,0},{4,6},{6,4},{8,10},{10,8},{12,14},{14,12},{16,18},{18,... | collective-permute-start | bytes 1646600 | tf_op jit(solution)/shard_map/ppermute | solution.py:322
  54.6 3.5 %collective-permute-start.14 = (bf16[2144,128]{1,0:T(8,128)(2,1)S(1)}, bf16[2144,128]{1,0:T(8,128)(2,1)S(1)}, u32[]{:S(2)}, u32[]{:S(2)}) collective-permute-start(bf16[2144,128]{1,0:T(8,128)(2,1)S(1)} %get-tuple-element.52), channel_id=1, source_target_pairs={{0,2},{2,0},{4,6},{6,4},{8,10},{10,8},{12,14},{14,12},{16,18},{18,... | collective-permute-start | bytes 1646600 | tf_op jit(solution)/shard_map/ppermute | solution.py:322
  56.9 8.6 %collective-permute-start.9 = (bf16[1056,128]{1,0:T(8,128)(2,1)S(1)}, bf16[1056,128]{1,0:T(8,128)(2,1)S(1)}, u32[]{:S(2)}, u32[]{:S(2)}) collective-permute-start(bf16[1056,128]{1,0:T(8,128)(2,1)S(1)} %get-tuple-element.48), channel_id=1, source_target_pairs={{0,4},{2,6},{4,0},{6,2},{8,12},{10,14},{12,8},{14,10},{16,20},{18,... | collective-permute-start | bytes 811016 | tf_op jit(solution)/shard_map/ppermute | solution.py:322
  58.6 8.7 %collective-permute-start.15 = (bf16[1056,128]{1,0:T(8,128)(2,1)S(1)}, bf16[1056,128]{1,0:T(8,128)(2,1)S(1)}, u32[]{:S(2)}, u32[]{:S(2)}) collective-permute-start(bf16[1056,128]{1,0:T(8,128)(2,1)S(1)} %get-tuple-element.54), channel_id=1, source_target_pairs={{0,8},{2,10},{4,12},{6,14},{8,0},{10,2},{12,4},{14,6},{16,24},{18,... | collective-permute-start | bytes 811016 | tf_op jit(solution)/shard_map/ppermute | solution.py:322
  65.8 5.1 %collective-permute-start.10 = (bf16[544,128]{1,0:T(8,128)(2,1)S(1)}, bf16[544,128]{1,0:T(8,128)(2,1)S(1)}, u32[]{:S(2)}, u32[]{:S(2)}) collective-permute-start(bf16[544,128]{1,0:T(8,128)(2,1)S(1)} %get-tuple-element.50), channel_id=1, source_target_pairs={{0,8},{2,10},{4,12},{6,14},{8,0},{10,2},{12,4},{14,6},{16,24},{18,... | collective-permute-start | bytes 417800 | tf_op jit(solution)/shard_map/ppermute | solution.py:322
  67.6 6.7 %collective-permute-start.16 = (bf16[544,128]{1,0:T(8,128)(2,1)S(1)}, bf16[544,128]{1,0:T(8,128)(2,1)S(1)}, u32[]{:S(2)}, u32[]{:S(2)}) collective-permute-start(bf16[544,128]{1,0:T(8,128)(2,1)S(1)} %get-tuple-element.56), channel_id=1, source_target_pairs={{0,4},{2,6},{4,0},{6,2},{8,12},{10,14},{12,8},{14,10},{16,20},{18,... | collective-permute-start | bytes 417800 | tf_op jit(solution)/shard_map/ppermute | solution.py:322
  71.2 12.4 %collective-permute-start.11 = (bf16[544,128]{1,0:T(8,128)(2,1)S(1)}, bf16[544,128]{1,0:T(8,128)(2,1)S(1)}, u32[]{:S(2)}, u32[]{:S(2)}) collective-permute-start(bf16[544,128]{1,0:T(8,128)(2,1)S(1)} %merge.10.keep), channel_id=1, source_target_pairs={{0,16},{2,18},{4,20},{6,22},{8,24},{10,26},{12,28},{14,30},{16,0},... | collective-permute-start | bytes 417800 | tf_op jit(solution)/shard_map/ppermute | solution.py:322
  74.6 10.7 %collective-permute-start.17 = (bf16[544,128]{1,0:T(8,128)(2,1)S(1)}, bf16[544,128]{1,0:T(8,128)(2,1)S(1)}, u32[]{:S(2)}, u32[]{:S(2)}) collective-permute-start(bf16[544,128]{1,0:T(8,128)(2,1)S(1)} %merge.14.keep), channel_id=1, source_target_pairs={{0,16},{2,18},{4,20},{6,22},{8,24},{10,26},{12,28},{14,30},{16,0},... | collective-permute-start | bytes 417800 | tf_op jit(solution)/shard_map/ppermute | solution.py:322
  83.9 5.0 %collective-permute-start.12 = (bf16[16,4096]{1,0:T(8,128)(2,1)S(1)}, bf16[16,4096]{1,0:T(8,128)(2,1)S(1)}, u32[]{:S(2)}, u32[]{:S(2)}) collective-permute-start(bf16[16,4096]{1,0:T(8,128)(2,1)S(1)} %reshape.117), channel_id=1, source_target_pairs={{0,8},{2,10},{4,12},{6,14},{8,0},{10,2},{12,4},{14,6},{16,24},{18,... | collective-permute-start | bytes 393224 | tf_op jit(solution)/shard_map/ppermute | solution.py:322
  85.7 6.4 %collective-permute-start.18 = (bf16[16,4096]{1,0:T(8,128)(2,1)S(1)}, bf16[16,4096]{1,0:T(8,128)(2,1)S(1)}, u32[]{:S(2)}, u32[]{:S(2)}) collective-permute-start(bf16[16,4096]{1,0:T(8,128)(2,1)S(1)} %reshape.118), channel_id=1, source_target_pairs={{0,4},{2,6},{4,0},{6,2},{8,12},{10,14},{12,8},{14,10},{16,20},{18,... | collective-permute-start | bytes 393224 | tf_op jit(solution)/shard_map/ppermute | solution.py:322
  89.0 7.2 %collective-permute-start.13 = (bf16[32,4096]{1,0:T(8,128)(2,1)S(1)}, bf16[32,4096]{1,0:T(8,128)(2,1)S(1)}, u32[]{:S(2)}, u32[]{:S(2)}) collective-permute-start(bf16[32,4096]{1,0:T(8,128)(2,1)S(1)} %pad_maximum_fusion.6), channel_id=1, source_target_pairs={{0,4},{2,6},{4,0},{6,2},{8,12},{10,14},{12,8},{14,10},{16,20},{18,... | collective-permute-start | bytes 786440 | tf_op jit(solution)/shard_map/ppermute | solution.py:322
  92.2 6.4 %collective-permute-start.19 = (bf16[32,4096]{1,0:T(8,128)(2,1)S(1)}, bf16[32,4096]{1,0:T(8,128)(2,1)S(1)}, u32[]{:S(2)}, u32[]{:S(2)}) collective-permute-start(bf16[32,4096]{1,0:T(8,128)(2,1)S(1)} %pad_maximum_fusion.7), channel_id=1, source_target_pairs={{0,8},{2,10},{4,12},{6,14},{8,0},{10,2},{12,4},{14,6},{16,24},{18,... | collective-permute-start | bytes 786440 | tf_op jit(solution)/shard_map/ppermute | solution.py:322
  96.2 3.4 %collective-permute-start.20 = (bf16[64,4096]{1,0:T(8,128)(2,1)S(1)}, bf16[64,4096]{1,0:T(8,128)(2,1)S(1)}, u32[]{:S(2)}, u32[]{:S(2)}) collective-permute-start(bf16[64,4096]{1,0:T(8,128)(2,1)S(1)} %pad_maximum_fusion.2), channel_id=1, source_target_pairs={{0,2},{2,0},{4,6},{6,4},{8,10},{10,8},{12,14},{14,12},{16,18},{18,... | collective-permute-start | bytes 1572872 | tf_op jit(solution)/shard_map/ppermute | solution.py:322
  98.7 2.0 %collective-permute-start.21 = (bf16[64,4096]{1,0:T(8,128)(2,1)S(1)}, bf16[64,4096]{1,0:T(8,128)(2,1)S(1)}, u32[]{:S(2)}, u32[]{:S(2)}) collective-permute-start(bf16[64,4096]{1,0:T(8,128)(2,1)S(1)} %pad_maximum_fusion.3), channel_id=1, source_target_pairs={{0,2},{2,0},{4,6},{6,4},{8,10},{10,8},{12,14},{14,12},{16,18},{18,... | collective-permute-start | bytes 1572872 | tf_op jit(solution)/shard_map/ppermute | solution.py:322
  102.0 5.6 %collective-permute-start.22 = (bf16[128,512]{1,0:T(8,128)(2,1)S(1)}, bf16[128,512]{1,0:T(8,128)(2,1)S(1)}, u32[]{:S(2)}, u32[]{:S(2)}) collective-permute-start(bf16[128,512]{1,0:T(8,128)(2,1)S(1)} %bitcast.28), channel_id=1, source_target_pairs={{0,1},{1,0},{2,3},{3,2},{4,5},{5,4},{6,7},{7,6},{8,9},{9,8},{10,11... | collective-permute-start | bytes 393224 | tf_op jit(solution)/shard_map/ppermute | solution.py:390
  (1 other events, 13.1 us)
